TPU v7x, 128 devices: a whole 4x4x4 slice. The times are simulated.
128 devices in a mesh: section: 4 (over x), expert: 32 (over z, y, core).
Axes of the slice: x: 4, y: 4, z: 4, core: 2. Of those that a mesh axis runs over, the one named last changes fastest.
Arguments:
- section_inputs: float32 [4, 4096, 2048], P('section', 'expert'), may hold values from -6 to 6
- stored_inputs: float32 [4, 4096, 2048], P('section', 'expert'), may hold values from -6 to 6
- out_grads: bfloat16 [4, 4096, 2048], P('section', 'expert'), may hold values from -6 to 6
- fwd_routes: int32 [4, 4096, 2], P('section', 'expert'), may hold values from 0 to 15, all different within a row; in each aligned block of 128 rows (0 to 127, 128 to 255, ..., all dimensions but the last counted through in order) at most 20 rows name the same one
- fwd_gates: float32 [4, 4096, 2], P('section', 'expert'), may hold values from 0.2 to 1
- fwd_modulation: float32 [4, 3, 2048], P('section'), may hold values from -3 to 3
- bwd_routes: int32 [4, 4096, 2], P('section', 'expert'), may hold values from 0 to 15, all different within a row; in each aligned block of 128 rows (0 to 127, 128 to 255, ..., all dimensions but the last counted through in order) at most 20 rows name the same one
- bwd_gates: float32 [4, 4096, 2], P('section', 'expert'), may hold values from 0.2 to 1
- bwd_modulation: float32 [4, 3, 2048], P('section'), may hold values from -3 to 3
- up_weight: bfloat16 [4, 32, 2048, 1024], P('section', 'expert'), may hold values from -0.125 to 0.125
- down_weight: bfloat16 [4, 32, 1024, 2048], P('section', 'expert'), may hold values from -0.125 to 0.125
Outputs:
- next_inputs: float32 [4, 4096, 2048], P('section', 'expert')
- input_grads: bfloat16 [4, 4096, 2048], P('section', 'expert')
Inputs may be any that keep to these rules, and one draw needn't show every extreme that they name: `fwd_routes`: A token names two different experts. In the rows of one index of expert (aligned blocks of 128 rows of a section) no expert is named more than 20 times, a bound that some block reaches. `bwd_routes`: A token names two different experts. In the rows of one index of expert (aligned blocks of 128 rows of a section) no expert is named more than 20 times, a bound that some block reaches.
All inputs are finite; a program needn't handle non-finite values.
Results may differ from a plain program's by a relative error of at most 0.0042.
Values may be sent and summed in bfloat16 or wider, within the bound.
No kernel may reach another device: no remote copies, remote signals or barrier semaphores. Data moves between devices by JAX's collectives and lax.ppermute only.
A program may use at most 128 MiB of HBM per device.

v0:
```python
import functools

import jax
import jax.numpy as jnp
from jax import lax
from jax.experimental import pallas as pl
from jax.experimental.pallas import tpu as pltpu
from jax.sharding import PartitionSpec as P

norm_eps = 1e-06
f32 = jnp.float32
bf16 = jnp.bfloat16
SPLIT = 2
GROUP = 4


def dot(a, b, dims=((1,), (0,))):
    return lax.dot_general(a, b, (dims, ((), ())), preferred_element_type=f32)


def iota(shape, dim):
    return lax.broadcasted_iota(jnp.int32, shape, dim)


def ones_where(cond):
    return jnp.where(cond, 1.0, 0.0)


def layer_norm(rows):
    mean_row = jnp.mean(rows, axis=-1, keepdims=True)
    centered = rows - mean_row
    variance = jnp.mean(centered * centered, axis=-1, keepdims=True)
    inv_std = lax.rsqrt(variance + norm_eps)
    return centered * inv_std, inv_std


def slot_rows(routes, experts, per_expert):
    tokens = routes.shape[1]
    earlier = ones_where(iota((tokens, tokens), 0) < iota((tokens, tokens), 1)).astype(bf16)
    numbers = iota((experts, tokens), 0)
    chosen = [ones_where(numbers == routes[k : k + 1, :]) for k in range(2)]
    before = [dot(c.astype(bf16), earlier) for c in chosen]
    before[1] = before[1] + jnp.sum(chosen[0], axis=1, keepdims=True)
    slots = [jnp.sum(b * c, axis=0, keepdims=True) for b, c in zip(before, chosen)]
    return [routes[k : k + 1, :] * per_expert + slots[k].astype(jnp.int32) for k in range(2)]


def pack_fwd_body(x_ref, mod_ref, route_ref, out_ref, *, experts, cap):
    normed, _ = layer_norm(x_ref[...])
    hidden = (normed * (1.0 + mod_ref[1]) + mod_ref[0]).astype(bf16)
    part = hidden.shape[1] // SPLIT
    first = slot_rows(route_ref[...], experts, SPLIT * cap)
    numbers = iota((out_ref.shape[0], hidden.shape[0]), 0)
    left, right = [], []
    for h in range(SPLIT):
        hit = (numbers == first[0] + h * cap) | (numbers == first[1] + h * cap)
        left.append(ones_where(hit).astype(bf16))
        right.append(hidden[:, h * part : (h + 1) * part])
    out_ref[...] = dot(jnp.concatenate(left, 1), jnp.concatenate(right, 0)).astype(bf16)


def pack_bwd_body(x_ref, g_ref, gate_ref, mod_ref, route_ref, out_ref, norm_ref, inv_ref, *, experts, cap):
    normed, inv = layer_norm(x_ref[...])
    norm_ref[...] = normed
    inv_ref[...] = inv
    hidden = (normed * (1.0 + mod_ref[1]) + mod_ref[0]).astype(bf16)
    tokens, width = hidden.shape
    part = width // SPLIT
    scaled = mod_ref[2] * g_ref[...].astype(f32)
    gates = jnp.transpose(jnp.concatenate([gate_ref[...]] * 4, 0))
    pair = [(gates[:, k : k + 1] * scaled).astype(bf16) for k in range(2)]
    first = slot_rows(route_ref[...], experts, 2 * SPLIT * cap)
    numbers = iota((out_ref.shape[0], tokens), 0)
    left, right = [], []
    for h in range(SPLIT):
        hit = (numbers == first[0] + h * cap) | (numbers == first[1] + h * cap)
        left.append(ones_where(hit).astype(bf16))
        right.append(hidden[:, h * part : (h + 1) * part])
        for k in range(2):
            left.append(ones_where(numbers == first[k] + (SPLIT + h) * cap).astype(bf16))
            right.append(pair[k][:, h * part : (h + 1) * part])
    out_ref[...] = dot(jnp.concatenate(left, 1), jnp.concatenate(right, 0)).astype(bf16)


def regroup_matrix(kinds, cap, forward):
    size = GROUP * kinds * cap
    by_kind, by_source = iota((size, size), 0 if forward else 1), iota((size, size), 1 if forward else 0)

    def block_of(r):
        return jnp.floor((r.astype(f32) + 0.5) * (1.0 / cap)).astype(jnp.int32)

    kb, sb = block_of(by_kind), block_of(by_source)
    shift = kinds.bit_length() - 1
    same_slot = (by_kind - kb * cap) == (by_source - sb * cap)
    return ones_where(same_slot & (kb == (sb & (kinds - 1)) * GROUP + (sb >> shift))).astype(bf16)


def unpack(x_ref, targets, cap):
    kinds = len(targets) * SPLIT
    matrix = regroup_matrix(kinds, cap, True)
    size, slab, part = GROUP * kinds * cap, GROUP * cap, x_ref.shape[1]
    for n in range(x_ref.shape[0] // size):
        rows = dot(matrix, x_ref[n * size : (n + 1) * size, :]).astype(bf16)
        for t, target in enumerate(targets):
            for h in range(SPLIT):
                kind = t * SPLIT + h
                target[n * slab : (n + 1) * slab, h * part : (h + 1) * part] = rows[kind * slab : (kind + 1) * slab, :]


def repack(acc_ref, out_ref, cap):
    matrix = regroup_matrix(SPLIT, cap, False)
    size, slab, part = GROUP * SPLIT * cap, GROUP * cap, out_ref.shape[1]
    for n in range(out_ref.shape[0] // size):
        rows = [acc_ref[n * slab : (n + 1) * slab, h * part : (h + 1) * part].astype(bf16) for h in range(SPLIT)]
        out_ref[n * size : (n + 1) * size, :] = dot(matrix, jnp.concatenate(rows, 0)).astype(bf16)


def add_to(acc_ref, value, first):
    @pl.when(first)
    def _():
        acc_ref[...] = value

    @pl.when(jnp.logical_not(first))
    def _():
        acc_ref[...] += value


def expert_fwd_body(x_ref, up_a, down_a, up_b, down_b, out_ref, rows_ref, acc_ref, *, cap, blocks):
    step = pl.program_id(0)

    @pl.when(step == 0)
    def _():
        unpack(x_ref, [rows_ref], cap)

    def one(up_ref, down_ref):
        act = jax.nn.gelu(dot(rows_ref[...], up_ref[...])).astype(bf16)
        add_to(acc_ref, dot(act, down_ref[...]), step == 0)

    pl.when(step < blocks)(lambda: one(up_a, down_a))
    pl.when(step >= blocks)(lambda: one(up_b, down_b))

    @pl.when(step == 2 * blocks - 1)
    def _():
        repack(acc_ref, out_ref, cap)


def gelu_slope(x):
    c = 0.7978845608028654
    square = x * x
    t = jnp.tanh(c * x * (1.0 + 0.044715 * square))
    return 0.5 * (1.0 + t) + (0.5 * c) * x * (1.0 - t * t) * (1.0 + (3.0 * 0.044715) * square)


def expert_bwd_body(x_ref, up_a, down_a, up_b, down_b, out_ref, rows_ref, grads_ref, acc_ref, *, cap, blocks):
    step = pl.program_id(0)

    @pl.when(step == 0)
    def _():
        unpack(x_ref, [rows_ref, grads_ref], cap)

    def one(up_ref, down_ref):
        up = up_ref[...]
        slope = gelu_slope(dot(rows_ref[...], up))
        act_grad = dot(grads_ref[...], down_ref[...], ((1,), (1,)))
        add_to(acc_ref, dot((act_grad * slope).astype(bf16), up, ((1,), (1,))), step == 0)

    pl.when(step < blocks)(lambda: one(up_a, down_a))
    pl.when(step >= blocks)(lambda: one(up_b, down_b))

    @pl.when(step == 2 * blocks - 1)
    def _():
        repack(acc_ref, out_ref, cap)


def combine_fwd_body(r_ref, gate_ref, route_ref, x_ref, mod_ref, out_ref, *, experts, cap):
    tokens, width = x_ref.shape
    part = width // SPLIT
    first = slot_rows(route_ref[...], experts, SPLIT * cap)
    numbers = iota((r_ref.shape[0], tokens), 0)
    for h in range(SPLIT):
        weights = sum(jnp.where(numbers == first[k] + h * cap, gate_ref[k : k + 1, :], 0.0) for k in range(2))
        high = weights.astype(bf16)
        low = (weights - high.astype(f32)).astype(bf16)
        both = dot(high, r_ref[...], ((0,), (0,))) + dot(low, r_ref[...], ((0,), (0,)))
        cols = slice(h * part, (h + 1) * part)
        out_ref[:, cols] = x_ref[:, cols] + mod_ref[2][:, cols] * both


def combine_bwd_body(r_ref, route_ref, norm_ref, inv_ref, g_ref, mod_ref, out_ref, *, experts, cap):
    tokens = norm_ref.shape[0]
    first = slot_rows(route_ref[...], experts, SPLIT * cap)
    numbers = iota((r_ref.shape[0], tokens), 0)
    halves = []
    for h in range(SPLIT):
        hit = (numbers == first[0] + h * cap) | (numbers == first[1] + h * cap)
        halves.append(dot(ones_where(hit).astype(bf16), r_ref[...], ((0,), (0,))))
    normed = norm_ref[...]
    dnorm = jnp.concatenate(halves, 1) * (1.0 + mod_ref[1])
    mean_one = jnp.mean(dnorm, axis=-1, keepdims=True)
    mean_two = jnp.mean(dnorm * normed, axis=-1, keepdims=True)
    grad = g_ref[...].astype(f32) + (dnorm - mean_one - normed * mean_two) * inv_ref[...]
    out_ref[...] = grad.astype(bf16)


def call(body, outs, args, flops, **statics):
    moved = sum(a.size * a.dtype.itemsize for a in list(args) + list(outs))
    return pl.pallas_call(
        functools.partial(body, **statics),
        out_shape=outs,
        cost_estimate=pl.CostEstimate(flops=flops, bytes_accessed=moved, transcendentals=0),
    )(*args)


def call_expert(body, rows, weights, scratch_rows, flops, cap, block=512):
    up, down = weights[0]
    width, ff = up.shape
    blocks = ff // block
    slots = rows.shape[0] * rows.shape[1] // width // scratch_rows
    own = lambda i: jnp.minimum(i, blocks - 1)
    other = lambda i: jnp.maximum(i - blocks, 0)
    whole = lambda shape: pl.BlockSpec(shape, lambda i: (0, 0))
    out = jax.ShapeDtypeStruct((slots * SPLIT, width // SPLIT), bf16)
    specs = [whole(rows.shape)]
    for pick in (own, other):
        specs.append(pl.BlockSpec((width, block), lambda i, pick=pick: (0, pick(i))))
        specs.append(pl.BlockSpec((block, width), lambda i, pick=pick: (pick(i), 0)))
    moved = 2 * (rows.size + out.size + 2 * up.size + 2 * down.size)
    return pl.pallas_call(
        functools.partial(body, cap=cap, blocks=blocks),
        out_shape=out,
        grid=(2 * blocks,),
        in_specs=specs,
        out_specs=whole(out.shape),
        scratch_shapes=[pltpu.VMEM((slots, width), bf16)] * scratch_rows + [pltpu.VMEM((slots, width), f32)],
        cost_estimate=pl.CostEstimate(flops=flops, bytes_accessed=moved, transcendentals=0),
        compiler_params=pltpu.CompilerParams(dimension_semantics=("arbitrary",)),
    )(rows, up, down, *weights[1])


def shifted(value, axis, steps):
    count = lax.axis_size(axis)
    leading, last = (max(0, -steps), min(count, count - steps))
    return lax.ppermute(value, axis, [(source, source + steps) for source in range(leading, last)])


def exchange(rows, experts):
    units = lax.axis_size("expert")
    cores = units // experts
    groups = [[e * cores + c for e in range(experts)] for c in range(cores)]
    parts = rows.reshape(experts, -1, rows.shape[1])
    swapped = lax.all_to_all(parts, "expert", 0, 0, axis_index_groups=groups, tiled=True)
    return swapped.reshape(rows.shape)


def on_device(
    section_inputs,
    stored_inputs,
    out_grads,
    fwd_routes,
    fwd_gates,
    fwd_modulation,
    bwd_routes,
    bwd_gates,
    bwd_modulation,
    up_weight,
    down_weight,
):
    units = lax.axis_size("expert")
    experts = units // 2
    tokens, width = section_inputs.shape[1:]
    cap = min(tokens, 5 * tokens // (2 * experts))
    slots = experts * cap
    ff = up_weight.shape[3]
    shape = jax.ShapeDtypeStruct
    sizes = dict(experts=experts, cap=cap)

    inputs, stored, grads = section_inputs[0], stored_inputs[0], out_grads[0]
    routes, gates = fwd_routes[0].T, fwd_gates[0].T
    routes_b, gates_b = bwd_routes[0].T, bwd_gates[0].T
    mod = fwd_modulation.reshape(3, 1, width)
    mod_b = bwd_modulation.reshape(3, 1, width)
    own = (up_weight[0, 0], down_weight[0, 0])
    swap = [(i, i ^ 1) for i in range(units)]
    other = tuple(lax.ppermute(w, "expert", swap) for w in own)

    (send,) = call(
        pack_fwd_body,
        [shape((SPLIT * slots, width // SPLIT), bf16)],
        (inputs, mod, routes),
        4 * tokens * slots * width,
        **sizes,
    )
    got = exchange(send, experts)

    send_b, normed_b, inv_b = call(
        pack_bwd_body,
        [
            shape((2 * SPLIT * slots, width // SPLIT), bf16),
            shape((tokens, width), f32),
            shape((tokens, 1), f32),
        ],
        (stored, grads, gates_b, mod_b, routes_b),
        12 * tokens * slots * width,
        **sizes,
    )
    got_b = exchange(send_b, experts)

    result = call_expert(expert_fwd_body, got, (own, other), 1, 8 * slots * width * ff, cap)
    back = exchange(result, experts)
    result_b = call_expert(expert_bwd_body, got_b, (own, other), 2, 12 * slots * width * ff, cap)
    back_b = exchange(result_b, experts)

    (out_fwd,) = call(
        combine_fwd_body,
        [shape((tokens, width), f32)],
        (back, gates, routes, inputs, mod),
        8 * tokens * slots * width,
        **sizes,
    )
    next_inputs = shifted(out_fwd[None], "section", 1)
    (section_grad,) = call(
        combine_bwd_body,
        [shape((tokens, width), bf16)],
        (back_b, routes_b, normed_b, inv_b, grads, mod_b),
        4 * tokens * slots * width,
        **sizes,
    )
    input_grads = shifted(section_grad[None], "section", -1)
    return (next_inputs, input_grads)


def solution(mesh):
    rows = P("section", "expert", None)
    mod = P("section", None, None)
    weight = P("section", "expert", None, None)
    placed = (rows, rows, rows, rows, rows, mod, rows, rows, mod, weight, weight)
    return jax.shard_map(
        on_device, mesh=mesh, in_specs=placed, out_specs=(rows, rows), check_vma=False
    )
```

profile of v0, /device:TPU:0, one launch (start us, length us, event | category | flops | bytes accessed | tf_op | source)
XLA Modules:
  0.0 146.3 jit_solution(7551242190432911327)
XLA Ops:
  0.6 0.1 collective-permute-start
  0.7 0.5 collective-permute-start.1
  1.2 3.2 %shard_map.122 = bf16[640,1024]{1,0:T(8,128)(2,1)} custom-call(f32[128,2048]{1,0:T(8,128)} %bitcast.32, f32[3,1,2048]{2,1,0:T(1,128)} %bitcast.43, s32[2,128]{1,0:T(2,128)} %bitcast.47), custom_call_target="tpu_custom_call" | custom-call | flops 335544320 | bytes 2384896 | tf_op jit(solution)/shard_map/pallas_call | solution.py:207
  4.4 8.2 %all-to-all-start = ((bf16[16,40,1024]{2,1,0:T(8,128)(2,1)}), bf16[16,40,1024]{2,1,0:T(8,128)(2,1)S(1)}, u32[]{:S(2)}, u32[]{:S(2)}) async-start(bf16[16,40,1024]{2,1,0:T(8,128)(2,1)} %bitcast.31), calls=%async_computation | async-start | bytes 2621440 | tf_op jit(solution)/shard_map/all_to_all | solution.py:251
  12.5 5.7 %shard_map.125 = (bf16[1280,1024]{1,0:T(8,128)(2,1)}, f32[128,2048]{1,0:T(8,128)}, f32[128,1]{1,0:T(8,128)}) custom-call(f32[128,2048]{1,0:T(8,128)} %bitcast.58, bf16[128,2048]{1,0:T(8,128)(2,1)} %bitcast.40, f32[2,128]{1,0:T(2,128)} %bitcast.59, f32[3,1,2048]{2,1,0:T(1,128)} %bitcast.45, s32[2,128]{1,0:T(2,128)} %bitcast.49), custom_call_target="tpu_custom_call" | custom-call | flops 1006632960 | bytes 5270016 | tf_op jit(solution)/shard_map/pallas_call | solution.py:207
  18.2 15.8 %all-to-all-done = bf16[16,40,1024]{2,1,0:T(8,128)(2,1)S(1)} async-done(((bf16[16,40,1024]{2,1,0:T(8,128)(2,1)}), bf16[16,40,1024]{2,1,0:T(8,128)(2,1)S(1)}, u32[]{:S(2)}, u32[]{:S(2)}) %all-to-all-start) | async-done | bytes 1310752 | tf_op jit(solution)/shard_map/all_to_all | solution.py:251
  34.1 0.0 copy-start.3
  34.1 1.1 copy-done.3
  35.2 3.7 %all-to-all-start.2 = ((bf16[16,80,1024]{2,1,0:T(8,128)(2,1)}), bf16[16,80,1024]{2,1,0:T(8,128)(2,1)S(1)}, u32[]{:S(2)}, u32[]{:S(2)}) async-start(bf16[16,80,1024]{2,1,0:T(8,128)(2,1)} %bitcast.35), calls=%async_computation.2 | async-start | bytes 5242880 | tf_op jit(solution)/shard_map/all_to_all | solution.py:251
  38.9 0.0 collective-permute-done.up_b
  38.9 0.0 collective-permute-done.1.down_b
  38.9 15.2 %shard_map.123 = bf16[640,1024]{1,0:T(8,128)(2,1)} custom-call(bf16[640,1024]{1,0:T(8,128)(2,1)} %bitcast.36, bf16[2048,1024]{1,0:T(8,128)(2,1)} %bitcast.53, bf16[1024,2048]{1,0:T(8,128)(2,1)} %bitcast.56, bf16[2048,1024]{1,0:T(8,128)(2,1)} %collective-permute-done.up_b, bf16[1024,2048]{1,0:T(8,128)(2,1)} %collective-permute-done.1.down_b), custom_call_target="tpu_custom_call" | custom-call | flops 5368709120 | bytes 19398656 | tf_op jit(solution)/shard_map/pallas_call | solution.py:228
  54.1 22.9 %all-to-all-done.2 = bf16[16,80,1024]{2,1,0:T(8,128)(2,1)S(1)} async-done(((bf16[16,80,1024]{2,1,0:T(8,128)(2,1)}), bf16[16,80,1024]{2,1,0:T(8,128)(2,1)S(1)}, u32[]{:S(2)}, u32[]{:S(2)}) %all-to-all-start.2) | async-done | bytes 2621472 | tf_op jit(solution)/shard_map/all_to_all | solution.py:251
  77.0 0.0 copy-start.2
  77.0 1.5 %copy-done.2 = bf16[16,80,1024]{2,1,0:T(8,128)(2,1)} copy-done((bf16[16,80,1024]{2,1,0:T(8,128)(2,1)}, bf16[16,80,1024]{2,1,0:T(8,128)(2,1)S(1)}, u32[]{:S(2)}) %copy-start.2) | copy-done | bytes 2621464
  78.5 3.9 %all-to-all-start.1 = ((bf16[16,40,1024]{2,1,0:T(8,128)(2,1)}), bf16[16,40,1024]{2,1,0:T(8,128)(2,1)S(1)}, u32[]{:S(2)}, u32[]{:S(2)}) async-start(bf16[16,40,1024]{2,1,0:T(8,128)(2,1)} %bitcast.38), calls=%async_computation.1 | async-start | bytes 2621440 | tf_op jit(solution)/shard_map/all_to_all | solution.py:251
  82.4 19.1 %shard_map.126 = bf16[640,1024]{1,0:T(8,128)(2,1)} custom-call(bf16[1280,1024]{1,0:T(8,128)(2,1)} %bitcast.34, bf16[2048,1024]{1,0:T(8,128)(2,1)} %bitcast.54, bf16[1024,2048]{1,0:T(8,128)(2,1)} %bitcast.57, bf16[2048,1024]{1,0:T(8,128)(2,1)} %collective-permute-done.up_b, bf16[1024,2048]{1,0:T(8,128)(2,1)} %collective-permute-done.1.down_b), custom_call_target="tpu_custom_call" | custom-call | flops 8053063680 | bytes 20709376 | tf_op jit(solution)/shard_map/pallas_call | solution.py:228
  101.6 0.0 all-to-all-done.1
  101.6 0.0 copy-start.1
  101.6 6.9 %all-to-all-start.3 = ((bf16[16,40,1024]{2,1,0:T(8,128)(2,1)}), bf16[16,40,1024]{2,1,0:T(8,128)(2,1)S(1)}, u32[]{:S(2)}, u32[]{:S(2)}) async-start(bf16[16,40,1024]{2,1,0:T(8,128)(2,1)} %bitcast.37), calls=%async_computation.3 | async-start | bytes 2621440 | tf_op jit(solution)/shard_map/all_to_all | solution.py:251
  108.6 0.0 copy-done.1
  108.6 3.9 %shard_map.124 = f32[128,2048]{1,0:T(8,128)} custom-call(bf16[640,1024]{1,0:T(8,128)(2,1)} %bitcast.30, f32[2,128]{1,0:T(2,128)} %bitcast.51, s32[2,128]{1,0:T(2,128)} %bitcast.48, f32[128,2048]{1,0:T(8,128)} %bitcast.33, f32[3,1,2048]{2,1,0:T(1,128)} %bitcast.44), custom_call_target="tpu_custom_call" | custom-call | flops 671088640 | bytes 3434496 | tf_op jit(solution)/shard_map/pallas_call | solution.py:207
  112.5 3.4 %collective-permute-start.2 = (f32[1,128,2048]{2,1,0:T(8,128)}, f32[1,128,2048]{2,1,0:T(8,128)S(1)}, u32[]{:S(2)}, u32[]{:S(2)}) collective-permute-start(f32[1,128,2048]{2,1,0:T(8,128)} %bitcast.39), channel_id=1, source_target_pairs={{0,32},{32,64},{64,96},{1,33},{33,65},{65,97},{2,34},{34,66},{66,9... | collective-permute-start | bytes 3145736 | tf_op jit(solution)/shard_map/ppermute | solution.py:243
  115.9 11.6 %all-to-all-done.3 = bf16[16,40,1024]{2,1,0:T(8,128)(2,1)S(1)} async-done(((bf16[16,40,1024]{2,1,0:T(8,128)(2,1)}), bf16[16,40,1024]{2,1,0:T(8,128)(2,1)S(1)}, u32[]{:S(2)}, u32[]{:S(2)}) %all-to-all-start.3) | async-done | bytes 1310752 | tf_op jit(solution)/shard_map/all_to_all | solution.py:251
  127.5 0.0 copy-start
  127.5 1.1 copy-done
  128.6 3.7 %shard_map.127 = bf16[128,2048]{1,0:T(8,128)(2,1)} custom-call(bf16[640,1024]{1,0:T(8,128)(2,1)} %bitcast.29, s32[2,128]{1,0:T(2,128)} %bitcast.50, f32[128,2048]{1,0:T(8,128)} %get-tuple-element.6.norm_ref, f32[128,1]{1,0:T(8,128)} %get-tuple-element.7.inv_ref, bf16[128,2048]{1,0:T(8,128)(2,1)} %bitcast.41, f32[3,1,2048]{2,1,0:T(1,128)} %bitcast.46), custom_call_target="tpu_custom_call" | custom-call | flops 335544320 | bytes 3433984 | tf_op jit(solution)/shard_map/pallas_call | solution.py:207
  132.3 1.3 collective-permute-start.3
  133.6 11.0 %collective-permute-done.3 = bf16[1,128,2048]{2,1,0:T(8,128)(2,1)S(1)} collective-permute-done((bf16[1,128,2048]{2,1,0:T(8,128)(2,1)}, bf16[1,128,2048]{2,1,0:T(8,128)(2,1)S(1)}, u32[]{:S(2)}, u32[]{:S(2)}) %collective-permute-start.3) | collective-permute-done | bytes 524320 | tf_op jit(solution)/shard_map/ppermute | solution.py:243
  144.6 0.0 collective-permute-done.2
  144.6 1.0 copy.15
  145.5 0.8 copy.16
Async XLA Ops:
  0.6 38.3 %collective-permute-start = (bf16[2048,1024]{1,0:T(8,128)(2,1)}, bf16[2048,1024]{1,0:T(8,128)(2,1)}, u32[]{:S(2)}, u32[]{:S(2)}) collective-permute-start(bf16[2048,1024]{1,0:T(8,128)(2,1)} %bitcast.52), channel_id=1, source_target_pairs={{0,1},{1,0},{2,3},{3,2},{4,5},{5,4},{6,7},{7,6},{8,9},{9,8},{10,11... | collective-permute-start | bytes 12582920 | tf_op jit(solution)/shard_map/ppermute | solution.py:284
  0.7 38.2 %collective-permute-start.1 = (bf16[1024,2048]{1,0:T(8,128)(2,1)}, bf16[1024,2048]{1,0:T(8,128)(2,1)}, u32[]{:S(2)}, u32[]{:S(2)}) collective-permute-start(bf16[1024,2048]{1,0:T(8,128)(2,1)} %bitcast.55), channel_id=1, source_target_pairs={{0,1},{1,0},{2,3},{3,2},{4,5},{5,4},{6,7},{7,6},{8,9},{9,8},{10,11... | collective-permute-start | bytes 12582920 | tf_op jit(solution)/shard_map/ppermute | solution.py:284
  4.4 29.7 %all-to-all-start = ((bf16[16,40,1024]{2,1,0:T(8,128)(2,1)}), bf16[16,40,1024]{2,1,0:T(8,128)(2,1)S(1)}, u32[]{:S(2)}, u32[]{:S(2)}) async-start(bf16[16,40,1024]{2,1,0:T(8,128)(2,1)} %bitcast.31), calls=%async_computation | async-start | bytes 2621440 | tf_op jit(solution)/shard_map/all_to_all | solution.py:251
  34.1 1.1 copy-start.3
  35.2 41.8 %all-to-all-start.2 = ((bf16[16,80,1024]{2,1,0:T(8,128)(2,1)}), bf16[16,80,1024]{2,1,0:T(8,128)(2,1)S(1)}, u32[]{:S(2)}, u32[]{:S(2)}) async-start(bf16[16,80,1024]{2,1,0:T(8,128)(2,1)} %bitcast.35), calls=%async_computation.2 | async-start | bytes 5242880 | tf_op jit(solution)/shard_map/all_to_all | solution.py:251
  77.0 1.5 %copy-start.2 = (bf16[16,80,1024]{2,1,0:T(8,128)(2,1)}, bf16[16,80,1024]{2,1,0:T(8,128)(2,1)S(1)}, u32[]{:S(2)}) copy-start(bf16[16,80,1024]{2,1,0:T(8,128)(2,1)S(1)} %all-to-all-done.2) | copy-start | bytes 7864324
  78.5 23.1 %all-to-all-start.1 = ((bf16[16,40,1024]{2,1,0:T(8,128)(2,1)}), bf16[16,40,1024]{2,1,0:T(8,128)(2,1)S(1)}, u32[]{:S(2)}, u32[]{:S(2)}) async-start(bf16[16,40,1024]{2,1,0:T(8,128)(2,1)} %bitcast.38), calls=%async_computation.1 | async-start | bytes 2621440 | tf_op jit(solution)/shard_map/all_to_all | solution.py:251
  101.6 7.0 %copy-start.1 = (bf16[16,40,1024]{2,1,0:T(8,128)(2,1)}, bf16[16,40,1024]{2,1,0:T(8,128)(2,1)S(1)}, u32[]{:S(2)}) copy-start(bf16[16,40,1024]{2,1,0:T(8,128)(2,1)S(1)} %all-to-all-done.1) | copy-start | bytes 3932164
  101.6 25.9 %all-to-all-start.3 = ((bf16[16,40,1024]{2,1,0:T(8,128)(2,1)}), bf16[16,40,1024]{2,1,0:T(8,128)(2,1)S(1)}, u32[]{:S(2)}, u32[]{:S(2)}) async-start(bf16[16,40,1024]{2,1,0:T(8,128)(2,1)} %bitcast.37), calls=%async_computation.3 | async-start | bytes 2621440 | tf_op jit(solution)/shard_map/all_to_all | solution.py:251
  112.5 32.1 %collective-permute-start.2 = (f32[1,128,2048]{2,1,0:T(8,128)}, f32[1,128,2048]{2,1,0:T(8,128)S(1)}, u32[]{:S(2)}, u32[]{:S(2)}) collective-permute-start(f32[1,128,2048]{2,1,0:T(8,128)} %bitcast.39), channel_id=1, source_target_pairs={{0,32},{32,64},{64,96},{1,33},{33,65},{65,97},{2,34},{34,66},{66,9... | collective-permute-start | bytes 3145736 | tf_op jit(solution)/shard_map/ppermute | solution.py:243
  127.5 1.1 copy-start
  132.3 12.3 %collective-permute-start.3 = (bf16[1,128,2048]{2,1,0:T(8,128)(2,1)}, bf16[1,128,2048]{2,1,0:T(8,128)(2,1)S(1)}, u32[]{:S(2)}, u32[]{:S(2)}) collective-permute-start(bf16[1,128,2048]{2,1,0:T(8,128)(2,1)} %bitcast.42), channel_id=1, source_target_pairs={{32,0},{64,32},{96,64},{33,1},{65,33},{97,65},{34,2},{66,34},{98,6... | collective-permute-start | bytes 1572872 | tf_op jit(solution)/shard_map/ppermute | solution.py:243
where the time goes:
time: 147 us; the launch traced here: 146 us
  waiting for transfers between devices  61.3 us (42%)
  Pallas kernels  50.8 us (35%)
  starting transfers between devices  28 us (19%)
  local copies, waits for them, and re-layouts  5.5 us (4%)
    all_to_all x4, waiting for transfers between devices, exchange(): lax.all_to_all(parts, 'expert', 0, 0, axis_index_groups=groups, tiled=True)  50.3 us
    pallas_call x2, Pallas kernels, call_expert(): pl.pallas_call(functools.partial(body, cap=cap, blocks=blocks), out_shape...  34.3 us
    all_to_all x4, starting transfers between devices, exchange(): lax.all_to_all(parts, 'expert', 0, 0, axis_index_groups=groups, tiled=True)  22.7 us
    pallas_call x4, Pallas kernels, call(): pl.pallas_call(functools.partial(body, **statics), out_shape=outs, cost_e...  16.4 us
    ppermute x2, waiting for transfers between devices, shifted(): lax.ppermute(value, axis, [(source, source + steps) for source in range(l...  11 us
    unnamed x10, local copies, waits for them, and re-layouts  5.5 us
    ppermute x2, starting transfers between devices, shifted(): lax.ppermute(value, axis, [(source, source + steps) for source in range(l...  4.71 us
  transfers between devices with their start and end apart: 8, of which 4 were waited for; matrix products, arithmetic and copies ran while one was open for 0% of the time, Pallas kernels for 35%

commit v1 on v0

v1 whole, which is shorter than its diff:
```python
import functools

import jax
import jax.numpy as jnp
from jax import lax
from jax.experimental import pallas as pl
from jax.experimental.pallas import tpu as pltpu
from jax.sharding import PartitionSpec as P


norm_eps = 1e-06
f32 = jnp.float32
bf16 = jnp.bfloat16
SPLIT = 2
GROUP = 4
BLOCK = 512


def dot(a, b, dims=((1,), (0,))):
    return lax.dot_general(a, b, (dims, ((), ())), preferred_element_type=f32)


def iota(shape, dim):
    return lax.broadcasted_iota(jnp.int32, shape, dim)


def ones_where(cond):
    return jnp.where(cond, 1.0, 0.0)


def layer_norm(rows):
    mean_row = jnp.mean(rows, axis=-1, keepdims=True)
    centered = rows - mean_row
    variance = jnp.mean(centered * centered, axis=-1, keepdims=True)
    inv_std = lax.rsqrt(variance + norm_eps)
    return centered * inv_std, inv_std


def slots_of(routes, experts):
    tokens = routes.shape[1]
    earlier = ones_where(iota((tokens, tokens), 0) < iota((tokens, tokens), 1)).astype(bf16)
    numbers = iota((experts, tokens), 0)
    chosen = [ones_where(numbers == routes[k : k + 1, :]) for k in range(2)]
    before = [dot(c.astype(bf16), earlier) for c in chosen]
    before[1] = before[1] + jnp.sum(chosen[0], axis=1, keepdims=True)
    return [jnp.sum(b * c, axis=0, keepdims=True).astype(jnp.int32) for b, c in zip(before, chosen)]


def slot_rows(routes, experts, per_expert):
    slots = slots_of(routes, experts)
    return [routes[k : k + 1, :] * per_expert + slots[k] for k in range(2)]


def pack_fwd_body(x_ref, mod_ref, route_ref, out_ref, *, experts, cap):
    normed, _ = layer_norm(x_ref[...])
    hidden = (normed * (1.0 + mod_ref[1]) + mod_ref[0]).astype(bf16)
    part = hidden.shape[1] // SPLIT
    first = slot_rows(route_ref[...], experts, SPLIT * cap)
    numbers = iota((out_ref.shape[0], hidden.shape[0]), 0)
    left, right = [], []
    for h in range(SPLIT):
        hit = (numbers == first[0] + h * cap) | (numbers == first[1] + h * cap)
        left.append(ones_where(hit).astype(bf16))
        right.append(hidden[:, h * part : (h + 1) * part])
    out_ref[...] = dot(jnp.concatenate(left, 1), jnp.concatenate(right, 0)).astype(bf16)


def pack_bwd_body(place_ref, x_ref, g_ref, gate_ref, mod_ref, route_ref, *outs, experts, cap, side):
    blocks, norm_ref, inv_ref, where_ref = outs[:experts], *outs[experts:]
    normed, inv = layer_norm(x_ref[...])
    norm_ref[...] = normed
    inv_ref[...] = inv
    hidden = (normed * (1.0 + mod_ref[1]) + mod_ref[0]).astype(bf16)
    tokens, width = hidden.shape
    part = width // SPLIT
    scaled = mod_ref[2] * g_ref[...].astype(f32)
    routes = route_ref[...]
    slots = slots_of(routes, experts)
    back = [(routes[k : k + 1, :] * (SPLIT * cap) + slots[k]).astype(f32) for k in range(2)]
    columns = jnp.transpose(jnp.concatenate([gate_ref[...], *back] * 2, 0))
    where_ref[...] = columns.astype(jnp.int32)
    pair = [(columns[:, k : k + 1] * scaled).astype(bf16) for k in range(2)]
    shift = side.bit_length() - 1
    z, y = place_ref[0] >> shift, place_ref[0] & (side - 1)
    ahead = (((routes >> shift) - z) & (side - 1)) * side + ((routes - y) & (side - 1))
    first = [ahead[k : k + 1, :] * (2 * SPLIT * cap) + slots[k] for k in range(2)]
    numbers = iota((experts * 2 * SPLIT * cap, tokens), 0)
    left, right = [], []
    for h in range(SPLIT):
        hit = (numbers == first[0] + h * cap) | (numbers == first[1] + h * cap)
        left.append(ones_where(hit).astype(bf16))
        right.append(hidden[:, h * part : (h + 1) * part])
        for k in range(2):
            left.append(ones_where(numbers == first[k] + (SPLIT + h) * cap).astype(bf16))
            right.append(pair[k][:, h * part : (h + 1) * part])
    rows = dot(jnp.concatenate(left, 1), jnp.concatenate(right, 0)).astype(bf16)
    size = 2 * SPLIT * cap
    for n, block in enumerate(blocks):
        block[...] = rows[n * size : (n + 1) * size, :]


def regroup_matrix(kinds, cap, forward):
    size = GROUP * kinds * cap
    by_kind, by_source = iota((size, size), 0 if forward else 1), iota((size, size), 1 if forward else 0)

    def block_of(r):
        return jnp.floor((r.astype(f32) + 0.5) * (1.0 / cap)).astype(jnp.int32)

    kb, sb = block_of(by_kind), block_of(by_source)
    shift = kinds.bit_length() - 1
    same_slot = (by_kind - kb * cap) == (by_source - sb * cap)
    return ones_where(same_slot & (kb == (sb & (kinds - 1)) * GROUP + (sb >> shift))).astype(bf16)


def unpack(pieces, targets, cap):
    kinds = len(targets) * SPLIT
    matrix = regroup_matrix(kinds, cap, True)
    slab = GROUP * cap
    for n, piece in enumerate(pieces):
        rows = dot(matrix, piece).astype(bf16)
        part = rows.shape[1]
        for t, target in enumerate(targets):
            for h in range(SPLIT):
                kind = t * SPLIT + h
                target[n * slab : (n + 1) * slab, h * part : (h + 1) * part] = rows[kind * slab : (kind + 1) * slab, :]


def repack(sum_ref, cap):
    matrix = regroup_matrix(SPLIT, cap, False)
    slab, part = GROUP * cap, sum_ref.shape[1] // SPLIT
    for n in range(sum_ref.shape[0] // slab):
        rows = [sum_ref[n * slab : (n + 1) * slab, h * part : (h + 1) * part] for h in range(SPLIT)]
        yield n, dot(matrix, jnp.concatenate(rows, 0)).astype(bf16)


def fetches(pieces, sems):
    copies = [pltpu.make_async_copy(source, target, sems.at[n]) for n, (source, target) in enumerate(pieces)]
    for copy in copies:
        copy.start()
    return iter(copies)


def expert_fwd_body(x_ref, *refs, cap):
    weights, (out_ref, rows_ref, act_ref, sum_ref), buffers, sems = refs[:4], refs[4:8], refs[8:12], refs[12]
    size = GROUP * SPLIT * cap
    ff, width = weights[1].shape
    pieces = []
    for n in (0, 2):
        for j in range(0, ff, BLOCK):
            pieces.append((weights[n].at[:, j : j + BLOCK], buffers[n].at[:, j : j + BLOCK]))
    for j in range(0, width, BLOCK):
        for n in (1, 3):
            pieces.append((weights[n].at[:, j : j + BLOCK], buffers[n].at[:, j : j + BLOCK]))
    copies = fetches(pieces, sems)
    unpack([x_ref[n : n + size, :] for n in range(0, x_ref.shape[0], size)], [rows_ref], cap)
    for n, up in enumerate((buffers[0], buffers[2])):
        for j in range(0, ff, BLOCK):
            next(copies).wait()
            act = jax.nn.gelu(dot(rows_ref[...], up[:, j : j + BLOCK]))
            act_ref[:, n * ff + j : n * ff + j + BLOCK] = act.astype(bf16)
    for j in range(0, width, BLOCK):
        cols = slice(j, j + BLOCK)
        next(copies).wait()
        next(copies).wait()
        both = dot(act_ref[:, :ff], buffers[1][:, cols]) + dot(act_ref[:, ff:], buffers[3][:, cols])
        sum_ref[:, cols] = both.astype(bf16)
    for n, rows in repack(sum_ref, cap):
        out_ref[n * size : (n + 1) * size, :] = rows


def gelu_slope(x):
    c = 0.7978845608028654
    square = x * x
    t = jnp.tanh(c * x * (1.0 + 0.044715 * square))
    return 0.5 * (1.0 + t) + (0.5 * c) * x * (1.0 - t * t) * (1.0 + (3.0 * 0.044715) * square)


def expert_bwd_body(place_ref, *refs, cap, side):
    experts = side * side
    blocks, weights, refs = refs[:experts], refs[experts : experts + 4], refs[experts + 4 :]
    (out_ref, rows_ref, grads_ref, pre_ref, sum_ref), buffers, sems = refs[:5], refs[5:9], refs[9]
    ff, width = weights[1].shape
    transposed = ((1,), (1,))
    pieces = []
    for n in (0, 2):
        for j in range(0, ff, BLOCK):
            pieces.append((weights[n].at[:, j : j + BLOCK], buffers[n].at[:, j : j + BLOCK]))
            pieces.append((weights[n + 1].at[j : j + BLOCK, :], buffers[n + 1].at[j : j + BLOCK, :]))
    copies = fetches(pieces, sems)
    slabs = [jnp.concatenate([b[...] for b in blocks[n : n + GROUP]], 0) for n in range(0, experts, GROUP)]
    unpack(slabs, [rows_ref, grads_ref], cap)
    up_a, up_b = buffers[0], buffers[2]
    for n in range(2):
        up, down = buffers[2 * n], buffers[2 * n + 1]
        for j in range(0, ff, BLOCK):
            next(copies).wait()
            next(copies).wait()
            slope = gelu_slope(dot(rows_ref[...], up[:, j : j + BLOCK]))
            act_grad = dot(grads_ref[...], down[j : j + BLOCK, :], transposed)
            pre_ref[:, n * ff + j : n * ff + j + BLOCK] = (act_grad * slope).astype(bf16)
    for j in range(0, width, BLOCK):
        cols = slice(j, j + BLOCK)
        both = dot(pre_ref[:, :ff], up_a[cols, :], transposed) + dot(pre_ref[:, ff:], up_b[cols, :], transposed)
        sum_ref[:, cols] = both.astype(bf16)
    size = SPLIT * cap
    own_z, own_y = place_ref[0] >> (side.bit_length() - 1), place_ref[0] & (side - 1)
    for n, rows in repack(sum_ref, cap):
        for i in range(GROUP):
            behind = n * GROUP + i
            z, y = (own_z - behind // side) & (side - 1), (own_y - behind % side) & (side - 1)
            out_ref[z * side + y] = rows[i * size : (i + 1) * size, :]


def combine_fwd_body(r_ref, gate_ref, route_ref, x_ref, mod_ref, out_ref, *, experts, cap):
    tokens, width = x_ref.shape
    part = width // SPLIT
    first = slot_rows(route_ref[...], experts, SPLIT * cap)
    numbers = iota((r_ref.shape[0], tokens), 0)
    for h in range(SPLIT):
        weights = sum(jnp.where(numbers == first[k] + h * cap, gate_ref[k : k + 1, :], 0.0) for k in range(2))
        high = weights.astype(bf16)
        low = (weights - high.astype(f32)).astype(bf16)
        both = dot(high, r_ref[...], ((0,), (0,))) + dot(low, r_ref[...], ((0,), (0,)))
        cols = slice(h * part, (h + 1) * part)
        out_ref[:, cols] = x_ref[:, cols] + mod_ref[2][:, cols] * both


def combine_bwd_body(r_ref, where_ref, norm_far, inv_ref, g_far, mod_ref, out_ref, norm_ref, g_ref, sems, *, cap):
    copies = fetches([(norm_far, norm_ref), (g_far, g_ref)], sems)
    tokens = norm_ref.shape[0]
    numbers = iota((tokens, r_ref.shape[0]), 1)
    places = where_ref[...]
    halves = []
    for h in range(SPLIT):
        hit = (numbers == places[:, 2:3] + h * cap) | (numbers == places[:, 3:4] + h * cap)
        halves.append(dot(ones_where(hit).astype(bf16), r_ref[...]))
    dnorm = jnp.concatenate(halves, 1) * (1.0 + mod_ref[1])
    mean_one = jnp.mean(dnorm, axis=-1, keepdims=True)
    next(copies).wait()
    normed = norm_ref[...]
    mean_two = jnp.mean(dnorm * normed, axis=-1, keepdims=True)
    next(copies).wait()
    grad = g_ref[...].astype(f32) + (dnorm - mean_one - normed * mean_two) * inv_ref[...]
    out_ref[...] = grad.astype(bf16)


def in_hbm(*arrays):
    return [pltpu.with_memory_space_constraint(a, pltpu.HBM) for a in arrays]


def in_vmem(*arrays):
    return [pltpu.with_memory_space_constraint(a, pltpu.VMEM) for a in arrays]


def call(body, outs, args, flops, limit, scratch=(), scalars=0, far=(), **statics):
    return kernel(body, outs, args, flops, limit, scratch, scalars, far, **statics)


def kernel(body, outs, args, flops, limit, scratch, scalars, far, **statics):
    moved = sum(2 * a.size for a in args)
    specs = [pl.BlockSpec(memory_space=pltpu.SMEM) if n < scalars else pl.BlockSpec() for n in range(len(args))]
    for n in far:
        specs[n] = pl.BlockSpec(memory_space=pltpu.HBM)
    return pl.pallas_call(
        functools.partial(body, **statics),
        out_shape=outs,
        in_specs=specs,
        scratch_shapes=scratch,
        cost_estimate=pl.CostEstimate(flops=flops, bytes_accessed=moved, transcendentals=0),
        compiler_params=pltpu.CompilerParams(vmem_limit_bytes=limit << 20),
    )(*args)


def shifted(value, axis, steps):
    count = lax.axis_size(axis)
    leading, last = (max(0, -steps), min(count, count - steps))
    return lax.ppermute(value, axis, [(source, source + steps) for source in range(leading, last)])


def offset_by(block, number, side):
    units = lax.axis_size("expert")
    cores = units // (side * side)
    pairs = []
    for u in range(units):
        chip, core = u // cores, u % cores
        z, y = (chip // side + number // side) % side, (chip + number) % side
        pairs.append((u, (z * side + y) * cores + core))
    return lax.ppermute(block, "expert", pairs)


def exchange(rows, experts):
    units = lax.axis_size("expert")
    cores = units // experts
    groups = [[e * cores + c for e in range(experts)] for c in range(cores)]
    parts = rows.reshape(experts, -1, rows.shape[1])
    swapped = lax.all_to_all(parts, "expert", 0, 0, axis_index_groups=groups, tiled=True)
    return swapped.reshape(rows.shape)


def tick(
    section_inputs,
    stored_inputs,
    out_grads,
    fwd_routes,
    fwd_gates,
    fwd_modulation,
    bwd_routes,
    bwd_gates,
    bwd_modulation,
    up_weight,
    down_weight,
):
    units = lax.axis_size("expert")
    experts = units // 2
    tokens, width = section_inputs.shape[1:]
    cap = min(tokens, 5 * tokens // (2 * experts))
    slots = experts * cap
    ff = up_weight.shape[3]
    shape = jax.ShapeDtypeStruct
    sizes = dict(experts=experts, cap=cap)

    inputs, stored, grads = section_inputs[0], stored_inputs[0], out_grads[0]
    routes, gates = fwd_routes[0].T, fwd_gates[0].T
    routes_b, gates_b = bwd_routes[0].T, bwd_gates[0].T
    mod = fwd_modulation.reshape(3, 1, width)
    mod_b = bwd_modulation.reshape(3, 1, width)
    own = (up_weight[0, 0], down_weight[0, 0])
    swap = [(i, i ^ 1) for i in range(units)]
    weights = in_hbm(*own, *(lax.ppermute(w, "expert", swap) for w in own))
    side = 1 << (experts.bit_length() // 2)
    place = (lax.axis_index("expert") >> 1).astype(jnp.int32).reshape(1)
    half = width // SPLIT

    (send,) = call(
        pack_fwd_body,
        [shape((SPLIT * slots, half), bf16)],
        (inputs, mod, routes),
        4 * tokens * slots * width,
        60,
        **sizes,
    )
    got = exchange(send, experts)

    *blocks, normed_b, inv_b, where_b = call(
        pack_bwd_body,
        [pltpu.HBM((2 * SPLIT * cap, half), bf16)] * experts
        + [pltpu.HBM((tokens, width), f32), shape((tokens, 1), f32), shape((tokens, 8), jnp.int32)],
        (place, stored, grads, gates_b, mod_b, routes_b),
        12 * tokens * slots * width,
        28,
        scalars=1,
        side=side,
        **sizes,
    )
    got_b = in_hbm(blocks[0]) + [offset_by(b, n, side) for n, b in enumerate(blocks) if n > 0]

    rows_buffer = pltpu.VMEM((slots, width), bf16)
    hidden_buffer = pltpu.VMEM((slots, 2 * ff), bf16)
    weight_buffers = [pltpu.VMEM(w.shape, bf16) for w in weights] + [pltpu.SemaphoreType.DMA((16,))]
    (result,) = call(
        expert_fwd_body,
        [pltpu.HBM((SPLIT * slots, half), bf16)],
        (*in_vmem(got), *weights),
        8 * slots * width * ff,
        30,
        scratch=[rows_buffer, hidden_buffer, rows_buffer] + weight_buffers,
        far=(1, 2, 3, 4),
        cap=cap,
    )
    back = exchange(result, experts)
    (result_b,) = call(
        expert_bwd_body,
        [pltpu.HBM((experts, SPLIT * cap, half), bf16)],
        (place, *got_b, *weights),
        12 * slots * width * ff,
        36,
        scratch=[rows_buffer, rows_buffer, hidden_buffer, rows_buffer] + weight_buffers,
        far=range(experts + 1, experts + 5),
        scalars=1,
        cap=cap,
        side=side,
    )
    back_b = exchange(result_b.reshape(SPLIT * slots, half), experts)

    (out_fwd,) = call(
        combine_fwd_body,
        [pltpu.HBM((tokens, width), f32)],
        (*in_vmem(back), gates, routes, *in_hbm(inputs), mod),
        8 * tokens * slots * width,
        16,
        **sizes,
    )
    next_inputs = shifted(out_fwd[None], "section", 1)
    (section_grad,) = call(
        combine_bwd_body,
        [shape((tokens, width), bf16)],
        (*in_vmem(back_b), where_b, *in_hbm(normed_b), inv_b, *in_hbm(grads), mod_b),
        4 * tokens * slots * width,
        16,
        scratch=[pltpu.VMEM((tokens, width), f32), pltpu.VMEM((tokens, width), bf16), pltpu.SemaphoreType.DMA((2,))],
        far=(2, 4),
        cap=cap,
    )
    input_grads = shifted(section_grad[None], "section", -1)
    return (next_inputs, input_grads)


def solution(mesh):
    rows = P("section", "expert", None)
    mod = P("section", None, None)
    weight = P("section", "expert", None, None)
    placed = (rows, rows, rows, rows, rows, mod, rows, rows, mod, weight, weight)
    return jax.shard_map(tick, mesh=mesh, in_specs=placed, out_specs=(rows, rows), check_vma=False)
```

time: 147 us -> 164 us (1.12)
  starting transfers between devices: 28 us -> 63.6 us
  Pallas kernels: 50.8 us -> 39 us
  waiting for transfers between devices: 61.3 us -> 57.6 us
  local copies, waits for them, and re-layouts: 5.5 us -> 1.84 us
    all_to_all x4 -> x3, waiting for transfers between devices: 50.3 us -> 16.4 us  [exchange(): lax.all_to_all(parts, 'expert', 0, 0, axis_index_groups=groups, tiled=True)]
    ppermute x2 -> x17, starting transfers between devices: 0.58 us -> 33.6 us  [the longest x15 33 us: offset_by(): return lax.ppermute(block, 'expert', pairs)]
    ppermute x2 -> x17, waiting for transfers between devices: 0.01 us -> 30.6 us  [the longest x15 30.6 us: offset_by(): return lax.ppermute(block, 'expert', pairs)]
    pallas_call x6, Pallas kernels: 50.8 us -> 39 us  [kernel(): pl.pallas_call(functools.partial(body, **statics), out_shape=outs, in_spe...]
    unnamed x10 -> x34, local copies, waits for them, and re-layouts: 5.5 us -> 1.84 us
    all_to_all x4 -> x3, starting transfers between devices: 22.7 us -> 25.3 us  [exchange(): lax.all_to_all(parts, 'expert', 0, 0, axis_index_groups=groups, tiled=True)]
  transfers between devices with their start and end apart: 8 -> 22, of which waited for: 4 -> 9; matrix products, arithmetic and copies ran while one was open for 0% -> 0% of each run, Pallas kernels for 35% -> 24%
where the time goes in v1:
time: 164 us; the launch traced here: 163 us
  starting transfers between devices  63.6 us (39%)
  waiting for transfers between devices  57.6 us (35%)
  Pallas kernels  39 us (24%)
  local copies, waits for them, and re-layouts  1.84 us (1%)
    pallas_call x6, Pallas kernels, kernel(): pl.pallas_call(functools.partial(body, **statics), out_shape=outs, in_spe...  39 us
    ppermute x15, starting transfers between devices, offset_by(): return lax.ppermute(block, 'expert', pairs)  33 us
    ppermute x15, waiting for transfers between devices, offset_by(): return lax.ppermute(block, 'expert', pairs)  30.6 us
    all_to_all x3, starting transfers between devices, exchange(): lax.all_to_all(parts, 'expert', 0, 0, axis_index_groups=groups, tiled=True)  25.3 us
    all_to_all x3, waiting for transfers between devices, exchange(): lax.all_to_all(parts, 'expert', 0, 0, axis_index_groups=groups, tiled=True)  16.4 us
    ppermute x2, waiting for transfers between devices, shifted(): lax.ppermute(value, axis, [(source, source + steps) for source in range(l...  10.6 us
    ppermute x2, starting transfers between devices, shifted(): lax.ppermute(value, axis, [(source, source + steps) for source in range(l...  4.72 us
  transfers between devices with their start and end apart: 22, of which 9 were waited for; matrix products, arithmetic and copies ran while one was open for 0% of the time, Pallas kernels for 24%

profile of v1, /device:TPU:0, one launch (start us, length us, event | category | flops | bytes accessed | tf_op | source)
XLA Modules:
  0.0 163.0 jit_solution(5415477058578533280)
XLA Ops:
  1.2 3.1 %shard_map.122 = bf16[640,1024]{1,0:T(8,128)(2,1)} custom-call(f32[128,2048]{1,0:T(8,128)} %bitcast.44, f32[3,1,2048]{2,1,0:T(1,128)} %bitcast.33, s32[2,128]{1,0:T(2,128)} %bitcast.37), custom_call_target="tpu_custom_call" | custom-call | flops 335544320 | bytes 537088 | tf_op jit(solution)/shard_map/pallas_call | solution.py:264
  4.4 8.3 %all-to-all-start = ((bf16[16,40,1024]{2,1,0:T(8,128)(2,1)}), bf16[16,40,1024]{2,1,0:T(8,128)(2,1)S(1)}, u32[]{:S(2)}, u32[]{:S(2)}) async-start(bf16[16,40,1024]{2,1,0:T(8,128)(2,1)} %bitcast.43), calls=%async_computation | async-start | bytes 2621440 | tf_op jit(solution)/shard_map/all_to_all | solution.py:296
  12.8 4.3 %shard_map.125 = (bf16[80,1024]{1,0:T(8,128)(2,1)}, bf16[80,1024]{1,0:T(8,128)(2,1)}, bf16[80,1024]{1,0:T(8,128)(2,1)}, bf16[80,1024]{1,0:T(8,128)(2,1)}, bf16[8...) custom-call(s32[1]{0:T(128)} %bitcast.13.place_ref, ...), custom_call_target="tpu_custom_call" | custom-call | flops 1006632960 | bytes 1061890 | tf_op jit(solution)/shard_map/pallas_call | solution.py:264
  17.0 3.4 %collective-permute-start.10 = (bf16[80,1024]{1,0:T(8,128)(2,1)}, bf16[80,1024]{1,0:T(8,128)(2,1)S(1)}, u32[]{:S(2)}, u32[]{:S(2)}) collective-permute-start(bf16[80,1024]{1,0:T(8,128)(2,1)} %get-tuple-element.29), channel_id=1, source_target_pairs={{0,16},{1,17},{2,18},{3,19},{4,20},{5,21},{6,22},{7,23},{8,24},{9,... | collective-permute-start | bytes 491528 | tf_op jit(solution)/shard_map/ppermute | solution.py:288
  20.5 1.5 collective-permute-start.11
  21.9 5.1 %collective-permute-start.12 = (bf16[80,1024]{1,0:T(8,128)(2,1)}, bf16[80,1024]{1,0:T(8,128)(2,1)S(1)}, u32[]{:S(2)}, u32[]{:S(2)}) collective-permute-start(bf16[80,1024]{1,0:T(8,128)(2,1)} %get-tuple-element.31), channel_id=1, source_target_pairs={{0,20},{1,21},{2,22},{3,23},{4,16},{5,17},{6,18},{7,19},{8,28},{9,... | collective-permute-start | bytes 491528 | tf_op jit(solution)/shard_map/ppermute | solution.py:288
  27.0 1.5 collective-permute-start.13
  28.5 2.7 %collective-permute-start.14 = (bf16[80,1024]{1,0:T(8,128)(2,1)}, bf16[80,1024]{1,0:T(8,128)(2,1)}, u32[]{:S(2)}, u32[]{:S(2)}) collective-permute-start(bf16[80,1024]{1,0:T(8,128)(2,1)} %get-tuple-element.33), channel_id=1, source_target_pairs={{0,24},{1,25},{2,26},{3,27},{4,28},{5,29},{6,30},{7,31},{8,0},{9,1... | collective-permute-start | bytes 491528 | tf_op jit(solution)/shard_map/ppermute | solution.py:288
  31.1 4.9 %all-to-all-done = bf16[16,40,1024]{2,1,0:T(8,128)(2,1)S(1)} async-done(((bf16[16,40,1024]{2,1,0:T(8,128)(2,1)}), bf16[16,40,1024]{2,1,0:T(8,128)(2,1)S(1)}, u32[]{:S(2)}, u32[]{:S(2)}) %all-to-all-start) | async-done | bytes 1310752 | tf_op jit(solution)/shard_map/all_to_all | solution.py:296
  36.0 10.7 %shard_map.123 = bf16[640,1024]{1,0:T(8,128)(2,1)} custom-call(bf16[640,1024]{1,0:T(8,128)(2,1)S(1)} %bitcast.29, bf16[2048,1024]{1,0:T(8,128)(2,1)} %bitcast.49, bf16[1024,2048]{1,0:T(8,128)(2,1)} %bitcast.52, bf16[2048,1024]{1,0:T(8,128)(2,1)} %collective-permute-done.refs_2_.refs_18_, bf16[1024,2048]{1,0:T(8,128)(2,1)} %collective-permute-done.1.refs_3_.refs_19_), custom_call_target="tpu_custom_call" | custom-call | flops 5368709120 | bytes 18087936 | tf_op jit(solution)/shard_map/pallas_call | solution.py:264
  46.8 13.3 %all-to-all-start.1 = ((bf16[16,40,1024]{2,1,0:T(8,128)(2,1)}), bf16[16,40,1024]{2,1,0:T(8,128)(2,1)S(1)}, u32[]{:S(2)}, u32[]{:S(2)}) async-start(bf16[16,40,1024]{2,1,0:T(8,128)(2,1)} %bitcast.46), calls=%async_computation.1 | async-start | bytes 2621440 | tf_op jit(solution)/shard_map/all_to_all | solution.py:296
  60.1 4.3 %collective-permute-start.15 = (bf16[80,1024]{1,0:T(8,128)(2,1)}, bf16[80,1024]{1,0:T(8,128)(2,1)S(1)}, u32[]{:S(2)}, u32[]{:S(2)}) collective-permute-start(bf16[80,1024]{1,0:T(8,128)(2,1)} %get-tuple-element.34), channel_id=1, source_target_pairs={{0,26},{1,27},{2,28},{3,29},{4,30},{5,31},{6,24},{7,25},{8,2},{9,3... | collective-permute-start | bytes 491528 | tf_op jit(solution)/shard_map/ppermute | solution.py:288
  64.4 3.0 %collective-permute-start.16 = (bf16[80,1024]{1,0:T(8,128)(2,1)}, bf16[80,1024]{1,0:T(8,128)(2,1)S(1)}, u32[]{:S(2)}, u32[]{:S(2)}) collective-permute-start(bf16[80,1024]{1,0:T(8,128)(2,1)} %get-tuple-element.35), channel_id=1, source_target_pairs={{0,28},{1,29},{2,30},{3,31},{4,24},{5,25},{6,26},{7,27},{8,4},{9,5... | collective-permute-start | bytes 491528 | tf_op jit(solution)/shard_map/ppermute | solution.py:288
  67.4 1.5 collective-permute-start.17
  69.4 1.0 collective-permute-start.4
  70.4 14.1 %collective-permute-done.15.refs_13_ = bf16[80,1024]{1,0:T(8,128)(2,1)S(1)} collective-permute-done((bf16[80,1024]{1,0:T(8,128)(2,1)}, bf16[80,1024]{1,0:T(8,128)(2,1)S(1)}, u32[]{:S(2)}, u32[]{:S(2)}) %collective-permute-start.15) | collective-permute-done | bytes 163872 | tf_op jit(solution)/shard_map/ppermute | solution.py:288
  84.5 5.6 %collective-permute-start.5 = (bf16[80,1024]{1,0:T(8,128)(2,1)S(1)}, bf16[80,1024]{1,0:T(8,128)(2,1)S(1)}, u32[]{:S(2)}, u32[]{:S(2)}) collective-permute-start(bf16[80,1024]{1,0:T(8,128)(2,1)S(1)} %copy-done.12), channel_id=1, source_target_pairs={{0,6},{1,7},{2,0},{3,1},{4,2},{5,3},{6,4},{7,5},{8,14},{9,15},{10,... | collective-permute-start | bytes 491528 | tf_op jit(solution)/shard_map/ppermute | solution.py:288
  90.1 1.6 %collective-permute-done.16.refs_14_ = bf16[80,1024]{1,0:T(8,128)(2,1)S(1)} collective-permute-done((bf16[80,1024]{1,0:T(8,128)(2,1)}, bf16[80,1024]{1,0:T(8,128)(2,1)S(1)}, u32[]{:S(2)}, u32[]{:S(2)}) %collective-permute-start.16) | collective-permute-done | bytes 163872 | tf_op jit(solution)/shard_map/ppermute | solution.py:288
  91.8 2.2 %collective-permute-start.6 = (bf16[80,1024]{1,0:T(8,128)(2,1)S(1)}, bf16[80,1024]{1,0:T(8,128)(2,1)S(1)}, u32[]{:S(2)}, u32[]{:S(2)}) collective-permute-start(bf16[80,1024]{1,0:T(8,128)(2,1)S(1)} %copy-done.11), channel_id=1, source_target_pairs={{0,8},{1,9},{2,10},{3,11},{4,12},{5,13},{6,14},{7,15},{8,16},{9,17... | collective-permute-start | bytes 491528 | tf_op jit(solution)/shard_map/ppermute | solution.py:288
  94.8 4.4 %collective-permute-done.4.refs_2_ = bf16[80,1024]{1,0:T(8,128)(2,1)S(1)} collective-permute-done((bf16[80,1024]{1,0:T(8,128)(2,1)S(1)}, bf16[80,1024]{1,0:T(8,128)(2,1)S(1)}, u32[]{:S(2)}, u32[]{:S(2)}) %collective-permute-start.4) | collective-permute-done | bytes 163872 | tf_op jit(solution)/shard_map/ppermute | solution.py:288
  99.2 5.5 %collective-permute-done.7.refs_5_ = bf16[80,1024]{1,0:T(8,128)(2,1)S(1)} collective-permute-done((bf16[80,1024]{1,0:T(8,128)(2,1)S(1)}, bf16[80,1024]{1,0:T(8,128)(2,1)S(1)}, u32[]{:S(2)}, u32[]{:S(2)}) %collective-permute-start.7) | collective-permute-done | bytes 163872 | tf_op jit(solution)/shard_map/ppermute | solution.py:288
  104.8 3.8 %collective-permute-done.8.refs_6_ = bf16[80,1024]{1,0:T(8,128)(2,1)S(1)} collective-permute-done((bf16[80,1024]{1,0:T(8,128)(2,1)S(1)}, bf16[80,1024]{1,0:T(8,128)(2,1)S(1)}, u32[]{:S(2)}, u32[]{:S(2)}) %collective-permute-start.8) | collective-permute-done | bytes 163872 | tf_op jit(solution)/shard_map/ppermute | solution.py:288
  108.6 1.0 collective-permute-done.9.refs_7_
  109.6 15.2 %shard_map.126 = bf16[16,40,1024]{2,1,0:T(8,128)(2,1)} custom-call(s32[1]{0:T(128)} %bitcast.13.place_ref, bf16[80,1024]{1,0:T(8,128)(2,1)} %get-tuple-element.21.refs_0_, bf16[80,1024]{1,0:T(8,128)(2,1)S(1)} %collective-permute-done.3.refs_1_, bf16[80,1024]{1,0:T(8,128)(2,1)S(1)} %collective-permute-done.4.refs_2_, ...), custom_call_target="tpu_custom_call" | custom-call | flops 8053063680 | bytes 19398658 | tf_op jit(solution)/shard_map/pallas_call | solution.py:264
  124.9 3.7 %all-to-all-start.2 = ((bf16[16,40,1024]{2,1,0:T(8,128)(2,1)}), bf16[16,40,1024]{2,1,0:T(8,128)(2,1)S(1)}, u32[]{:S(2)}, u32[]{:S(2)}) async-start(bf16[16,40,1024]{2,1,0:T(8,128)(2,1)} %shard_map.126), calls=%async_computation.2 | async-start | bytes 2621440 | tf_op jit(solution)/shard_map/all_to_all | solution.py:296
  128.6 3.5 %shard_map.124 = f32[128,2048]{1,0:T(8,128)} custom-call(bf16[640,1024]{1,0:T(8,128)(2,1)S(1)} %bitcast.28, f32[2,128]{1,0:T(2,128)S(1)} %bitcast.39, s32[2,128]{1,0:T(2,128)S(1)} %bitcast.38, f32[128,2048]{1,0:T(8,128)} %bitcast.45, f32[3,1,2048]{2,1,0:T(1,128)S(1)} %bitcast.34), custom_call_target="tpu_custom_call" | custom-call | flops 671088640 | bytes 1848320 | tf_op jit(solution)/shard_map/pallas_call | solution.py:264
  132.1 3.4 %collective-permute-start.2 = (f32[1,128,2048]{2,1,0:T(8,128)}, f32[1,128,2048]{2,1,0:T(8,128)S(1)}, u32[]{:S(2)}, u32[]{:S(2)}) collective-permute-start(f32[1,128,2048]{2,1,0:T(8,128)} %bitcast.47), channel_id=1, source_target_pairs={{0,32},{32,64},{64,96},{1,33},{33,65},{65,97},{2,34},{34,66},{66,9... | collective-permute-start | bytes 3145736 | tf_op jit(solution)/shard_map/ppermute | solution.py:277
  135.5 11.6 %all-to-all-done.2 = bf16[16,40,1024]{2,1,0:T(8,128)(2,1)S(1)} async-done(((bf16[16,40,1024]{2,1,0:T(8,128)(2,1)}), bf16[16,40,1024]{2,1,0:T(8,128)(2,1)S(1)}, u32[]{:S(2)}, u32[]{:S(2)}) %all-to-all-start.2) | async-done | bytes 1310752 | tf_op jit(solution)/shard_map/all_to_all | solution.py:296
  147.1 2.2 %shard_map.127 = bf16[128,2048]{1,0:T(8,128)(2,1)S(1)} custom-call(bf16[640,1024]{1,0:T(8,128)(2,1)S(1)} %bitcast.27, s32[128,8]{1,0:T(8,128)S(1)} %get-tuple-element.37.where_ref, f32[128,2048]{1,0:T(8,128)} %get-tuple-element.38.norm_far, f32[128,1]{1,0:T(8,128)S(1)} %get-tuple-element.39.inv_ref, bf16[128,2048]{1,0:T(8,128)(2,1)} %bitcast.30, ...), custom_call_target="tpu_custom_call" | custom-call | flops 335544320 | bytes 2373888 | tf_op jit(solution)/shard_map/pallas_call | solution.py:264
  149.3 1.3 collective-permute-start.18
  150.6 10.6 %collective-permute-done.18 = bf16[1,128,2048]{2,1,0:T(8,128)(2,1)S(1)} collective-permute-done((bf16[1,128,2048]{2,1,0:T(8,128)(2,1)S(1)}, bf16[1,128,2048]{2,1,0:T(8,128)(2,1)S(1)}, u32[]{:S(2)}, u32[]{:S(2)}) %collective-permute-start.18) | collective-permute-done | bytes 524320 | tf_op jit(solution)/shard_map/ppermute | solution.py:277
  161.3 1.0 copy.15
  (52 shorter events, 2.9 us)
Async XLA Ops:
  0.6 26.4 %collective-permute-start = (bf16[2048,1024]{1,0:T(8,128)(2,1)}, bf16[2048,1024]{1,0:T(8,128)(2,1)}, u32[]{:S(2)}, u32[]{:S(2)}) collective-permute-start(bf16[2048,1024]{1,0:T(8,128)(2,1)} %bitcast.48), channel_id=1, source_target_pairs={{0,1},{1,0},{2,3},{3,2},{4,5},{5,4},{6,7},{7,6},{8,9},{9,8},{10,11... | collective-permute-start | bytes 12582920 | tf_op jit(solution)/shard_map/ppermute | solution.py:329
  0.7 27.7 %collective-permute-start.1 = (bf16[1024,2048]{1,0:T(8,128)(2,1)}, bf16[1024,2048]{1,0:T(8,128)(2,1)}, u32[]{:S(2)}, u32[]{:S(2)}) collective-permute-start(bf16[1024,2048]{1,0:T(8,128)(2,1)} %bitcast.51), channel_id=1, source_target_pairs={{0,1},{1,0},{2,3},{3,2},{4,5},{5,4},{6,7},{7,6},{8,9},{9,8},{10,11... | collective-permute-start | bytes 12582920 | tf_op jit(solution)/shard_map/ppermute | solution.py:329
  4.4 8.4 %copy-start.6 = (f32[1,128,2]{1,2,0:T(2,128)S(1)}, f32[1,128,2]{1,2,0:T(2,128)}, u32[]{:S(2)}) copy-start(f32[1,128,2]{1,2,0:T(2,128)} %param.18) | copy-start | bytes 3076
  4.4 8.4 %copy-start.7 = (s32[1,128,2]{1,2,0:T(2,128)S(1)}, s32[1,128,2]{1,2,0:T(2,128)}, u32[]{:S(2)}) copy-start(s32[1,128,2]{1,2,0:T(2,128)} %param.17) | copy-start | bytes 3076
  4.4 31.6 %all-to-all-start = ((bf16[16,40,1024]{2,1,0:T(8,128)(2,1)}), bf16[16,40,1024]{2,1,0:T(8,128)(2,1)S(1)}, u32[]{:S(2)}, u32[]{:S(2)}) async-start(bf16[16,40,1024]{2,1,0:T(8,128)(2,1)} %bitcast.43), calls=%async_computation | async-start | bytes 2621440 | tf_op jit(solution)/shard_map/all_to_all | solution.py:296
  17.0 43.1 %collective-permute-start.10 = (bf16[80,1024]{1,0:T(8,128)(2,1)}, bf16[80,1024]{1,0:T(8,128)(2,1)S(1)}, u32[]{:S(2)}, u32[]{:S(2)}) collective-permute-start(bf16[80,1024]{1,0:T(8,128)(2,1)} %get-tuple-element.29), channel_id=1, source_target_pairs={{0,16},{1,17},{2,18},{3,19},{4,20},{5,21},{6,22},{7,23},{8,24},{9,... | collective-permute-start | bytes 491528 | tf_op jit(solution)/shard_map/ppermute | solution.py:288
  20.5 43.9 %collective-permute-start.11 = (bf16[80,1024]{1,0:T(8,128)(2,1)}, bf16[80,1024]{1,0:T(8,128)(2,1)S(1)}, u32[]{:S(2)}, u32[]{:S(2)}) collective-permute-start(bf16[80,1024]{1,0:T(8,128)(2,1)} %get-tuple-element.30), channel_id=1, source_target_pairs={{0,18},{1,19},{2,20},{3,21},{4,22},{5,23},{6,16},{7,17},{8,26},{9,... | collective-permute-start | bytes 491528 | tf_op jit(solution)/shard_map/ppermute | solution.py:288
  21.9 45.5 %collective-permute-start.12 = (bf16[80,1024]{1,0:T(8,128)(2,1)}, bf16[80,1024]{1,0:T(8,128)(2,1)S(1)}, u32[]{:S(2)}, u32[]{:S(2)}) collective-permute-start(bf16[80,1024]{1,0:T(8,128)(2,1)} %get-tuple-element.31), channel_id=1, source_target_pairs={{0,20},{1,21},{2,22},{3,23},{4,16},{5,17},{6,18},{7,19},{8,28},{9,... | collective-permute-start | bytes 491528 | tf_op jit(solution)/shard_map/ppermute | solution.py:288
  27.0 41.8 %collective-permute-start.13 = (bf16[80,1024]{1,0:T(8,128)(2,1)}, bf16[80,1024]{1,0:T(8,128)(2,1)S(1)}, u32[]{:S(2)}, u32[]{:S(2)}) collective-permute-start(bf16[80,1024]{1,0:T(8,128)(2,1)} %get-tuple-element.32), channel_id=1, source_target_pairs={{0,22},{1,23},{2,16},{3,17},{4,18},{5,19},{6,20},{7,21},{8,30},{9,... | collective-permute-start | bytes 491528 | tf_op jit(solution)/shard_map/ppermute | solution.py:288
  28.5 41.0 %collective-permute-start.14 = (bf16[80,1024]{1,0:T(8,128)(2,1)}, bf16[80,1024]{1,0:T(8,128)(2,1)}, u32[]{:S(2)}, u32[]{:S(2)}) collective-permute-start(bf16[80,1024]{1,0:T(8,128)(2,1)} %get-tuple-element.33), channel_id=1, source_target_pairs={{0,24},{1,25},{2,26},{3,27},{4,28},{5,29},{6,30},{7,31},{8,0},{9,1... | collective-permute-start | bytes 491528 | tf_op jit(solution)/shard_map/ppermute | solution.py:288
  46.7 20.7 %copy-start.15 = (bf16[80,1024]{1,0:T(8,128)(2,1)S(1)}, bf16[80,1024]{1,0:T(8,128)(2,1)}, u32[]{:S(2)}) copy-start(bf16[80,1024]{1,0:T(8,128)(2,1)} %get-tuple-element.36) | copy-start | bytes 491524
  46.7 22.1 %copy-start.14 = (bf16[80,1024]{1,0:T(8,128)(2,1)S(1)}, bf16[80,1024]{1,0:T(8,128)(2,1)}, u32[]{:S(2)}) copy-start(bf16[80,1024]{1,0:T(8,128)(2,1)} %get-tuple-element.22) | copy-start | bytes 491524
  46.7 22.7 %copy-start.13 = (bf16[80,1024]{1,0:T(8,128)(2,1)S(1)}, bf16[80,1024]{1,0:T(8,128)(2,1)}, u32[]{:S(2)}) copy-start(bf16[80,1024]{1,0:T(8,128)(2,1)} %get-tuple-element.23) | copy-start | bytes 491524
  46.8 37.8 %copy-start.12 = (bf16[80,1024]{1,0:T(8,128)(2,1)S(1)}, bf16[80,1024]{1,0:T(8,128)(2,1)}, u32[]{:S(2)}) copy-start(bf16[80,1024]{1,0:T(8,128)(2,1)} %get-tuple-element.24) | copy-start | bytes 491524
  46.8 45.0 %copy-start.11 = (bf16[80,1024]{1,0:T(8,128)(2,1)S(1)}, bf16[80,1024]{1,0:T(8,128)(2,1)}, u32[]{:S(2)}) copy-start(bf16[80,1024]{1,0:T(8,128)(2,1)} %get-tuple-element.25) | copy-start | bytes 491524
  46.8 47.2 %copy-start.10 = (bf16[80,1024]{1,0:T(8,128)(2,1)S(1)}, bf16[80,1024]{1,0:T(8,128)(2,1)}, u32[]{:S(2)}) copy-start(bf16[80,1024]{1,0:T(8,128)(2,1)} %get-tuple-element.26) | copy-start | bytes 491524
  46.8 47.2 %copy-start.9 = (bf16[80,1024]{1,0:T(8,128)(2,1)S(1)}, bf16[80,1024]{1,0:T(8,128)(2,1)}, u32[]{:S(2)}) copy-start(bf16[80,1024]{1,0:T(8,128)(2,1)} %get-tuple-element.27) | copy-start | bytes 491524
  46.8 52.4 %copy-start.8 = (bf16[80,1024]{1,0:T(8,128)(2,1)S(1)}, bf16[80,1024]{1,0:T(8,128)(2,1)}, u32[]{:S(2)}) copy-start(bf16[80,1024]{1,0:T(8,128)(2,1)} %get-tuple-element.28) | copy-start | bytes 491524
  46.8 78.1 %all-to-all-start.1 = ((bf16[16,40,1024]{2,1,0:T(8,128)(2,1)}), bf16[16,40,1024]{2,1,0:T(8,128)(2,1)S(1)}, u32[]{:S(2)}, u32[]{:S(2)}) async-start(bf16[16,40,1024]{2,1,0:T(8,128)(2,1)} %bitcast.46), calls=%async_computation.1 | async-start | bytes 2621440 | tf_op jit(solution)/shard_map/all_to_all | solution.py:296
  60.1 24.4 %collective-permute-start.15 = (bf16[80,1024]{1,0:T(8,128)(2,1)}, bf16[80,1024]{1,0:T(8,128)(2,1)S(1)}, u32[]{:S(2)}, u32[]{:S(2)}) collective-permute-start(bf16[80,1024]{1,0:T(8,128)(2,1)} %get-tuple-element.34), channel_id=1, source_target_pairs={{0,26},{1,27},{2,28},{3,29},{4,30},{5,31},{6,24},{7,25},{8,2},{9,3... | collective-permute-start | bytes 491528 | tf_op jit(solution)/shard_map/ppermute | solution.py:288
  64.4 27.4 %collective-permute-start.16 = (bf16[80,1024]{1,0:T(8,128)(2,1)}, bf16[80,1024]{1,0:T(8,128)(2,1)S(1)}, u32[]{:S(2)}, u32[]{:S(2)}) collective-permute-start(bf16[80,1024]{1,0:T(8,128)(2,1)} %get-tuple-element.35), channel_id=1, source_target_pairs={{0,28},{1,29},{2,30},{3,31},{4,24},{5,25},{6,26},{7,27},{8,4},{9,5... | collective-permute-start | bytes 491528 | tf_op jit(solution)/shard_map/ppermute | solution.py:288
  67.4 26.6 %collective-permute-start.17 = (bf16[80,1024]{1,0:T(8,128)(2,1)S(1)}, bf16[80,1024]{1,0:T(8,128)(2,1)S(1)}, u32[]{:S(2)}, u32[]{:S(2)}) collective-permute-start(bf16[80,1024]{1,0:T(8,128)(2,1)S(1)} %copy-done.15), channel_id=1, source_target_pairs={{0,30},{1,31},{2,24},{3,25},{4,26},{5,27},{6,28},{7,29},{8,6},{9,7... | collective-permute-start | bytes 491528 | tf_op jit(solution)/shard_map/ppermute | solution.py:288
  68.8 25.1 %collective-permute-start.3 = (bf16[80,1024]{1,0:T(8,128)(2,1)S(1)}, bf16[80,1024]{1,0:T(8,128)(2,1)S(1)}, u32[]{:S(2)}, u32[]{:S(2)}) collective-permute-start(bf16[80,1024]{1,0:T(8,128)(2,1)S(1)} %copy-done.14), channel_id=1, source_target_pairs={{0,2},{1,3},{2,4},{3,5},{4,6},{5,7},{6,0},{7,1},{8,10},{9,11},{10,... | collective-permute-start | bytes 491528 | tf_op jit(solution)/shard_map/ppermute | solution.py:288
  69.4 29.8 %collective-permute-start.4 = (bf16[80,1024]{1,0:T(8,128)(2,1)S(1)}, bf16[80,1024]{1,0:T(8,128)(2,1)S(1)}, u32[]{:S(2)}, u32[]{:S(2)}) collective-permute-start(bf16[80,1024]{1,0:T(8,128)(2,1)S(1)} %copy-done.13), channel_id=1, source_target_pairs={{0,4},{1,5},{2,6},{3,7},{4,0},{5,1},{6,2},{7,3},{8,12},{9,13},{10,... | collective-permute-start | bytes 491528 | tf_op jit(solution)/shard_map/ppermute | solution.py:288
  84.5 14.7 %collective-permute-start.5 = (bf16[80,1024]{1,0:T(8,128)(2,1)S(1)}, bf16[80,1024]{1,0:T(8,128)(2,1)S(1)}, u32[]{:S(2)}, u32[]{:S(2)}) collective-permute-start(bf16[80,1024]{1,0:T(8,128)(2,1)S(1)} %copy-done.12), channel_id=1, source_target_pairs={{0,6},{1,7},{2,0},{3,1},{4,2},{5,3},{6,4},{7,5},{8,14},{9,15},{10,... | collective-permute-start | bytes 491528 | tf_op jit(solution)/shard_map/ppermute | solution.py:288
  91.8 7.5 %collective-permute-start.6 = (bf16[80,1024]{1,0:T(8,128)(2,1)S(1)}, bf16[80,1024]{1,0:T(8,128)(2,1)S(1)}, u32[]{:S(2)}, u32[]{:S(2)}) collective-permute-start(bf16[80,1024]{1,0:T(8,128)(2,1)S(1)} %copy-done.11), channel_id=1, source_target_pairs={{0,8},{1,9},{2,10},{3,11},{4,12},{5,13},{6,14},{7,15},{8,16},{9,17... | collective-permute-start | bytes 491528 | tf_op jit(solution)/shard_map/ppermute | solution.py:288
  94.0 10.8 %collective-permute-start.7 = (bf16[80,1024]{1,0:T(8,128)(2,1)S(1)}, bf16[80,1024]{1,0:T(8,128)(2,1)S(1)}, u32[]{:S(2)}, u32[]{:S(2)}) collective-permute-start(bf16[80,1024]{1,0:T(8,128)(2,1)S(1)} %copy-done.10), channel_id=1, source_target_pairs={{0,10},{1,11},{2,12},{3,13},{4,14},{5,15},{6,8},{7,9},{8,18},{9,19... | collective-permute-start | bytes 491528 | tf_op jit(solution)/shard_map/ppermute | solution.py:288
  94.0 14.6 %collective-permute-start.8 = (bf16[80,1024]{1,0:T(8,128)(2,1)S(1)}, bf16[80,1024]{1,0:T(8,128)(2,1)S(1)}, u32[]{:S(2)}, u32[]{:S(2)}) collective-permute-start(bf16[80,1024]{1,0:T(8,128)(2,1)S(1)} %copy-done.9), channel_id=1, source_target_pairs={{0,12},{1,13},{2,14},{3,15},{4,8},{5,9},{6,10},{7,11},{8,20},{9,21... | collective-permute-start | bytes 491528 | tf_op jit(solution)/shard_map/ppermute | solution.py:288
  99.2 10.4 %collective-permute-start.9 = (bf16[80,1024]{1,0:T(8,128)(2,1)S(1)}, bf16[80,1024]{1,0:T(8,128)(2,1)S(1)}, u32[]{:S(2)}, u32[]{:S(2)}) collective-permute-start(bf16[80,1024]{1,0:T(8,128)(2,1)S(1)} %copy-done.8), channel_id=1, source_target_pairs={{0,14},{1,15},{2,8},{3,9},{4,10},{5,11},{6,12},{7,13},{8,22},{9,23... | collective-permute-start | bytes 491528 | tf_op jit(solution)/shard_map/ppermute | solution.py:288
  124.9 22.2 %all-to-all-start.2 = ((bf16[16,40,1024]{2,1,0:T(8,128)(2,1)}), bf16[16,40,1024]{2,1,0:T(8,128)(2,1)S(1)}, u32[]{:S(2)}, u32[]{:S(2)}) async-start(bf16[16,40,1024]{2,1,0:T(8,128)(2,1)} %shard_map.126), calls=%async_computation.2 | async-start | bytes 2621440 | tf_op jit(solution)/shard_map/all_to_all | solution.py:296
  132.1 29.2 %collective-permute-start.2 = (f32[1,128,2048]{2,1,0:T(8,128)}, f32[1,128,2048]{2,1,0:T(8,128)S(1)}, u32[]{:S(2)}, u32[]{:S(2)}) collective-permute-start(f32[1,128,2048]{2,1,0:T(8,128)} %bitcast.47), channel_id=1, source_target_pairs={{0,32},{32,64},{64,96},{1,33},{33,65},{65,97},{2,34},{34,66},{66,9... | collective-permute-start | bytes 3145736 | tf_op jit(solution)/shard_map/ppermute | solution.py:277
  149.3 11.9 %collective-permute-start.18 = (bf16[1,128,2048]{2,1,0:T(8,128)(2,1)S(1)}, bf16[1,128,2048]{2,1,0:T(8,128)(2,1)S(1)}, u32[]{:S(2)}, u32[]{:S(2)}) collective-permute-start(bf16[1,128,2048]{2,1,0:T(8,128)(2,1)S(1)} %bitcast.32), channel_id=1, source_target_pairs={{32,0},{64,32},{96,64},{33,1},{65,33},{97,65},{34,2},{66,34},{98,6... | collective-permute-start | bytes 1572872 | tf_op jit(solution)/shard_map/ppermute | solution.py:277
  (6 other events, 36.4 us)

commit v2 on v1

--- a/solution.py
+++ b/solution.py
@@ -14,6 +14,7 @@
 SPLIT = 2
 GROUP = 4
 BLOCK = 512
+AHEAD = 12
 
 
 def dot(a, b, dims=((1,), (0,))):
@@ -66,9 +67,10 @@
 
 
 def pack_bwd_body(place_ref, x_ref, g_ref, gate_ref, mod_ref, route_ref, *outs, experts, cap, side):
-    blocks, norm_ref, inv_ref, where_ref = outs[:experts], *outs[experts:]
+    blocks, (norm_far, inv_ref, where_ref, norm_ref, right_ref, out_ref, sems) = outs[:experts], outs[experts:]
     normed, inv = layer_norm(x_ref[...])
     norm_ref[...] = normed
+    copies = sends([(norm_ref, norm_far)], sems, 0)
     inv_ref[...] = inv
     hidden = (normed * (1.0 + mod_ref[1]) + mod_ref[0]).astype(bf16)
     tokens, width = hidden.shape
@@ -79,24 +81,28 @@
     back = [(routes[k : k + 1, :] * (SPLIT * cap) + slots[k]).astype(f32) for k in range(2)]
     columns = jnp.transpose(jnp.concatenate([gate_ref[...], *back] * 2, 0))
     where_ref[...] = columns.astype(jnp.int32)
-    pair = [(columns[:, k : k + 1] * scaled).astype(bf16) for k in range(2)]
     shift = side.bit_length() - 1
     z, y = place_ref[0] >> shift, place_ref[0] & (side - 1)
     ahead = (((routes >> shift) - z) & (side - 1)) * side + ((routes - y) & (side - 1))
     first = [ahead[k : k + 1, :] * (2 * SPLIT * cap) + slots[k] for k in range(2)]
-    numbers = iota((experts * 2 * SPLIT * cap, tokens), 0)
-    left, right = [], []
-    for h in range(SPLIT):
-        hit = (numbers == first[0] + h * cap) | (numbers == first[1] + h * cap)
-        left.append(ones_where(hit).astype(bf16))
-        right.append(hidden[:, h * part : (h + 1) * part])
-        for k in range(2):
-            left.append(ones_where(numbers == first[k] + (SPLIT + h) * cap).astype(bf16))
-            right.append(pair[k][:, h * part : (h + 1) * part])
-    rows = dot(jnp.concatenate(left, 1), jnp.concatenate(right, 0)).astype(bf16)
+    for n, value in enumerate((hidden, *((columns[:, k : k + 1] * scaled).astype(bf16) for k in range(2)))):
+        for h in range(SPLIT):
+            at = (3 * h + n) * tokens
+            right_ref[at : at + tokens, :] = value[:, h * part : (h + 1) * part]
     size = 2 * SPLIT * cap
-    for n, block in enumerate(blocks):
-        block[...] = rows[n * size : (n + 1) * size, :]
+    for n in range(0, experts, GROUP):
+        numbers = iota((GROUP * size, tokens), 0) + n * size
+        left = []
+        for h in range(SPLIT):
+            hit = (numbers == first[0] + h * cap) | (numbers == first[1] + h * cap)
+            left.append(ones_where(hit).astype(bf16))
+            for k in range(2):
+                left.append(ones_where(numbers == first[k] + (SPLIT + h) * cap).astype(bf16))
+        out_ref[n * size : (n + GROUP) * size, :] = dot(jnp.concatenate(left, 1), right_ref[...]).astype(bf16)
+        pieces = [(out_ref.at[m * size : (m + 1) * size, :], blocks[m]) for m in range(n, n + GROUP)]
+        copies += sends(pieces, sems, len(copies))
+    for copy in copies:
+        copy.wait()
 
 
 def regroup_matrix(kinds, cap, forward):
@@ -125,47 +131,66 @@
                 target[n * slab : (n + 1) * slab, h * part : (h + 1) * part] = rows[kind * slab : (kind + 1) * slab, :]
 
 
-def repack(sum_ref, cap):
+def repack(halves, cap):
     matrix = regroup_matrix(SPLIT, cap, False)
-    slab, part = GROUP * cap, sum_ref.shape[1] // SPLIT
-    for n in range(sum_ref.shape[0] // slab):
-        rows = [sum_ref[n * slab : (n + 1) * slab, h * part : (h + 1) * part] for h in range(SPLIT)]
-        yield n, dot(matrix, jnp.concatenate(rows, 0)).astype(bf16)
-
-
-def fetches(pieces, sems):
+    slab = GROUP * cap
+    for n in range(halves[0].shape[0] // slab):
+        yield n, dot(matrix, jnp.concatenate([v[n * slab : (n + 1) * slab, :] for v in halves], 0)).astype(bf16)
+
+
+def fetches(pieces, sems, ahead):
     copies = [pltpu.make_async_copy(source, target, sems.at[n]) for n, (source, target) in enumerate(pieces)]
+    for copy in copies[:ahead]:
+        copy.start()
+    for n, copy in enumerate(copies):
+        copy.wait()
+        for later in copies[n + ahead : n + ahead + 1]:
+            later.start()
+        yield
+
+
+def sends(pieces, sems, first):
+    copies = [pltpu.make_async_copy(s, t, sems.at[first + n]) for n, (s, t) in enumerate(pieces)]
     for copy in copies:
         copy.start()
-    return iter(copies)
+    return copies
 
 
 def expert_fwd_body(x_ref, *refs, cap):
-    weights, (out_ref, rows_ref, act_ref, sum_ref), buffers, sems = refs[:4], refs[4:8], refs[8:12], refs[12]
+    weights, (out_far, rows_ref, act_ref, out_ref), buffers, sems = refs[:4], refs[4:8], refs[8:12], refs[12]
     size = GROUP * SPLIT * cap
     ff, width = weights[1].shape
+    part = width // SPLIT
+    columns = [h * part + j for j in range(0, part, BLOCK) for h in range(SPLIT)]
     pieces = []
     for n in (0, 2):
         for j in range(0, ff, BLOCK):
             pieces.append((weights[n].at[:, j : j + BLOCK], buffers[n].at[:, j : j + BLOCK]))
-    for j in range(0, width, BLOCK):
+    for j in columns:
         for n in (1, 3):
             pieces.append((weights[n].at[:, j : j + BLOCK], buffers[n].at[:, j : j + BLOCK]))
-    copies = fetches(pieces, sems)
+    ready = fetches(pieces, sems, AHEAD)
     unpack([x_ref[n : n + size, :] for n in range(0, x_ref.shape[0], size)], [rows_ref], cap)
     for n, up in enumerate((buffers[0], buffers[2])):
         for j in range(0, ff, BLOCK):
-            next(copies).wait()
+            next(ready)
             act = jax.nn.gelu(dot(rows_ref[...], up[:, j : j + BLOCK]))
             act_ref[:, n * ff + j : n * ff + j + BLOCK] = act.astype(bf16)
-    for j in range(0, width, BLOCK):
+    halves, copies = [], []
+    for j in columns:
         cols = slice(j, j + BLOCK)
-        next(copies).wait()
-        next(copies).wait()
+        next(ready)
+        next(ready)
         both = dot(act_ref[:, :ff], buffers[1][:, cols]) + dot(act_ref[:, ff:], buffers[3][:, cols])
-        sum_ref[:, cols] = both.astype(bf16)
-    for n, rows in repack(sum_ref, cap):
-        out_ref[n * size : (n + 1) * size, :] = rows
+        halves.append(both.astype(bf16))
+        if len(halves) == SPLIT:
+            cols = slice(j % part, j % part + BLOCK)
+            for n, rows in repack(halves, cap):
+                out_ref[n * size : (n + 1) * size, cols] = rows
+            copies += sends([(out_ref.at[:, cols], out_far.at[:, cols])], sems, len(pieces) + len(copies))
+            halves = []
+    for copy in copies:
+        copy.wait()
 
 
 def gelu_slope(x):
@@ -178,37 +203,49 @@
 def expert_bwd_body(place_ref, *refs, cap, side):
     experts = side * side
     blocks, weights, refs = refs[:experts], refs[experts : experts + 4], refs[experts + 4 :]
-    (out_ref, rows_ref, grads_ref, pre_ref, sum_ref), buffers, sems = refs[:5], refs[5:9], refs[9]
+    (out_far, rows_ref, grads_ref, pre_ref, out_ref), buffers, sems = refs[:5], refs[5:9], refs[9]
     ff, width = weights[1].shape
+    part = width // SPLIT
     transposed = ((1,), (1,))
     pieces = []
     for n in (0, 2):
         for j in range(0, ff, BLOCK):
             pieces.append((weights[n].at[:, j : j + BLOCK], buffers[n].at[:, j : j + BLOCK]))
             pieces.append((weights[n + 1].at[j : j + BLOCK, :], buffers[n + 1].at[j : j + BLOCK, :]))
-    copies = fetches(pieces, sems)
+    ready = fetches(pieces, sems, AHEAD)
     slabs = [jnp.concatenate([b[...] for b in blocks[n : n + GROUP]], 0) for n in range(0, experts, GROUP)]
     unpack(slabs, [rows_ref, grads_ref], cap)
     up_a, up_b = buffers[0], buffers[2]
     for n in range(2):
         up, down = buffers[2 * n], buffers[2 * n + 1]
         for j in range(0, ff, BLOCK):
-            next(copies).wait()
-            next(copies).wait()
+            next(ready)
+            next(ready)
             slope = gelu_slope(dot(rows_ref[...], up[:, j : j + BLOCK]))
             act_grad = dot(grads_ref[...], down[j : j + BLOCK, :], transposed)
             pre_ref[:, n * ff + j : n * ff + j + BLOCK] = (act_grad * slope).astype(bf16)
-    for j in range(0, width, BLOCK):
-        cols = slice(j, j + BLOCK)
-        both = dot(pre_ref[:, :ff], up_a[cols, :], transposed) + dot(pre_ref[:, ff:], up_b[cols, :], transposed)
-        sum_ref[:, cols] = both.astype(bf16)
     size = SPLIT * cap
     own_z, own_y = place_ref[0] >> (side.bit_length() - 1), place_ref[0] & (side - 1)
-    for n, rows in repack(sum_ref, cap):
-        for i in range(GROUP):
-            behind = n * GROUP + i
-            z, y = (own_z - behind // side) & (side - 1), (own_y - behind % side) & (side - 1)
-            out_ref[z * side + y] = rows[i * size : (i + 1) * size, :]
+    copies = []
+    for j in range(0, part, BLOCK):
+        halves = []
+        for h in range(SPLIT):
+            cols = slice(h * part + j, h * part + j + BLOCK)
+            both = dot(pre_ref[:, :ff], up_a[cols, :], transposed) + dot(pre_ref[:, ff:], up_b[cols, :], transposed)
+            halves.append(both.astype(bf16))
+        cols = slice(j, j + BLOCK)
+        for n, rows in repack(halves, cap):
+            for i in range(GROUP):
+                behind = n * GROUP + i
+                z, y = (own_z - behind // side) & (side - 1), (own_y - behind % side) & (side - 1)
+                out_ref[z * side + y, :, cols] = rows[i * size : (i + 1) * size, :]
+        copies += sends([(out_ref.at[:, :, cols], out_far.at[:, :, cols])], sems, len(pieces) + len(copies))
+    for copy in copies:
+        copy.wait()
+
+
+def settle_body(x_ref, out_ref):
+    out_ref[...] = x_ref[...]
 
 
 def combine_fwd_body(r_ref, gate_ref, route_ref, x_ref, mod_ref, out_ref, *, experts, cap):
@@ -226,7 +263,7 @@
 
 
 def combine_bwd_body(r_ref, where_ref, norm_far, inv_ref, g_far, mod_ref, out_ref, norm_ref, g_ref, sems, *, cap):
-    copies = fetches([(norm_far, norm_ref), (g_far, g_ref)], sems)
+    ready = fetches([(norm_far, norm_ref), (g_far, g_ref)], sems, 2)
     tokens = norm_ref.shape[0]
     numbers = iota((tokens, r_ref.shape[0]), 1)
     places = where_ref[...]
@@ -236,10 +273,10 @@
         halves.append(dot(ones_where(hit).astype(bf16), r_ref[...]))
     dnorm = jnp.concatenate(halves, 1) * (1.0 + mod_ref[1])
     mean_one = jnp.mean(dnorm, axis=-1, keepdims=True)
-    next(copies).wait()
+    next(ready)
     normed = norm_ref[...]
     mean_two = jnp.mean(dnorm * normed, axis=-1, keepdims=True)
-    next(copies).wait()
+    next(ready)
     grad = g_ref[...].astype(f32) + (dnorm - mean_one - normed * mean_two) * inv_ref[...]
     out_ref[...] = grad.astype(bf16)
 
@@ -252,11 +289,11 @@
     return [pltpu.with_memory_space_constraint(a, pltpu.VMEM) for a in arrays]
 
 
-def call(body, outs, args, flops, limit, scratch=(), scalars=0, far=(), **statics):
-    return kernel(body, outs, args, flops, limit, scratch, scalars, far, **statics)
-
-
-def kernel(body, outs, args, flops, limit, scratch, scalars, far, **statics):
+def call(body, outs, args, flops, limit, scratch=(), scalars=0, far=(), far_outs=(), **statics):
+    return kernel(body, outs, args, flops, limit, scratch, scalars, far, far_outs, **statics)
+
+
+def kernel(body, outs, args, flops, limit, scratch, scalars, far, far_outs, **statics):
     moved = sum(2 * a.size for a in args)
     specs = [pl.BlockSpec(memory_space=pltpu.SMEM) if n < scalars else pl.BlockSpec() for n in range(len(args))]
     for n in far:
@@ -265,6 +302,7 @@
         functools.partial(body, **statics),
         out_shape=outs,
         in_specs=specs,
+        out_specs=[pl.BlockSpec(memory_space=pltpu.HBM) if n in far_outs else pl.BlockSpec() for n in range(len(outs))],
         scratch_shapes=scratch,
         cost_estimate=pl.CostEstimate(flops=flops, bytes_accessed=moved, transcendentals=0),
         compiler_params=pltpu.CompilerParams(vmem_limit_bytes=limit << 20),
@@ -333,8 +371,8 @@
 
     (send,) = call(
         pack_fwd_body,
-        [shape((SPLIT * slots, half), bf16)],
-        (inputs, mod, routes),
+        [pltpu.HBM((SPLIT * slots, half), bf16)],
+        (*in_hbm(inputs), mod, routes),
         4 * tokens * slots * width,
         60,
         **sizes,
@@ -348,7 +386,14 @@
         (place, stored, grads, gates_b, mod_b, routes_b),
         12 * tokens * slots * width,
         28,
+        scratch=[
+            pltpu.VMEM((tokens, width), f32),
+            pltpu.VMEM((3 * SPLIT * tokens, half), bf16),
+            pltpu.VMEM((2 * SPLIT * slots, half), bf16),
+            pltpu.SemaphoreType.DMA((experts + 1,)),
+        ],
         scalars=1,
+        far_outs=range(experts + 1),
         side=side,
         **sizes,
     )
@@ -356,15 +401,16 @@
 
     rows_buffer = pltpu.VMEM((slots, width), bf16)
     hidden_buffer = pltpu.VMEM((slots, 2 * ff), bf16)
-    weight_buffers = [pltpu.VMEM(w.shape, bf16) for w in weights] + [pltpu.SemaphoreType.DMA((16,))]
+    weight_buffers = [pltpu.VMEM(w.shape, bf16) for w in weights] + [pltpu.SemaphoreType.DMA((20,))]
     (result,) = call(
         expert_fwd_body,
         [pltpu.HBM((SPLIT * slots, half), bf16)],
         (*in_vmem(got), *weights),
         8 * slots * width * ff,
         30,
-        scratch=[rows_buffer, hidden_buffer, rows_buffer] + weight_buffers,
+        scratch=[rows_buffer, hidden_buffer, pltpu.VMEM((SPLIT * slots, half), bf16)] + weight_buffers,
         far=(1, 2, 3, 4),
+        far_outs=(0,),
         cap=cap,
     )
     back = exchange(result, experts)
@@ -374,8 +420,10 @@
         (place, *got_b, *weights),
         12 * slots * width * ff,
         36,
-        scratch=[rows_buffer, rows_buffer, hidden_buffer, rows_buffer] + weight_buffers,
+        scratch=[rows_buffer, rows_buffer, hidden_buffer, pltpu.VMEM((experts, SPLIT * cap, half), bf16)]
+        + weight_buffers,
         far=range(experts + 1, experts + 5),
+        far_outs=(0,),
         scalars=1,
         cap=cap,
         side=side,
@@ -402,6 +450,8 @@
         cap=cap,
     )
     input_grads = shifted(section_grad[None], "section", -1)
+    (next_inputs,) = call(settle_body, [shape((tokens, width), f32)], (next_inputs[0],), 1000, 8)
+    next_inputs = next_inputs[None]
     return (next_inputs, input_grads)
 
 

time: 164 us -> 163 us (level)
    pallas_call x6 -> x7, Pallas kernels: 39 us -> 39.4 us  [kernel(): pl.pallas_call(functools.partial(body, **statics), out_shape=outs, in_spe...]
where the time goes in v2:
time: 163 us
  starting transfers between devices  63.5 us (39%)
  waiting for transfers between devices  58 us (36%)
  Pallas kernels  39.4 us (24%)
    pallas_call x7, Pallas kernels, kernel(): pl.pallas_call(functools.partial(body, **statics), out_shape=outs, in_spe...  39.4 us
    ppermute x15, starting transfers between devices, offset_by(): return lax.ppermute(block, 'expert', pairs)  32.9 us
    ppermute x15, waiting for transfers between devices, offset_by(): return lax.ppermute(block, 'expert', pairs)  30.7 us
    all_to_all x3, starting transfers between devices, exchange(): lax.all_to_all(parts, 'expert', 0, 0, axis_index_groups=groups, tiled=True)  25.2 us
    all_to_all x3, waiting for transfers between devices, exchange(): lax.all_to_all(parts, 'expert', 0, 0, axis_index_groups=groups, tiled=True)  17 us
    ppermute x2, waiting for transfers between devices, shifted(): lax.ppermute(value, axis, [(source, source + steps) for source in range(l...  10.3 us
    ppermute x2, starting transfers between devices, shifted(): lax.ppermute(value, axis, [(source, source + steps) for source in range(l...  4.76 us
  transfers between devices with their start and end apart: 22, of which 9 were waited for; matrix products, arithmetic and copies ran while one was open for 0% of the time, Pallas kernels for 24%

profile of v2, /device:TPU:0, one launch (start us, length us, event | category | flops | bytes accessed | tf_op | source)
XLA Modules:
  0.0 162.7 jit_solution(14788404253331395965)
XLA Ops:
  1.2 3.1 %shard_map.122 = bf16[640,1024]{1,0:T(8,128)(2,1)} custom-call(f32[128,2048]{1,0:T(8,128)} %bitcast.47, f32[3,1,2048]{2,1,0:T(1,128)} %bitcast.36, s32[2,128]{1,0:T(2,128)} %bitcast.40), custom_call_target="tpu_custom_call" | custom-call | flops 335544320 | bytes 537088 | tf_op jit(solution)/shard_map/pallas_call | solution.py:301
  4.4 8.3 %all-to-all-start = ((bf16[16,40,1024]{2,1,0:T(8,128)(2,1)}), bf16[16,40,1024]{2,1,0:T(8,128)(2,1)S(1)}, u32[]{:S(2)}, u32[]{:S(2)}) async-start(bf16[16,40,1024]{2,1,0:T(8,128)(2,1)} %bitcast.46), calls=%async_computation | async-start | bytes 2621440 | tf_op jit(solution)/shard_map/all_to_all | solution.py:334
  12.8 3.6 %shard_map.126 = (bf16[80,1024]{1,0:T(8,128)(2,1)}, bf16[80,1024]{1,0:T(8,128)(2,1)}, bf16[80,1024]{1,0:T(8,128)(2,1)}, bf16[80,1024]{1,0:T(8,128)(2,1)}, bf16[8...) custom-call(s32[1]{0:T(128)} %bitcast.15.place_ref, ...), custom_call_target="tpu_custom_call" | custom-call | flops 1006632960 | bytes 1061890 | tf_op jit(solution)/shard_map/pallas_call | solution.py:301
  16.4 3.5 %collective-permute-start.10 = (bf16[80,1024]{1,0:T(8,128)(2,1)}, bf16[80,1024]{1,0:T(8,128)(2,1)S(1)}, u32[]{:S(2)}, u32[]{:S(2)}) collective-permute-start(bf16[80,1024]{1,0:T(8,128)(2,1)} %get-tuple-element.29), channel_id=1, source_target_pairs={{0,16},{1,17},{2,18},{3,19},{4,20},{5,21},{6,22},{7,23},{8,24},{9,... | collective-permute-start | bytes 491528 | tf_op jit(solution)/shard_map/ppermute | solution.py:326
  19.9 1.5 collective-permute-start.11
  21.4 5.1 %collective-permute-start.12 = (bf16[80,1024]{1,0:T(8,128)(2,1)}, bf16[80,1024]{1,0:T(8,128)(2,1)S(1)}, u32[]{:S(2)}, u32[]{:S(2)}) collective-permute-start(bf16[80,1024]{1,0:T(8,128)(2,1)} %get-tuple-element.31), channel_id=1, source_target_pairs={{0,20},{1,21},{2,22},{3,23},{4,16},{5,17},{6,18},{7,19},{8,28},{9,... | collective-permute-start | bytes 491528 | tf_op jit(solution)/shard_map/ppermute | solution.py:326
  26.5 1.5 collective-permute-start.13
  27.9 2.7 %collective-permute-start.14 = (bf16[80,1024]{1,0:T(8,128)(2,1)}, bf16[80,1024]{1,0:T(8,128)(2,1)}, u32[]{:S(2)}, u32[]{:S(2)}) collective-permute-start(bf16[80,1024]{1,0:T(8,128)(2,1)} %get-tuple-element.33), channel_id=1, source_target_pairs={{0,24},{1,25},{2,26},{3,27},{4,28},{5,29},{6,30},{7,31},{8,0},{9,1... | collective-permute-start | bytes 491528 | tf_op jit(solution)/shard_map/ppermute | solution.py:326
  30.6 5.8 %all-to-all-done = bf16[16,40,1024]{2,1,0:T(8,128)(2,1)S(1)} async-done(((bf16[16,40,1024]{2,1,0:T(8,128)(2,1)}), bf16[16,40,1024]{2,1,0:T(8,128)(2,1)S(1)}, u32[]{:S(2)}, u32[]{:S(2)}) %all-to-all-start) | async-done | bytes 1310752 | tf_op jit(solution)/shard_map/all_to_all | solution.py:334
  36.4 10.7 %shard_map.123 = bf16[640,1024]{1,0:T(8,128)(2,1)} custom-call(bf16[640,1024]{1,0:T(8,128)(2,1)S(1)} %bitcast.31, bf16[2048,1024]{1,0:T(8,128)(2,1)} %bitcast.53, bf16[1024,2048]{1,0:T(8,128)(2,1)} %bitcast.56, bf16[2048,1024]{1,0:T(8,128)(2,1)} %collective-permute-done.refs_2_.refs_18_, bf16[1024,2048]{1,0:T(8,128)(2,1)} %collective-permute-done.1.refs_3_.refs_19_), custom_call_target="tpu_custom_call" | custom-call | flops 5368709120 | bytes 18087936 | tf_op jit(solution)/shard_map/pallas_call | solution.py:301
  47.2 12.9 %all-to-all-start.1 = ((bf16[16,40,1024]{2,1,0:T(8,128)(2,1)}), bf16[16,40,1024]{2,1,0:T(8,128)(2,1)S(1)}, u32[]{:S(2)}, u32[]{:S(2)}) async-start(bf16[16,40,1024]{2,1,0:T(8,128)(2,1)} %bitcast.49), calls=%async_computation.1 | async-start | bytes 2621440 | tf_op jit(solution)/shard_map/all_to_all | solution.py:334
  60.1 4.1 %collective-permute-start.15 = (bf16[80,1024]{1,0:T(8,128)(2,1)}, bf16[80,1024]{1,0:T(8,128)(2,1)S(1)}, u32[]{:S(2)}, u32[]{:S(2)}) collective-permute-start(bf16[80,1024]{1,0:T(8,128)(2,1)} %get-tuple-element.34), channel_id=1, source_target_pairs={{0,26},{1,27},{2,28},{3,29},{4,30},{5,31},{6,24},{7,25},{8,2},{9,3... | collective-permute-start | bytes 491528 | tf_op jit(solution)/shard_map/ppermute | solution.py:326
  64.2 3.0 %collective-permute-start.16 = (bf16[80,1024]{1,0:T(8,128)(2,1)}, bf16[80,1024]{1,0:T(8,128)(2,1)S(1)}, u32[]{:S(2)}, u32[]{:S(2)}) collective-permute-start(bf16[80,1024]{1,0:T(8,128)(2,1)} %get-tuple-element.35), channel_id=1, source_target_pairs={{0,28},{1,29},{2,30},{3,31},{4,24},{5,25},{6,26},{7,27},{8,4},{9,5... | collective-permute-start | bytes 491528 | tf_op jit(solution)/shard_map/ppermute | solution.py:326
  67.2 1.5 collective-permute-start.17
  69.2 1.0 collective-permute-start.4
  70.2 14.3 %collective-permute-done.15.refs_13_ = bf16[80,1024]{1,0:T(8,128)(2,1)S(1)} collective-permute-done((bf16[80,1024]{1,0:T(8,128)(2,1)}, bf16[80,1024]{1,0:T(8,128)(2,1)S(1)}, u32[]{:S(2)}, u32[]{:S(2)}) %collective-permute-start.15) | collective-permute-done | bytes 163872 | tf_op jit(solution)/shard_map/ppermute | solution.py:326
  84.5 5.6 %collective-permute-start.5 = (bf16[80,1024]{1,0:T(8,128)(2,1)S(1)}, bf16[80,1024]{1,0:T(8,128)(2,1)S(1)}, u32[]{:S(2)}, u32[]{:S(2)}) collective-permute-start(bf16[80,1024]{1,0:T(8,128)(2,1)S(1)} %copy-done.12), channel_id=1, source_target_pairs={{0,6},{1,7},{2,0},{3,1},{4,2},{5,3},{6,4},{7,5},{8,14},{9,15},{10,... | collective-permute-start | bytes 491528 | tf_op jit(solution)/shard_map/ppermute | solution.py:326
  90.1 1.6 %collective-permute-done.16.refs_14_ = bf16[80,1024]{1,0:T(8,128)(2,1)S(1)} collective-permute-done((bf16[80,1024]{1,0:T(8,128)(2,1)}, bf16[80,1024]{1,0:T(8,128)(2,1)S(1)}, u32[]{:S(2)}, u32[]{:S(2)}) %collective-permute-start.16) | collective-permute-done | bytes 163872 | tf_op jit(solution)/shard_map/ppermute | solution.py:326
  91.8 2.2 %collective-permute-start.6 = (bf16[80,1024]{1,0:T(8,128)(2,1)S(1)}, bf16[80,1024]{1,0:T(8,128)(2,1)S(1)}, u32[]{:S(2)}, u32[]{:S(2)}) collective-permute-start(bf16[80,1024]{1,0:T(8,128)(2,1)S(1)} %copy-done.11), channel_id=1, source_target_pairs={{0,8},{1,9},{2,10},{3,11},{4,12},{5,13},{6,14},{7,15},{8,16},{9,17... | collective-permute-start | bytes 491528 | tf_op jit(solution)/shard_map/ppermute | solution.py:326
  94.8 4.3 %collective-permute-done.4.refs_2_ = bf16[80,1024]{1,0:T(8,128)(2,1)S(1)} collective-permute-done((bf16[80,1024]{1,0:T(8,128)(2,1)S(1)}, bf16[80,1024]{1,0:T(8,128)(2,1)S(1)}, u32[]{:S(2)}, u32[]{:S(2)}) %collective-permute-start.4) | collective-permute-done | bytes 163872 | tf_op jit(solution)/shard_map/ppermute | solution.py:326
  99.2 5.6 %collective-permute-done.7.refs_5_ = bf16[80,1024]{1,0:T(8,128)(2,1)S(1)} collective-permute-done((bf16[80,1024]{1,0:T(8,128)(2,1)S(1)}, bf16[80,1024]{1,0:T(8,128)(2,1)S(1)}, u32[]{:S(2)}, u32[]{:S(2)}) %collective-permute-start.7) | collective-permute-done | bytes 163872 | tf_op jit(solution)/shard_map/ppermute | solution.py:326
  104.8 3.8 %collective-permute-done.8.refs_6_ = bf16[80,1024]{1,0:T(8,128)(2,1)S(1)} collective-permute-done((bf16[80,1024]{1,0:T(8,128)(2,1)S(1)}, bf16[80,1024]{1,0:T(8,128)(2,1)S(1)}, u32[]{:S(2)}, u32[]{:S(2)}) %collective-permute-start.8) | collective-permute-done | bytes 163872 | tf_op jit(solution)/shard_map/ppermute | solution.py:326
  108.6 1.0 collective-permute-done.9.refs_7_
  109.6 15.2 %shard_map.127 = bf16[16,40,1024]{2,1,0:T(8,128)(2,1)} custom-call(s32[1]{0:T(128)} %bitcast.15.place_ref, bf16[80,1024]{1,0:T(8,128)(2,1)} %get-tuple-element.21.refs_0_, bf16[80,1024]{1,0:T(8,128)(2,1)S(1)} %collective-permute-done.3.refs_1_, bf16[80,1024]{1,0:T(8,128)(2,1)S(1)} %collective-permute-done.4.refs_2_, ...), custom_call_target="tpu_custom_call" | custom-call | flops 8053063680 | bytes 19398658 | tf_op jit(solution)/shard_map/pallas_call | solution.py:301
  124.8 3.9 %all-to-all-start.2 = ((bf16[16,40,1024]{2,1,0:T(8,128)(2,1)}), bf16[16,40,1024]{2,1,0:T(8,128)(2,1)S(1)}, u32[]{:S(2)}, u32[]{:S(2)}) async-start(bf16[16,40,1024]{2,1,0:T(8,128)(2,1)} %shard_map.127), calls=%async_computation.2 | async-start | bytes 2621440 | tf_op jit(solution)/shard_map/all_to_all | solution.py:334
  128.8 3.5 %shard_map.124 = f32[128,2048]{1,0:T(8,128)} custom-call(bf16[640,1024]{1,0:T(8,128)(2,1)S(1)} %bitcast.30, f32[2,128]{1,0:T(2,128)S(1)} %bitcast.42, s32[2,128]{1,0:T(2,128)S(1)} %bitcast.41, f32[128,2048]{1,0:T(8,128)} %bitcast.48, f32[3,1,2048]{2,1,0:T(1,128)S(1)} %bitcast.37), custom_call_target="tpu_custom_call" | custom-call | flops 671088640 | bytes 1848320 | tf_op jit(solution)/shard_map/pallas_call | solution.py:301
  132.3 3.5 %collective-permute-start.2 = (f32[1,128,2048]{2,1,0:T(8,128)}, f32[1,128,2048]{2,1,0:T(8,128)S(1)}, u32[]{:S(2)}, u32[]{:S(2)}) collective-permute-start(f32[1,128,2048]{2,1,0:T(8,128)} %bitcast.50), channel_id=1, source_target_pairs={{0,32},{32,64},{64,96},{1,33},{33,65},{65,97},{2,34},{34,66},{66,9... | collective-permute-start | bytes 3145736 | tf_op jit(solution)/shard_map/ppermute | solution.py:315
  135.8 11.2 %all-to-all-done.2 = bf16[16,40,1024]{2,1,0:T(8,128)(2,1)S(1)} async-done(((bf16[16,40,1024]{2,1,0:T(8,128)(2,1)}), bf16[16,40,1024]{2,1,0:T(8,128)(2,1)S(1)}, u32[]{:S(2)}, u32[]{:S(2)}) %all-to-all-start.2) | async-done | bytes 1310752 | tf_op jit(solution)/shard_map/all_to_all | solution.py:334
  147.0 2.2 %shard_map.128 = bf16[128,2048]{1,0:T(8,128)(2,1)S(1)} custom-call(bf16[640,1024]{1,0:T(8,128)(2,1)S(1)} %bitcast.29, s32[128,8]{1,0:T(8,128)S(1)} %get-tuple-element.37.where_ref, f32[128,2048]{1,0:T(8,128)} %get-tuple-element.38.norm_far, f32[128,1]{1,0:T(8,128)S(1)} %get-tuple-element.39.inv_ref, bf16[128,2048]{1,0:T(8,128)(2,1)} %bitcast.33, ...), custom_call_target="tpu_custom_call" | custom-call | flops 335544320 | bytes 2373888 | tf_op jit(solution)/shard_map/pallas_call | solution.py:301
  149.3 1.3 collective-permute-start.18
  150.6 10.3 %collective-permute-done.18 = bf16[1,128,2048]{2,1,0:T(8,128)(2,1)S(1)} collective-permute-done((bf16[1,128,2048]{2,1,0:T(8,128)(2,1)S(1)}, bf16[1,128,2048]{2,1,0:T(8,128)(2,1)S(1)}, u32[]{:S(2)}, u32[]{:S(2)}) %collective-permute-start.18) | collective-permute-done | bytes 524320 | tf_op jit(solution)/shard_map/ppermute | solution.py:315
  160.9 1.0 shard_map.125
  (52 shorter events, 2.9 us)
Async XLA Ops:
  0.6 25.8 %collective-permute-start = (bf16[2048,1024]{1,0:T(8,128)(2,1)}, bf16[2048,1024]{1,0:T(8,128)(2,1)}, u32[]{:S(2)}, u32[]{:S(2)}) collective-permute-start(bf16[2048,1024]{1,0:T(8,128)(2,1)} %bitcast.52), channel_id=1, source_target_pairs={{0,1},{1,0},{2,3},{3,2},{4,5},{5,4},{6,7},{7,6},{8,9},{9,8},{10,11... | collective-permute-start | bytes 12582920 | tf_op jit(solution)/shard_map/ppermute | solution.py:367
  0.7 27.2 %collective-permute-start.1 = (bf16[1024,2048]{1,0:T(8,128)(2,1)}, bf16[1024,2048]{1,0:T(8,128)(2,1)}, u32[]{:S(2)}, u32[]{:S(2)}) collective-permute-start(bf16[1024,2048]{1,0:T(8,128)(2,1)} %bitcast.55), channel_id=1, source_target_pairs={{0,1},{1,0},{2,3},{3,2},{4,5},{5,4},{6,7},{7,6},{8,9},{9,8},{10,11... | collective-permute-start | bytes 12582920 | tf_op jit(solution)/shard_map/ppermute | solution.py:367
  4.4 8.4 %copy-start.6 = (f32[1,128,2]{1,2,0:T(2,128)S(1)}, f32[1,128,2]{1,2,0:T(2,128)}, u32[]{:S(2)}) copy-start(f32[1,128,2]{1,2,0:T(2,128)} %param.18) | copy-start | bytes 3076
  4.4 8.4 %copy-start.7 = (s32[1,128,2]{1,2,0:T(2,128)S(1)}, s32[1,128,2]{1,2,0:T(2,128)}, u32[]{:S(2)}) copy-start(s32[1,128,2]{1,2,0:T(2,128)} %param.17) | copy-start | bytes 3076
  4.4 32.0 %all-to-all-start = ((bf16[16,40,1024]{2,1,0:T(8,128)(2,1)}), bf16[16,40,1024]{2,1,0:T(8,128)(2,1)S(1)}, u32[]{:S(2)}, u32[]{:S(2)}) async-start(bf16[16,40,1024]{2,1,0:T(8,128)(2,1)} %bitcast.46), calls=%async_computation | async-start | bytes 2621440 | tf_op jit(solution)/shard_map/all_to_all | solution.py:334
  16.4 43.7 %collective-permute-start.10 = (bf16[80,1024]{1,0:T(8,128)(2,1)}, bf16[80,1024]{1,0:T(8,128)(2,1)S(1)}, u32[]{:S(2)}, u32[]{:S(2)}) collective-permute-start(bf16[80,1024]{1,0:T(8,128)(2,1)} %get-tuple-element.29), channel_id=1, source_target_pairs={{0,16},{1,17},{2,18},{3,19},{4,20},{5,21},{6,22},{7,23},{8,24},{9,... | collective-permute-start | bytes 491528 | tf_op jit(solution)/shard_map/ppermute | solution.py:326
  19.9 44.3 %collective-permute-start.11 = (bf16[80,1024]{1,0:T(8,128)(2,1)}, bf16[80,1024]{1,0:T(8,128)(2,1)S(1)}, u32[]{:S(2)}, u32[]{:S(2)}) collective-permute-start(bf16[80,1024]{1,0:T(8,128)(2,1)} %get-tuple-element.30), channel_id=1, source_target_pairs={{0,18},{1,19},{2,20},{3,21},{4,22},{5,23},{6,16},{7,17},{8,26},{9,... | collective-permute-start | bytes 491528 | tf_op jit(solution)/shard_map/ppermute | solution.py:326
  21.4 45.8 %collective-permute-start.12 = (bf16[80,1024]{1,0:T(8,128)(2,1)}, bf16[80,1024]{1,0:T(8,128)(2,1)S(1)}, u32[]{:S(2)}, u32[]{:S(2)}) collective-permute-start(bf16[80,1024]{1,0:T(8,128)(2,1)} %get-tuple-element.31), channel_id=1, source_target_pairs={{0,20},{1,21},{2,22},{3,23},{4,16},{5,17},{6,18},{7,19},{8,28},{9,... | collective-permute-start | bytes 491528 | tf_op jit(solution)/shard_map/ppermute | solution.py:326
  26.5 42.2 %collective-permute-start.13 = (bf16[80,1024]{1,0:T(8,128)(2,1)}, bf16[80,1024]{1,0:T(8,128)(2,1)S(1)}, u32[]{:S(2)}, u32[]{:S(2)}) collective-permute-start(bf16[80,1024]{1,0:T(8,128)(2,1)} %get-tuple-element.32), channel_id=1, source_target_pairs={{0,22},{1,23},{2,16},{3,17},{4,18},{5,19},{6,20},{7,21},{8,30},{9,... | collective-permute-start | bytes 491528 | tf_op jit(solution)/shard_map/ppermute | solution.py:326
  27.9 41.3 %collective-permute-start.14 = (bf16[80,1024]{1,0:T(8,128)(2,1)}, bf16[80,1024]{1,0:T(8,128)(2,1)}, u32[]{:S(2)}, u32[]{:S(2)}) collective-permute-start(bf16[80,1024]{1,0:T(8,128)(2,1)} %get-tuple-element.33), channel_id=1, source_target_pairs={{0,24},{1,25},{2,26},{3,27},{4,28},{5,29},{6,30},{7,31},{8,0},{9,1... | collective-permute-start | bytes 491528 | tf_op jit(solution)/shard_map/ppermute | solution.py:326
  47.1 20.1 %copy-start.15 = (bf16[80,1024]{1,0:T(8,128)(2,1)S(1)}, bf16[80,1024]{1,0:T(8,128)(2,1)}, u32[]{:S(2)}) copy-start(bf16[80,1024]{1,0:T(8,128)(2,1)} %get-tuple-element.36) | copy-start | bytes 491524
  47.1 21.6 %copy-start.14 = (bf16[80,1024]{1,0:T(8,128)(2,1)S(1)}, bf16[80,1024]{1,0:T(8,128)(2,1)}, u32[]{:S(2)}) copy-start(bf16[80,1024]{1,0:T(8,128)(2,1)} %get-tuple-element.22) | copy-start | bytes 491524
  47.1 22.1 %copy-start.13 = (bf16[80,1024]{1,0:T(8,128)(2,1)S(1)}, bf16[80,1024]{1,0:T(8,128)(2,1)}, u32[]{:S(2)}) copy-start(bf16[80,1024]{1,0:T(8,128)(2,1)} %get-tuple-element.23) | copy-start | bytes 491524
  47.1 37.4 %copy-start.12 = (bf16[80,1024]{1,0:T(8,128)(2,1)S(1)}, bf16[80,1024]{1,0:T(8,128)(2,1)}, u32[]{:S(2)}) copy-start(bf16[80,1024]{1,0:T(8,128)(2,1)} %get-tuple-element.24) | copy-start | bytes 491524
  47.1 44.6 %copy-start.11 = (bf16[80,1024]{1,0:T(8,128)(2,1)S(1)}, bf16[80,1024]{1,0:T(8,128)(2,1)}, u32[]{:S(2)}) copy-start(bf16[80,1024]{1,0:T(8,128)(2,1)} %get-tuple-element.25) | copy-start | bytes 491524
  47.1 46.8 %copy-start.10 = (bf16[80,1024]{1,0:T(8,128)(2,1)S(1)}, bf16[80,1024]{1,0:T(8,128)(2,1)}, u32[]{:S(2)}) copy-start(bf16[80,1024]{1,0:T(8,128)(2,1)} %get-tuple-element.26) | copy-start | bytes 491524
  47.1 46.8 %copy-start.9 = (bf16[80,1024]{1,0:T(8,128)(2,1)S(1)}, bf16[80,1024]{1,0:T(8,128)(2,1)}, u32[]{:S(2)}) copy-start(bf16[80,1024]{1,0:T(8,128)(2,1)} %get-tuple-element.27) | copy-start | bytes 491524
  47.2 52.0 %copy-start.8 = (bf16[80,1024]{1,0:T(8,128)(2,1)S(1)}, bf16[80,1024]{1,0:T(8,128)(2,1)}, u32[]{:S(2)}) copy-start(bf16[80,1024]{1,0:T(8,128)(2,1)} %get-tuple-element.28) | copy-start | bytes 491524
  47.2 77.7 %all-to-all-start.1 = ((bf16[16,40,1024]{2,1,0:T(8,128)(2,1)}), bf16[16,40,1024]{2,1,0:T(8,128)(2,1)S(1)}, u32[]{:S(2)}, u32[]{:S(2)}) async-start(bf16[16,40,1024]{2,1,0:T(8,128)(2,1)} %bitcast.49), calls=%async_computation.1 | async-start | bytes 2621440 | tf_op jit(solution)/shard_map/all_to_all | solution.py:334
  60.1 24.4 %collective-permute-start.15 = (bf16[80,1024]{1,0:T(8,128)(2,1)}, bf16[80,1024]{1,0:T(8,128)(2,1)S(1)}, u32[]{:S(2)}, u32[]{:S(2)}) collective-permute-start(bf16[80,1024]{1,0:T(8,128)(2,1)} %get-tuple-element.34), channel_id=1, source_target_pairs={{0,26},{1,27},{2,28},{3,29},{4,30},{5,31},{6,24},{7,25},{8,2},{9,3... | collective-permute-start | bytes 491528 | tf_op jit(solution)/shard_map/ppermute | solution.py:326
  64.2 27.5 %collective-permute-start.16 = (bf16[80,1024]{1,0:T(8,128)(2,1)}, bf16[80,1024]{1,0:T(8,128)(2,1)S(1)}, u32[]{:S(2)}, u32[]{:S(2)}) collective-permute-start(bf16[80,1024]{1,0:T(8,128)(2,1)} %get-tuple-element.35), channel_id=1, source_target_pairs={{0,28},{1,29},{2,30},{3,31},{4,24},{5,25},{6,26},{7,27},{8,4},{9,5... | collective-permute-start | bytes 491528 | tf_op jit(solution)/shard_map/ppermute | solution.py:326
  67.2 26.7 %collective-permute-start.17 = (bf16[80,1024]{1,0:T(8,128)(2,1)S(1)}, bf16[80,1024]{1,0:T(8,128)(2,1)S(1)}, u32[]{:S(2)}, u32[]{:S(2)}) collective-permute-start(bf16[80,1024]{1,0:T(8,128)(2,1)S(1)} %copy-done.15), channel_id=1, source_target_pairs={{0,30},{1,31},{2,24},{3,25},{4,26},{5,27},{6,28},{7,29},{8,6},{9,7... | collective-permute-start | bytes 491528 | tf_op jit(solution)/shard_map/ppermute | solution.py:326
  68.7 25.3 %collective-permute-start.3 = (bf16[80,1024]{1,0:T(8,128)(2,1)S(1)}, bf16[80,1024]{1,0:T(8,128)(2,1)S(1)}, u32[]{:S(2)}, u32[]{:S(2)}) collective-permute-start(bf16[80,1024]{1,0:T(8,128)(2,1)S(1)} %copy-done.14), channel_id=1, source_target_pairs={{0,2},{1,3},{2,4},{3,5},{4,6},{5,7},{6,0},{7,1},{8,10},{9,11},{10,... | collective-permute-start | bytes 491528 | tf_op jit(solution)/shard_map/ppermute | solution.py:326
  69.2 29.9 %collective-permute-start.4 = (bf16[80,1024]{1,0:T(8,128)(2,1)S(1)}, bf16[80,1024]{1,0:T(8,128)(2,1)S(1)}, u32[]{:S(2)}, u32[]{:S(2)}) collective-permute-start(bf16[80,1024]{1,0:T(8,128)(2,1)S(1)} %copy-done.13), channel_id=1, source_target_pairs={{0,4},{1,5},{2,6},{3,7},{4,0},{5,1},{6,2},{7,3},{8,12},{9,13},{10,... | collective-permute-start | bytes 491528 | tf_op jit(solution)/shard_map/ppermute | solution.py:326
  84.5 14.7 %collective-permute-start.5 = (bf16[80,1024]{1,0:T(8,128)(2,1)S(1)}, bf16[80,1024]{1,0:T(8,128)(2,1)S(1)}, u32[]{:S(2)}, u32[]{:S(2)}) collective-permute-start(bf16[80,1024]{1,0:T(8,128)(2,1)S(1)} %copy-done.12), channel_id=1, source_target_pairs={{0,6},{1,7},{2,0},{3,1},{4,2},{5,3},{6,4},{7,5},{8,14},{9,15},{10,... | collective-permute-start | bytes 491528 | tf_op jit(solution)/shard_map/ppermute | solution.py:326
  91.8 7.4 %collective-permute-start.6 = (bf16[80,1024]{1,0:T(8,128)(2,1)S(1)}, bf16[80,1024]{1,0:T(8,128)(2,1)S(1)}, u32[]{:S(2)}, u32[]{:S(2)}) collective-permute-start(bf16[80,1024]{1,0:T(8,128)(2,1)S(1)} %copy-done.11), channel_id=1, source_target_pairs={{0,8},{1,9},{2,10},{3,11},{4,12},{5,13},{6,14},{7,15},{8,16},{9,17... | collective-permute-start | bytes 491528 | tf_op jit(solution)/shard_map/ppermute | solution.py:326
  93.9 10.9 %collective-permute-start.7 = (bf16[80,1024]{1,0:T(8,128)(2,1)S(1)}, bf16[80,1024]{1,0:T(8,128)(2,1)S(1)}, u32[]{:S(2)}, u32[]{:S(2)}) collective-permute-start(bf16[80,1024]{1,0:T(8,128)(2,1)S(1)} %copy-done.10), channel_id=1, source_target_pairs={{0,10},{1,11},{2,12},{3,13},{4,14},{5,15},{6,8},{7,9},{8,18},{9,19... | collective-permute-start | bytes 491528 | tf_op jit(solution)/shard_map/ppermute | solution.py:326
  94.0 14.6 %collective-permute-start.8 = (bf16[80,1024]{1,0:T(8,128)(2,1)S(1)}, bf16[80,1024]{1,0:T(8,128)(2,1)S(1)}, u32[]{:S(2)}, u32[]{:S(2)}) collective-permute-start(bf16[80,1024]{1,0:T(8,128)(2,1)S(1)} %copy-done.9), channel_id=1, source_target_pairs={{0,12},{1,13},{2,14},{3,15},{4,8},{5,9},{6,10},{7,11},{8,20},{9,21... | collective-permute-start | bytes 491528 | tf_op jit(solution)/shard_map/ppermute | solution.py:326
  99.2 10.4 %collective-permute-start.9 = (bf16[80,1024]{1,0:T(8,128)(2,1)S(1)}, bf16[80,1024]{1,0:T(8,128)(2,1)S(1)}, u32[]{:S(2)}, u32[]{:S(2)}) collective-permute-start(bf16[80,1024]{1,0:T(8,128)(2,1)S(1)} %copy-done.8), channel_id=1, source_target_pairs={{0,14},{1,15},{2,8},{3,9},{4,10},{5,11},{6,12},{7,13},{8,22},{9,23... | collective-permute-start | bytes 491528 | tf_op jit(solution)/shard_map/ppermute | solution.py:326
  124.8 22.2 %all-to-all-start.2 = ((bf16[16,40,1024]{2,1,0:T(8,128)(2,1)}), bf16[16,40,1024]{2,1,0:T(8,128)(2,1)S(1)}, u32[]{:S(2)}, u32[]{:S(2)}) async-start(bf16[16,40,1024]{2,1,0:T(8,128)(2,1)} %shard_map.127), calls=%async_computation.2 | async-start | bytes 2621440 | tf_op jit(solution)/shard_map/all_to_all | solution.py:334
  132.3 28.5 %collective-permute-start.2 = (f32[1,128,2048]{2,1,0:T(8,128)}, f32[1,128,2048]{2,1,0:T(8,128)S(1)}, u32[]{:S(2)}, u32[]{:S(2)}) collective-permute-start(f32[1,128,2048]{2,1,0:T(8,128)} %bitcast.50), channel_id=1, source_target_pairs={{0,32},{32,64},{64,96},{1,33},{33,65},{65,97},{2,34},{34,66},{66,9... | collective-permute-start | bytes 3145736 | tf_op jit(solution)/shard_map/ppermute | solution.py:315
  149.3 11.6 %collective-permute-start.18 = (bf16[1,128,2048]{2,1,0:T(8,128)(2,1)S(1)}, bf16[1,128,2048]{2,1,0:T(8,128)(2,1)S(1)}, u32[]{:S(2)}, u32[]{:S(2)}) collective-permute-start(bf16[1,128,2048]{2,1,0:T(8,128)(2,1)S(1)} %bitcast.35), channel_id=1, source_target_pairs={{32,0},{64,32},{96,64},{33,1},{65,33},{97,65},{34,2},{66,34},{98,6... | collective-permute-start | bytes 1572872 | tf_op jit(solution)/shard_map/ppermute | solution.py:315
  (6 other events, 37.0 us)

commit v3 on v2

--- a/solution.py
+++ b/solution.py
@@ -66,7 +66,7 @@
     out_ref[...] = dot(jnp.concatenate(left, 1), jnp.concatenate(right, 0)).astype(bf16)
 
 
-def pack_bwd_body(place_ref, x_ref, g_ref, gate_ref, mod_ref, route_ref, *outs, experts, cap, side):
+def pack_bwd_body(place_ref, x_ref, g_ref, gate_ref, mod_ref, route_ref, *outs, experts, cap):
     blocks, (norm_far, inv_ref, where_ref, norm_ref, right_ref, out_ref, sems) = outs[:experts], outs[experts:]
     normed, inv = layer_norm(x_ref[...])
     norm_ref[...] = normed
@@ -81,9 +81,7 @@
     back = [(routes[k : k + 1, :] * (SPLIT * cap) + slots[k]).astype(f32) for k in range(2)]
     columns = jnp.transpose(jnp.concatenate([gate_ref[...], *back] * 2, 0))
     where_ref[...] = columns.astype(jnp.int32)
-    shift = side.bit_length() - 1
-    z, y = place_ref[0] >> shift, place_ref[0] & (side - 1)
-    ahead = (((routes >> shift) - z) & (side - 1)) * side + ((routes - y) & (side - 1))
+    ahead = routes ^ place_ref[0]
     first = [ahead[k : k + 1, :] * (2 * SPLIT * cap) + slots[k] for k in range(2)]
     for n, value in enumerate((hidden, *((columns[:, k : k + 1] * scaled).astype(bf16) for k in range(2)))):
         for h in range(SPLIT):
@@ -200,8 +198,8 @@
     return 0.5 * (1.0 + t) + (0.5 * c) * x * (1.0 - t * t) * (1.0 + (3.0 * 0.044715) * square)
 
 
-def expert_bwd_body(place_ref, *refs, cap, side):
-    experts = side * side
+def expert_bwd_body(place_ref, *refs, cap):
+    experts = len(refs) - 14
     blocks, weights, refs = refs[:experts], refs[experts : experts + 4], refs[experts + 4 :]
     (out_far, rows_ref, grads_ref, pre_ref, out_ref), buffers, sems = refs[:5], refs[5:9], refs[9]
     ff, width = weights[1].shape
@@ -225,7 +223,6 @@
             act_grad = dot(grads_ref[...], down[j : j + BLOCK, :], transposed)
             pre_ref[:, n * ff + j : n * ff + j + BLOCK] = (act_grad * slope).astype(bf16)
     size = SPLIT * cap
-    own_z, own_y = place_ref[0] >> (side.bit_length() - 1), place_ref[0] & (side - 1)
     copies = []
     for j in range(0, part, BLOCK):
         halves = []
@@ -236,9 +233,7 @@
         cols = slice(j, j + BLOCK)
         for n, rows in repack(halves, cap):
             for i in range(GROUP):
-                behind = n * GROUP + i
-                z, y = (own_z - behind // side) & (side - 1), (own_y - behind % side) & (side - 1)
-                out_ref[z * side + y, :, cols] = rows[i * size : (i + 1) * size, :]
+                out_ref[place_ref[0] ^ (n * GROUP + i), :, cols] = rows[i * size : (i + 1) * size, :]
         copies += sends([(out_ref.at[:, :, cols], out_far.at[:, :, cols])], sems, len(pieces) + len(copies))
     for copy in copies:
         copy.wait()
@@ -315,14 +310,8 @@
     return lax.ppermute(value, axis, [(source, source + steps) for source in range(leading, last)])
 
 
-def offset_by(block, number, side):
-    units = lax.axis_size("expert")
-    cores = units // (side * side)
-    pairs = []
-    for u in range(units):
-        chip, core = u // cores, u % cores
-        z, y = (chip // side + number // side) % side, (chip + number) % side
-        pairs.append((u, (z * side + y) * cores + core))
+def trade(block, number):
+    pairs = [(u, (u // 2 ^ number) * 2 + u % 2) for u in range(lax.axis_size("expert"))]
     return lax.ppermute(block, "expert", pairs)
 
 
@@ -365,7 +354,6 @@
     own = (up_weight[0, 0], down_weight[0, 0])
     swap = [(i, i ^ 1) for i in range(units)]
     weights = in_hbm(*own, *(lax.ppermute(w, "expert", swap) for w in own))
-    side = 1 << (experts.bit_length() // 2)
     place = (lax.axis_index("expert") >> 1).astype(jnp.int32).reshape(1)
     half = width // SPLIT
 
@@ -394,10 +382,9 @@
         ],
         scalars=1,
         far_outs=range(experts + 1),
-        side=side,
         **sizes,
     )
-    got_b = in_hbm(blocks[0]) + [offset_by(b, n, side) for n, b in enumerate(blocks) if n > 0]
+    got_b = in_hbm(blocks[0]) + [trade(b, n) for n, b in enumerate(blocks) if n > 0]
 
     rows_buffer = pltpu.VMEM((slots, width), bf16)
     hidden_buffer = pltpu.VMEM((slots, 2 * ff), bf16)
@@ -426,7 +413,6 @@
         far_outs=(0,),
         scalars=1,
         cap=cap,
-        side=side,
     )
     back_b = exchange(result_b.reshape(SPLIT * slots, half), experts)
 

time: 163 us -> 163 us (level)
  waiting for transfers between devices: 58 us -> 55.5 us
  starting transfers between devices: 63.5 us -> 65.9 us
    ppermute x15, waiting for transfers between devices: 30.7 us -> 24.6 us  [trade(): return lax.ppermute(block, 'expert', pairs)]
    all_to_all x3, waiting for transfers between devices: 17 us -> 19.5 us  [exchange(): lax.all_to_all(parts, 'expert', 0, 0, axis_index_groups=groups, tiled=True)]
    ppermute x15, starting transfers between devices: 32.9 us -> 35.2 us  [trade(): return lax.ppermute(block, 'expert', pairs)]
where the time goes in v3:
time: 163 us
  starting transfers between devices  65.9 us (40%)
  waiting for transfers between devices  55.5 us (34%)
  Pallas kernels  39.4 us (24%)
    pallas_call x7, Pallas kernels, kernel(): pl.pallas_call(functools.partial(body, **statics), out_shape=outs, in_spe...  39.4 us
    ppermute x15, starting transfers between devices, trade(): return lax.ppermute(block, 'expert', pairs)  35.2 us
    all_to_all x3, starting transfers between devices, exchange(): lax.all_to_all(parts, 'expert', 0, 0, axis_index_groups=groups, tiled=True)  25.4 us
    ppermute x15, waiting for transfers between devices, trade(): return lax.ppermute(block, 'expert', pairs)  24.6 us
    all_to_all x3, waiting for transfers between devices, exchange(): lax.all_to_all(parts, 'expert', 0, 0, axis_index_groups=groups, tiled=True)  19.5 us
    ppermute x2, waiting for transfers between devices, shifted(): lax.ppermute(value, axis, [(source, source + steps) for source in range(l...  11.4 us
    ppermute x2, starting transfers between devices, shifted(): lax.ppermute(value, axis, [(source, source + steps) for source in range(l...  4.76 us
  transfers between devices with their start and end apart: 22, of which 9 were waited for; matrix products, arithmetic and copies ran while one was open for 0% of the time, Pallas kernels for 24%

profile of v3, /device:TPU:0, one launch (start us, length us, event | category | flops | bytes accessed | tf_op | source)
XLA Modules:
  0.0 162.6 jit_solution(12169912604496780904)
XLA Ops:
  1.2 3.1 %shard_map.122 = bf16[640,1024]{1,0:T(8,128)(2,1)} custom-call(f32[128,2048]{1,0:T(8,128)} %bitcast.47, f32[3,1,2048]{2,1,0:T(1,128)} %bitcast.36, s32[2,128]{1,0:T(2,128)} %bitcast.40), custom_call_target="tpu_custom_call" | custom-call | flops 335544320 | bytes 537088 | tf_op jit(solution)/shard_map/pallas_call | solution.py:296
  4.4 8.3 %all-to-all-start = ((bf16[16,40,1024]{2,1,0:T(8,128)(2,1)}), bf16[16,40,1024]{2,1,0:T(8,128)(2,1)S(1)}, u32[]{:S(2)}, u32[]{:S(2)}) async-start(bf16[16,40,1024]{2,1,0:T(8,128)(2,1)} %bitcast.46), calls=%async_computation | async-start | bytes 2621440 | tf_op jit(solution)/shard_map/all_to_all | solution.py:323
  12.8 3.6 %shard_map.126 = (bf16[80,1024]{1,0:T(8,128)(2,1)}, bf16[80,1024]{1,0:T(8,128)(2,1)}, bf16[80,1024]{1,0:T(8,128)(2,1)}, bf16[80,1024]{1,0:T(8,128)(2,1)}, bf16[8...) custom-call(s32[1]{0:T(128)} %bitcast.15.place_ref, ...), custom_call_target="tpu_custom_call" | custom-call | flops 1006632960 | bytes 1061890 | tf_op jit(solution)/shard_map/pallas_call | solution.py:296
  16.4 3.5 %collective-permute-start.10 = (bf16[80,1024]{1,0:T(8,128)(2,1)}, bf16[80,1024]{1,0:T(8,128)(2,1)S(1)}, u32[]{:S(2)}, u32[]{:S(2)}) collective-permute-start(bf16[80,1024]{1,0:T(8,128)(2,1)} %get-tuple-element.29), channel_id=1, source_target_pairs={{0,16},{1,17},{2,18},{3,19},{4,20},{5,21},{6,22},{7,23},{8,24},{9,... | collective-permute-start | bytes 491528 | tf_op jit(solution)/shard_map/ppermute | solution.py:315
  19.9 1.5 collective-permute-start.11
  21.4 5.1 %collective-permute-start.12 = (bf16[80,1024]{1,0:T(8,128)(2,1)}, bf16[80,1024]{1,0:T(8,128)(2,1)S(1)}, u32[]{:S(2)}, u32[]{:S(2)}) collective-permute-start(bf16[80,1024]{1,0:T(8,128)(2,1)} %get-tuple-element.31), channel_id=1, source_target_pairs={{0,20},{1,21},{2,22},{3,23},{4,16},{5,17},{6,18},{7,19},{8,28},{9,... | collective-permute-start | bytes 491528 | tf_op jit(solution)/shard_map/ppermute | solution.py:315
  26.6 3.1 %collective-permute-start.14 = (bf16[80,1024]{1,0:T(8,128)(2,1)}, bf16[80,1024]{1,0:T(8,128)(2,1)}, u32[]{:S(2)}, u32[]{:S(2)}) collective-permute-start(bf16[80,1024]{1,0:T(8,128)(2,1)} %get-tuple-element.33), channel_id=1, source_target_pairs={{0,24},{1,25},{2,26},{3,27},{4,28},{5,29},{6,30},{7,31},{8,16},{9,... | collective-permute-start | bytes 491528 | tf_op jit(solution)/shard_map/ppermute | solution.py:315
  29.7 6.7 %all-to-all-done = bf16[16,40,1024]{2,1,0:T(8,128)(2,1)S(1)} async-done(((bf16[16,40,1024]{2,1,0:T(8,128)(2,1)}), bf16[16,40,1024]{2,1,0:T(8,128)(2,1)S(1)}, u32[]{:S(2)}, u32[]{:S(2)}) %all-to-all-start) | async-done | bytes 1310752 | tf_op jit(solution)/shard_map/all_to_all | solution.py:323
  36.4 10.7 %shard_map.123 = bf16[640,1024]{1,0:T(8,128)(2,1)} custom-call(bf16[640,1024]{1,0:T(8,128)(2,1)S(1)} %bitcast.31, bf16[2048,1024]{1,0:T(8,128)(2,1)} %bitcast.53, bf16[1024,2048]{1,0:T(8,128)(2,1)} %bitcast.56, bf16[2048,1024]{1,0:T(8,128)(2,1)} %collective-permute-done.refs_2_.refs_18_, bf16[1024,2048]{1,0:T(8,128)(2,1)} %collective-permute-done.1.refs_3_.refs_19_), custom_call_target="tpu_custom_call" | custom-call | flops 5368709120 | bytes 18087936 | tf_op jit(solution)/shard_map/pallas_call | solution.py:296
  47.2 13.0 %all-to-all-start.1 = ((bf16[16,40,1024]{2,1,0:T(8,128)(2,1)}), bf16[16,40,1024]{2,1,0:T(8,128)(2,1)S(1)}, u32[]{:S(2)}, u32[]{:S(2)}) async-start(bf16[16,40,1024]{2,1,0:T(8,128)(2,1)} %bitcast.49), calls=%async_computation.1 | async-start | bytes 2621440 | tf_op jit(solution)/shard_map/all_to_all | solution.py:323
  60.2 4.1 %collective-permute-start.15 = (bf16[80,1024]{1,0:T(8,128)(2,1)}, bf16[80,1024]{1,0:T(8,128)(2,1)S(1)}, u32[]{:S(2)}, u32[]{:S(2)}) collective-permute-start(bf16[80,1024]{1,0:T(8,128)(2,1)} %get-tuple-element.34), channel_id=1, source_target_pairs={{0,26},{1,27},{2,24},{3,25},{4,30},{5,31},{6,28},{7,29},{8,18},{9,... | collective-permute-start | bytes 491528 | tf_op jit(solution)/shard_map/ppermute | solution.py:315
  64.3 2.7 %collective-permute-start.16 = (bf16[80,1024]{1,0:T(8,128)(2,1)}, bf16[80,1024]{1,0:T(8,128)(2,1)S(1)}, u32[]{:S(2)}, u32[]{:S(2)}) collective-permute-start(bf16[80,1024]{1,0:T(8,128)(2,1)} %get-tuple-element.35), channel_id=1, source_target_pairs={{0,28},{1,29},{2,30},{3,31},{4,24},{5,25},{6,26},{7,27},{8,20},{9,... | collective-permute-start | bytes 491528 | tf_op jit(solution)/shard_map/ppermute | solution.py:315
  67.0 2.7 %collective-permute-start.17 = (bf16[80,1024]{1,0:T(8,128)(2,1)S(1)}, bf16[80,1024]{1,0:T(8,128)(2,1)S(1)}, u32[]{:S(2)}, u32[]{:S(2)}) collective-permute-start(bf16[80,1024]{1,0:T(8,128)(2,1)S(1)} %copy-done.15), channel_id=1, source_target_pairs={{0,30},{1,31},{2,28},{3,29},{4,26},{5,27},{6,24},{7,25},{8,22},{9,... | collective-permute-start | bytes 491528 | tf_op jit(solution)/shard_map/ppermute | solution.py:315
  70.0 3.9 %collective-permute-start.4 = (bf16[80,1024]{1,0:T(8,128)(2,1)S(1)}, bf16[80,1024]{1,0:T(8,128)(2,1)S(1)}, u32[]{:S(2)}, u32[]{:S(2)}) collective-permute-start(bf16[80,1024]{1,0:T(8,128)(2,1)S(1)} %copy-done.13), channel_id=1, source_target_pairs={{0,4},{1,5},{2,6},{3,7},{4,0},{5,1},{6,2},{7,3},{8,12},{9,13},{10,... | collective-permute-start | bytes 491528 | tf_op jit(solution)/shard_map/ppermute | solution.py:315
  73.8 11.6 %collective-permute-done.15.refs_13_ = bf16[80,1024]{1,0:T(8,128)(2,1)S(1)} collective-permute-done((bf16[80,1024]{1,0:T(8,128)(2,1)}, bf16[80,1024]{1,0:T(8,128)(2,1)S(1)}, u32[]{:S(2)}, u32[]{:S(2)}) %collective-permute-start.15) | collective-permute-done | bytes 163872 | tf_op jit(solution)/shard_map/ppermute | solution.py:315
  85.4 4.6 %collective-permute-start.5 = (bf16[80,1024]{1,0:T(8,128)(2,1)S(1)}, bf16[80,1024]{1,0:T(8,128)(2,1)S(1)}, u32[]{:S(2)}, u32[]{:S(2)}) collective-permute-start(bf16[80,1024]{1,0:T(8,128)(2,1)S(1)} %copy-done.12), channel_id=1, source_target_pairs={{0,6},{1,7},{2,4},{3,5},{4,2},{5,3},{6,0},{7,1},{8,14},{9,15},{10,... | collective-permute-start | bytes 491528 | tf_op jit(solution)/shard_map/ppermute | solution.py:315
  90.1 1.4 collective-permute-done.16.refs_14_
  91.4 2.0 %collective-permute-start.6 = (bf16[80,1024]{1,0:T(8,128)(2,1)S(1)}, bf16[80,1024]{1,0:T(8,128)(2,1)S(1)}, u32[]{:S(2)}, u32[]{:S(2)}) collective-permute-start(bf16[80,1024]{1,0:T(8,128)(2,1)S(1)} %copy-done.11), channel_id=1, source_target_pairs={{0,8},{1,9},{2,10},{3,11},{4,12},{5,13},{6,14},{7,15},{8,0},{9,1},... | collective-permute-start | bytes 491528 | tf_op jit(solution)/shard_map/ppermute | solution.py:315
  93.5 1.5 collective-permute-start.8
  95.0 3.5 %collective-permute-done.4.refs_2_ = bf16[80,1024]{1,0:T(8,128)(2,1)S(1)} collective-permute-done((bf16[80,1024]{1,0:T(8,128)(2,1)S(1)}, bf16[80,1024]{1,0:T(8,128)(2,1)S(1)}, u32[]{:S(2)}, u32[]{:S(2)}) %collective-permute-start.4) | collective-permute-done | bytes 163872 | tf_op jit(solution)/shard_map/ppermute | solution.py:315
  98.6 1.9 %collective-permute-done.6.refs_4_ = bf16[80,1024]{1,0:T(8,128)(2,1)S(1)} collective-permute-done((bf16[80,1024]{1,0:T(8,128)(2,1)S(1)}, bf16[80,1024]{1,0:T(8,128)(2,1)S(1)}, u32[]{:S(2)}, u32[]{:S(2)}) %collective-permute-start.6) | collective-permute-done | bytes 163872 | tf_op jit(solution)/shard_map/ppermute | solution.py:315
  100.5 2.8 %collective-permute-done.8.refs_6_ = bf16[80,1024]{1,0:T(8,128)(2,1)S(1)} collective-permute-done((bf16[80,1024]{1,0:T(8,128)(2,1)S(1)}, bf16[80,1024]{1,0:T(8,128)(2,1)S(1)}, u32[]{:S(2)}, u32[]{:S(2)}) %collective-permute-start.8) | collective-permute-done | bytes 163872 | tf_op jit(solution)/shard_map/ppermute | solution.py:315
  103.3 3.4 %collective-permute-done.9.refs_7_ = bf16[80,1024]{1,0:T(8,128)(2,1)S(1)} collective-permute-done((bf16[80,1024]{1,0:T(8,128)(2,1)S(1)}, bf16[80,1024]{1,0:T(8,128)(2,1)S(1)}, u32[]{:S(2)}, u32[]{:S(2)}) %collective-permute-start.9) | collective-permute-done | bytes 163872 | tf_op jit(solution)/shard_map/ppermute | solution.py:315
  106.7 15.2 %shard_map.127 = bf16[16,40,1024]{2,1,0:T(8,128)(2,1)} custom-call(s32[1]{0:T(128)} %bitcast.15.place_ref, bf16[80,1024]{1,0:T(8,128)(2,1)} %get-tuple-element.21.refs_0_, bf16[80,1024]{1,0:T(8,128)(2,1)S(1)} %collective-permute-done.3.refs_1_, bf16[80,1024]{1,0:T(8,128)(2,1)S(1)} %collective-permute-done.4.refs_2_, ...), custom_call_target="tpu_custom_call" | custom-call | flops 8053063680 | bytes 19398658 | tf_op jit(solution)/shard_map/pallas_call | solution.py:296
  121.9 4.1 %all-to-all-start.2 = ((bf16[16,40,1024]{2,1,0:T(8,128)(2,1)}), bf16[16,40,1024]{2,1,0:T(8,128)(2,1)S(1)}, u32[]{:S(2)}, u32[]{:S(2)}) async-start(bf16[16,40,1024]{2,1,0:T(8,128)(2,1)} %shard_map.127), calls=%async_computation.2 | async-start | bytes 2621440 | tf_op jit(solution)/shard_map/all_to_all | solution.py:323
  126.1 3.5 %shard_map.124 = f32[128,2048]{1,0:T(8,128)} custom-call(bf16[640,1024]{1,0:T(8,128)(2,1)S(1)} %bitcast.30, f32[2,128]{1,0:T(2,128)S(1)} %bitcast.42, s32[2,128]{1,0:T(2,128)S(1)} %bitcast.41, f32[128,2048]{1,0:T(8,128)} %bitcast.48, f32[3,1,2048]{2,1,0:T(1,128)S(1)} %bitcast.37), custom_call_target="tpu_custom_call" | custom-call | flops 671088640 | bytes 1848320 | tf_op jit(solution)/shard_map/pallas_call | solution.py:296
  129.6 3.5 %collective-permute-start.2 = (f32[1,128,2048]{2,1,0:T(8,128)}, f32[1,128,2048]{2,1,0:T(8,128)S(1)}, u32[]{:S(2)}, u32[]{:S(2)}) collective-permute-start(f32[1,128,2048]{2,1,0:T(8,128)} %bitcast.50), channel_id=1, source_target_pairs={{0,32},{32,64},{64,96},{1,33},{33,65},{65,97},{2,34},{34,66},{66,9... | collective-permute-start | bytes 3145736 | tf_op jit(solution)/shard_map/ppermute | solution.py:310
  133.0 12.8 %all-to-all-done.2 = bf16[16,40,1024]{2,1,0:T(8,128)(2,1)S(1)} async-done(((bf16[16,40,1024]{2,1,0:T(8,128)(2,1)}), bf16[16,40,1024]{2,1,0:T(8,128)(2,1)S(1)}, u32[]{:S(2)}, u32[]{:S(2)}) %all-to-all-start.2) | async-done | bytes 1310752 | tf_op jit(solution)/shard_map/all_to_all | solution.py:323
  145.8 2.2 %shard_map.128 = bf16[128,2048]{1,0:T(8,128)(2,1)S(1)} custom-call(bf16[640,1024]{1,0:T(8,128)(2,1)S(1)} %bitcast.29, s32[128,8]{1,0:T(8,128)S(1)} %get-tuple-element.37.where_ref, f32[128,2048]{1,0:T(8,128)} %get-tuple-element.38.norm_far, f32[128,1]{1,0:T(8,128)S(1)} %get-tuple-element.39.inv_ref, bf16[128,2048]{1,0:T(8,128)(2,1)} %bitcast.33, ...), custom_call_target="tpu_custom_call" | custom-call | flops 335544320 | bytes 2373888 | tf_op jit(solution)/shard_map/pallas_call | solution.py:296
  148.0 1.3 collective-permute-start.18
  149.3 11.4 %collective-permute-done.18 = bf16[1,128,2048]{2,1,0:T(8,128)(2,1)S(1)} collective-permute-done((bf16[1,128,2048]{2,1,0:T(8,128)(2,1)S(1)}, bf16[1,128,2048]{2,1,0:T(8,128)(2,1)S(1)}, u32[]{:S(2)}, u32[]{:S(2)}) %collective-permute-start.18) | collective-permute-done | bytes 524320 | tf_op jit(solution)/shard_map/ppermute | solution.py:310
  160.7 1.0 shard_map.125
  (52 shorter events, 1.9 us)
Async XLA Ops:
  0.6 25.8 %collective-permute-start = (bf16[2048,1024]{1,0:T(8,128)(2,1)}, bf16[2048,1024]{1,0:T(8,128)(2,1)}, u32[]{:S(2)}, u32[]{:S(2)}) collective-permute-start(bf16[2048,1024]{1,0:T(8,128)(2,1)} %bitcast.52), channel_id=1, source_target_pairs={{0,1},{1,0},{2,3},{3,2},{4,5},{5,4},{6,7},{7,6},{8,9},{9,8},{10,11... | collective-permute-start | bytes 12582920 | tf_op jit(solution)/shard_map/ppermute | solution.py:356
  0.7 25.8 %collective-permute-start.1 = (bf16[1024,2048]{1,0:T(8,128)(2,1)}, bf16[1024,2048]{1,0:T(8,128)(2,1)}, u32[]{:S(2)}, u32[]{:S(2)}) collective-permute-start(bf16[1024,2048]{1,0:T(8,128)(2,1)} %bitcast.55), channel_id=1, source_target_pairs={{0,1},{1,0},{2,3},{3,2},{4,5},{5,4},{6,7},{7,6},{8,9},{9,8},{10,11... | collective-permute-start | bytes 12582920 | tf_op jit(solution)/shard_map/ppermute | solution.py:356
  4.4 8.4 %copy-start.6 = (f32[1,128,2]{1,2,0:T(2,128)S(1)}, f32[1,128,2]{1,2,0:T(2,128)}, u32[]{:S(2)}) copy-start(f32[1,128,2]{1,2,0:T(2,128)} %param.18) | copy-start | bytes 3076
  4.4 8.4 %copy-start.7 = (s32[1,128,2]{1,2,0:T(2,128)S(1)}, s32[1,128,2]{1,2,0:T(2,128)}, u32[]{:S(2)}) copy-start(s32[1,128,2]{1,2,0:T(2,128)} %param.17) | copy-start | bytes 3076
  4.4 32.0 %all-to-all-start = ((bf16[16,40,1024]{2,1,0:T(8,128)(2,1)}), bf16[16,40,1024]{2,1,0:T(8,128)(2,1)S(1)}, u32[]{:S(2)}, u32[]{:S(2)}) async-start(bf16[16,40,1024]{2,1,0:T(8,128)(2,1)} %bitcast.46), calls=%async_computation | async-start | bytes 2621440 | tf_op jit(solution)/shard_map/all_to_all | solution.py:323
  16.4 43.8 %collective-permute-start.10 = (bf16[80,1024]{1,0:T(8,128)(2,1)}, bf16[80,1024]{1,0:T(8,128)(2,1)S(1)}, u32[]{:S(2)}, u32[]{:S(2)}) collective-permute-start(bf16[80,1024]{1,0:T(8,128)(2,1)} %get-tuple-element.29), channel_id=1, source_target_pairs={{0,16},{1,17},{2,18},{3,19},{4,20},{5,21},{6,22},{7,23},{8,24},{9,... | collective-permute-start | bytes 491528 | tf_op jit(solution)/shard_map/ppermute | solution.py:315
  19.9 44.4 %collective-permute-start.11 = (bf16[80,1024]{1,0:T(8,128)(2,1)}, bf16[80,1024]{1,0:T(8,128)(2,1)S(1)}, u32[]{:S(2)}, u32[]{:S(2)}) collective-permute-start(bf16[80,1024]{1,0:T(8,128)(2,1)} %get-tuple-element.30), channel_id=1, source_target_pairs={{0,18},{1,19},{2,16},{3,17},{4,22},{5,23},{6,20},{7,21},{8,26},{9,... | collective-permute-start | bytes 491528 | tf_op jit(solution)/shard_map/ppermute | solution.py:315
  21.4 45.6 %collective-permute-start.12 = (bf16[80,1024]{1,0:T(8,128)(2,1)}, bf16[80,1024]{1,0:T(8,128)(2,1)S(1)}, u32[]{:S(2)}, u32[]{:S(2)}) collective-permute-start(bf16[80,1024]{1,0:T(8,128)(2,1)} %get-tuple-element.31), channel_id=1, source_target_pairs={{0,20},{1,21},{2,22},{3,23},{4,16},{5,17},{6,18},{7,19},{8,28},{9,... | collective-permute-start | bytes 491528 | tf_op jit(solution)/shard_map/ppermute | solution.py:315
  26.5 43.2 %collective-permute-start.13 = (bf16[80,1024]{1,0:T(8,128)(2,1)}, bf16[80,1024]{1,0:T(8,128)(2,1)S(1)}, u32[]{:S(2)}, u32[]{:S(2)}) collective-permute-start(bf16[80,1024]{1,0:T(8,128)(2,1)} %get-tuple-element.32), channel_id=1, source_target_pairs={{0,22},{1,23},{2,20},{3,21},{4,18},{5,19},{6,16},{7,17},{8,30},{9,... | collective-permute-start | bytes 491528 | tf_op jit(solution)/shard_map/ppermute | solution.py:315
  26.6 43.4 %collective-permute-start.14 = (bf16[80,1024]{1,0:T(8,128)(2,1)}, bf16[80,1024]{1,0:T(8,128)(2,1)}, u32[]{:S(2)}, u32[]{:S(2)}) collective-permute-start(bf16[80,1024]{1,0:T(8,128)(2,1)} %get-tuple-element.33), channel_id=1, source_target_pairs={{0,24},{1,25},{2,26},{3,27},{4,28},{5,29},{6,30},{7,31},{8,16},{9,... | collective-permute-start | bytes 491528 | tf_op jit(solution)/shard_map/ppermute | solution.py:315
  47.2 19.9 %copy-start.15 = (bf16[80,1024]{1,0:T(8,128)(2,1)S(1)}, bf16[80,1024]{1,0:T(8,128)(2,1)}, u32[]{:S(2)}) copy-start(bf16[80,1024]{1,0:T(8,128)(2,1)} %get-tuple-element.36) | copy-start | bytes 491524
  47.2 22.5 %copy-start.14 = (bf16[80,1024]{1,0:T(8,128)(2,1)S(1)}, bf16[80,1024]{1,0:T(8,128)(2,1)}, u32[]{:S(2)}) copy-start(bf16[80,1024]{1,0:T(8,128)(2,1)} %get-tuple-element.22) | copy-start | bytes 491524
  47.2 22.8 %copy-start.13 = (bf16[80,1024]{1,0:T(8,128)(2,1)S(1)}, bf16[80,1024]{1,0:T(8,128)(2,1)}, u32[]{:S(2)}) copy-start(bf16[80,1024]{1,0:T(8,128)(2,1)} %get-tuple-element.23) | copy-start | bytes 491524
  47.2 38.2 %copy-start.12 = (bf16[80,1024]{1,0:T(8,128)(2,1)S(1)}, bf16[80,1024]{1,0:T(8,128)(2,1)}, u32[]{:S(2)}) copy-start(bf16[80,1024]{1,0:T(8,128)(2,1)} %get-tuple-element.24) | copy-start | bytes 491524
  47.2 44.2 %copy-start.11 = (bf16[80,1024]{1,0:T(8,128)(2,1)S(1)}, bf16[80,1024]{1,0:T(8,128)(2,1)}, u32[]{:S(2)}) copy-start(bf16[80,1024]{1,0:T(8,128)(2,1)} %get-tuple-element.25) | copy-start | bytes 491524
  47.2 46.3 %copy-start.10 = (bf16[80,1024]{1,0:T(8,128)(2,1)S(1)}, bf16[80,1024]{1,0:T(8,128)(2,1)}, u32[]{:S(2)}) copy-start(bf16[80,1024]{1,0:T(8,128)(2,1)} %get-tuple-element.26) | copy-start | bytes 491524
  47.2 46.3 %copy-start.9 = (bf16[80,1024]{1,0:T(8,128)(2,1)S(1)}, bf16[80,1024]{1,0:T(8,128)(2,1)}, u32[]{:S(2)}) copy-start(bf16[80,1024]{1,0:T(8,128)(2,1)} %get-tuple-element.27) | copy-start | bytes 491524
  47.2 51.3 %copy-start.8 = (bf16[80,1024]{1,0:T(8,128)(2,1)S(1)}, bf16[80,1024]{1,0:T(8,128)(2,1)}, u32[]{:S(2)}) copy-start(bf16[80,1024]{1,0:T(8,128)(2,1)} %get-tuple-element.28) | copy-start | bytes 491524
  47.2 74.7 %all-to-all-start.1 = ((bf16[16,40,1024]{2,1,0:T(8,128)(2,1)}), bf16[16,40,1024]{2,1,0:T(8,128)(2,1)S(1)}, u32[]{:S(2)}, u32[]{:S(2)}) async-start(bf16[16,40,1024]{2,1,0:T(8,128)(2,1)} %bitcast.49), calls=%async_computation.1 | async-start | bytes 2621440 | tf_op jit(solution)/shard_map/all_to_all | solution.py:323
  60.2 25.2 %collective-permute-start.15 = (bf16[80,1024]{1,0:T(8,128)(2,1)}, bf16[80,1024]{1,0:T(8,128)(2,1)S(1)}, u32[]{:S(2)}, u32[]{:S(2)}) collective-permute-start(bf16[80,1024]{1,0:T(8,128)(2,1)} %get-tuple-element.34), channel_id=1, source_target_pairs={{0,26},{1,27},{2,24},{3,25},{4,30},{5,31},{6,28},{7,29},{8,18},{9,... | collective-permute-start | bytes 491528 | tf_op jit(solution)/shard_map/ppermute | solution.py:315
  64.3 27.1 %collective-permute-start.16 = (bf16[80,1024]{1,0:T(8,128)(2,1)}, bf16[80,1024]{1,0:T(8,128)(2,1)S(1)}, u32[]{:S(2)}, u32[]{:S(2)}) collective-permute-start(bf16[80,1024]{1,0:T(8,128)(2,1)} %get-tuple-element.35), channel_id=1, source_target_pairs={{0,28},{1,29},{2,30},{3,31},{4,24},{5,25},{6,26},{7,27},{8,20},{9,... | collective-permute-start | bytes 491528 | tf_op jit(solution)/shard_map/ppermute | solution.py:315
  67.0 26.5 %collective-permute-start.17 = (bf16[80,1024]{1,0:T(8,128)(2,1)S(1)}, bf16[80,1024]{1,0:T(8,128)(2,1)S(1)}, u32[]{:S(2)}, u32[]{:S(2)}) collective-permute-start(bf16[80,1024]{1,0:T(8,128)(2,1)S(1)} %copy-done.15), channel_id=1, source_target_pairs={{0,30},{1,31},{2,28},{3,29},{4,26},{5,27},{6,24},{7,25},{8,22},{9,... | collective-permute-start | bytes 491528 | tf_op jit(solution)/shard_map/ppermute | solution.py:315
  69.7 23.8 %collective-permute-start.3 = (bf16[80,1024]{1,0:T(8,128)(2,1)S(1)}, bf16[80,1024]{1,0:T(8,128)(2,1)S(1)}, u32[]{:S(2)}, u32[]{:S(2)}) collective-permute-start(bf16[80,1024]{1,0:T(8,128)(2,1)S(1)} %copy-done.14), channel_id=1, source_target_pairs={{0,2},{1,3},{2,0},{3,1},{4,6},{5,7},{6,4},{7,5},{8,10},{9,11},{10,... | collective-permute-start | bytes 491528 | tf_op jit(solution)/shard_map/ppermute | solution.py:315
  70.0 28.6 %collective-permute-start.4 = (bf16[80,1024]{1,0:T(8,128)(2,1)S(1)}, bf16[80,1024]{1,0:T(8,128)(2,1)S(1)}, u32[]{:S(2)}, u32[]{:S(2)}) collective-permute-start(bf16[80,1024]{1,0:T(8,128)(2,1)S(1)} %copy-done.13), channel_id=1, source_target_pairs={{0,4},{1,5},{2,6},{3,7},{4,0},{5,1},{6,2},{7,3},{8,12},{9,13},{10,... | collective-permute-start | bytes 491528 | tf_op jit(solution)/shard_map/ppermute | solution.py:315
  85.4 13.2 %collective-permute-start.5 = (bf16[80,1024]{1,0:T(8,128)(2,1)S(1)}, bf16[80,1024]{1,0:T(8,128)(2,1)S(1)}, u32[]{:S(2)}, u32[]{:S(2)}) collective-permute-start(bf16[80,1024]{1,0:T(8,128)(2,1)S(1)} %copy-done.12), channel_id=1, source_target_pairs={{0,6},{1,7},{2,4},{3,5},{4,2},{5,3},{6,0},{7,1},{8,14},{9,15},{10,... | collective-permute-start | bytes 491528 | tf_op jit(solution)/shard_map/ppermute | solution.py:315
  91.4 9.1 %collective-permute-start.6 = (bf16[80,1024]{1,0:T(8,128)(2,1)S(1)}, bf16[80,1024]{1,0:T(8,128)(2,1)S(1)}, u32[]{:S(2)}, u32[]{:S(2)}) collective-permute-start(bf16[80,1024]{1,0:T(8,128)(2,1)S(1)} %copy-done.11), channel_id=1, source_target_pairs={{0,8},{1,9},{2,10},{3,11},{4,12},{5,13},{6,14},{7,15},{8,0},{9,1},... | collective-permute-start | bytes 491528 | tf_op jit(solution)/shard_map/ppermute | solution.py:315
  93.5 7.0 %collective-permute-start.7 = (bf16[80,1024]{1,0:T(8,128)(2,1)S(1)}, bf16[80,1024]{1,0:T(8,128)(2,1)S(1)}, u32[]{:S(2)}, u32[]{:S(2)}) collective-permute-start(bf16[80,1024]{1,0:T(8,128)(2,1)S(1)} %copy-done.10), channel_id=1, source_target_pairs={{0,10},{1,11},{2,8},{3,9},{4,14},{5,15},{6,12},{7,13},{8,2},{9,3},... | collective-permute-start | bytes 491528 | tf_op jit(solution)/shard_map/ppermute | solution.py:315
  93.5 9.8 %collective-permute-start.8 = (bf16[80,1024]{1,0:T(8,128)(2,1)S(1)}, bf16[80,1024]{1,0:T(8,128)(2,1)S(1)}, u32[]{:S(2)}, u32[]{:S(2)}) collective-permute-start(bf16[80,1024]{1,0:T(8,128)(2,1)S(1)} %copy-done.9), channel_id=1, source_target_pairs={{0,12},{1,13},{2,14},{3,15},{4,8},{5,9},{6,10},{7,11},{8,4},{9,5},... | collective-permute-start | bytes 491528 | tf_op jit(solution)/shard_map/ppermute | solution.py:315
  98.5 8.2 %collective-permute-start.9 = (bf16[80,1024]{1,0:T(8,128)(2,1)S(1)}, bf16[80,1024]{1,0:T(8,128)(2,1)S(1)}, u32[]{:S(2)}, u32[]{:S(2)}) collective-permute-start(bf16[80,1024]{1,0:T(8,128)(2,1)S(1)} %copy-done.8), channel_id=1, source_target_pairs={{0,14},{1,15},{2,12},{3,13},{4,10},{5,11},{6,8},{7,9},{8,6},{9,7},... | collective-permute-start | bytes 491528 | tf_op jit(solution)/shard_map/ppermute | solution.py:315
  121.9 23.8 %all-to-all-start.2 = ((bf16[16,40,1024]{2,1,0:T(8,128)(2,1)}), bf16[16,40,1024]{2,1,0:T(8,128)(2,1)S(1)}, u32[]{:S(2)}, u32[]{:S(2)}) async-start(bf16[16,40,1024]{2,1,0:T(8,128)(2,1)} %shard_map.127), calls=%async_computation.2 | async-start | bytes 2621440 | tf_op jit(solution)/shard_map/all_to_all | solution.py:323
  129.6 31.2 %collective-permute-start.2 = (f32[1,128,2048]{2,1,0:T(8,128)}, f32[1,128,2048]{2,1,0:T(8,128)S(1)}, u32[]{:S(2)}, u32[]{:S(2)}) collective-permute-start(f32[1,128,2048]{2,1,0:T(8,128)} %bitcast.50), channel_id=1, source_target_pairs={{0,32},{32,64},{64,96},{1,33},{33,65},{65,97},{2,34},{34,66},{66,9... | collective-permute-start | bytes 3145736 | tf_op jit(solution)/shard_map/ppermute | solution.py:310
  148.0 12.7 %collective-permute-start.18 = (bf16[1,128,2048]{2,1,0:T(8,128)(2,1)S(1)}, bf16[1,128,2048]{2,1,0:T(8,128)(2,1)S(1)}, u32[]{:S(2)}, u32[]{:S(2)}) collective-permute-start(bf16[1,128,2048]{2,1,0:T(8,128)(2,1)S(1)} %bitcast.35), channel_id=1, source_target_pairs={{32,0},{64,32},{96,64},{33,1},{65,33},{97,65},{34,2},{66,34},{98,6... | collective-permute-start | bytes 1572872 | tf_op jit(solution)/shard_map/ppermute | solution.py:310
  (6 other events, 37.5 us)

commit v4 on v3

--- a/solution.py
+++ b/solution.py
@@ -262,10 +262,12 @@
     tokens = norm_ref.shape[0]
     numbers = iota((tokens, r_ref.shape[0]), 1)
     places = where_ref[...]
-    halves = []
+    picks = []
     for h in range(SPLIT):
         hit = (numbers == places[:, 2:3] + h * cap) | (numbers == places[:, 3:4] + h * cap)
-        halves.append(dot(ones_where(hit).astype(bf16), r_ref[...]))
+        picks.append(ones_where(hit).astype(bf16))
+    both = dot(jnp.concatenate(picks, 0), r_ref[...])
+    halves = [both[h * tokens : (h + 1) * tokens, :] for h in range(SPLIT)]
     dnorm = jnp.concatenate(halves, 1) * (1.0 + mod_ref[1])
     mean_one = jnp.mean(dnorm, axis=-1, keepdims=True)
     next(ready)

time: 163 us -> 163 us (level)
  no operation moved by 1% of the time
where the time goes in v4:
time: 163 us
  starting transfers between devices  65.9 us (40%)
  waiting for transfers between devices  55.5 us (34%)
  Pallas kernels  39.4 us (24%)
    pallas_call x7, Pallas kernels, kernel(): pl.pallas_call(functools.partial(body, **statics), out_shape=outs, in_spe...  39.4 us
    ppermute x15, starting transfers between devices, trade(): return lax.ppermute(block, 'expert', pairs)  35.2 us
    all_to_all x3, starting transfers between devices, exchange(): lax.all_to_all(parts, 'expert', 0, 0, axis_index_groups=groups, tiled=True)  25.4 us
    ppermute x15, waiting for transfers between devices, trade(): return lax.ppermute(block, 'expert', pairs)  24.6 us
    all_to_all x3, waiting for transfers between devices, exchange(): lax.all_to_all(parts, 'expert', 0, 0, axis_index_groups=groups, tiled=True)  19.5 us
    ppermute x2, waiting for transfers between devices, shifted(): lax.ppermute(value, axis, [(source, source + steps) for source in range(l...  11.4 us
    ppermute x2, starting transfers between devices, shifted(): lax.ppermute(value, axis, [(source, source + steps) for source in range(l...  4.76 us
  transfers between devices with their start and end apart: 22, of which 9 were waited for; matrix products, arithmetic and copies ran while one was open for 0% of the time, Pallas kernels for 24%

profile of v4, /device:TPU:0, one launch (start us, length us, event | category | flops | bytes accessed | tf_op | source)
XLA Modules:
  0.0 162.6 jit_solution(9942874196835210073)
XLA Ops:
  1.2 3.1 %shard_map.122 = bf16[640,1024]{1,0:T(8,128)(2,1)} custom-call(f32[128,2048]{1,0:T(8,128)} %bitcast.47, f32[3,1,2048]{2,1,0:T(1,128)} %bitcast.36, s32[2,128]{1,0:T(2,128)} %bitcast.40), custom_call_target="tpu_custom_call" | custom-call | flops 335544320 | bytes 537088 | tf_op jit(solution)/shard_map/pallas_call | solution.py:298
  4.4 8.3 %all-to-all-start = ((bf16[16,40,1024]{2,1,0:T(8,128)(2,1)}), bf16[16,40,1024]{2,1,0:T(8,128)(2,1)S(1)}, u32[]{:S(2)}, u32[]{:S(2)}) async-start(bf16[16,40,1024]{2,1,0:T(8,128)(2,1)} %bitcast.46), calls=%async_computation | async-start | bytes 2621440 | tf_op jit(solution)/shard_map/all_to_all | solution.py:325
  12.8 3.6 %shard_map.126 = (bf16[80,1024]{1,0:T(8,128)(2,1)}, bf16[80,1024]{1,0:T(8,128)(2,1)}, bf16[80,1024]{1,0:T(8,128)(2,1)}, bf16[80,1024]{1,0:T(8,128)(2,1)}, bf16[8...) custom-call(s32[1]{0:T(128)} %bitcast.15.place_ref, ...), custom_call_target="tpu_custom_call" | custom-call | flops 1006632960 | bytes 1061890 | tf_op jit(solution)/shard_map/pallas_call | solution.py:298
  16.4 3.5 %collective-permute-start.10 = (bf16[80,1024]{1,0:T(8,128)(2,1)}, bf16[80,1024]{1,0:T(8,128)(2,1)S(1)}, u32[]{:S(2)}, u32[]{:S(2)}) collective-permute-start(bf16[80,1024]{1,0:T(8,128)(2,1)} %get-tuple-element.29), channel_id=1, source_target_pairs={{0,16},{1,17},{2,18},{3,19},{4,20},{5,21},{6,22},{7,23},{8,24},{9,... | collective-permute-start | bytes 491528 | tf_op jit(solution)/shard_map/ppermute | solution.py:317
  19.9 1.5 collective-permute-start.11
  21.4 5.1 %collective-permute-start.12 = (bf16[80,1024]{1,0:T(8,128)(2,1)}, bf16[80,1024]{1,0:T(8,128)(2,1)S(1)}, u32[]{:S(2)}, u32[]{:S(2)}) collective-permute-start(bf16[80,1024]{1,0:T(8,128)(2,1)} %get-tuple-element.31), channel_id=1, source_target_pairs={{0,20},{1,21},{2,22},{3,23},{4,16},{5,17},{6,18},{7,19},{8,28},{9,... | collective-permute-start | bytes 491528 | tf_op jit(solution)/shard_map/ppermute | solution.py:317
  26.6 3.1 %collective-permute-start.14 = (bf16[80,1024]{1,0:T(8,128)(2,1)}, bf16[80,1024]{1,0:T(8,128)(2,1)}, u32[]{:S(2)}, u32[]{:S(2)}) collective-permute-start(bf16[80,1024]{1,0:T(8,128)(2,1)} %get-tuple-element.33), channel_id=1, source_target_pairs={{0,24},{1,25},{2,26},{3,27},{4,28},{5,29},{6,30},{7,31},{8,16},{9,... | collective-permute-start | bytes 491528 | tf_op jit(solution)/shard_map/ppermute | solution.py:317
  29.7 6.7 %all-to-all-done = bf16[16,40,1024]{2,1,0:T(8,128)(2,1)S(1)} async-done(((bf16[16,40,1024]{2,1,0:T(8,128)(2,1)}), bf16[16,40,1024]{2,1,0:T(8,128)(2,1)S(1)}, u32[]{:S(2)}, u32[]{:S(2)}) %all-to-all-start) | async-done | bytes 1310752 | tf_op jit(solution)/shard_map/all_to_all | solution.py:325
  36.4 10.7 %shard_map.123 = bf16[640,1024]{1,0:T(8,128)(2,1)} custom-call(bf16[640,1024]{1,0:T(8,128)(2,1)S(1)} %bitcast.31, bf16[2048,1024]{1,0:T(8,128)(2,1)} %bitcast.53, bf16[1024,2048]{1,0:T(8,128)(2,1)} %bitcast.56, bf16[2048,1024]{1,0:T(8,128)(2,1)} %collective-permute-done.refs_2_.refs_18_, bf16[1024,2048]{1,0:T(8,128)(2,1)} %collective-permute-done.1.refs_3_.refs_19_), custom_call_target="tpu_custom_call" | custom-call | flops 5368709120 | bytes 18087936 | tf_op jit(solution)/shard_map/pallas_call | solution.py:298
  47.2 13.0 %all-to-all-start.1 = ((bf16[16,40,1024]{2,1,0:T(8,128)(2,1)}), bf16[16,40,1024]{2,1,0:T(8,128)(2,1)S(1)}, u32[]{:S(2)}, u32[]{:S(2)}) async-start(bf16[16,40,1024]{2,1,0:T(8,128)(2,1)} %bitcast.49), calls=%async_computation.1 | async-start | bytes 2621440 | tf_op jit(solution)/shard_map/all_to_all | solution.py:325
  60.2 4.1 %collective-permute-start.15 = (bf16[80,1024]{1,0:T(8,128)(2,1)}, bf16[80,1024]{1,0:T(8,128)(2,1)S(1)}, u32[]{:S(2)}, u32[]{:S(2)}) collective-permute-start(bf16[80,1024]{1,0:T(8,128)(2,1)} %get-tuple-element.34), channel_id=1, source_target_pairs={{0,26},{1,27},{2,24},{3,25},{4,30},{5,31},{6,28},{7,29},{8,18},{9,... | collective-permute-start | bytes 491528 | tf_op jit(solution)/shard_map/ppermute | solution.py:317
  64.3 2.7 %collective-permute-start.16 = (bf16[80,1024]{1,0:T(8,128)(2,1)}, bf16[80,1024]{1,0:T(8,128)(2,1)S(1)}, u32[]{:S(2)}, u32[]{:S(2)}) collective-permute-start(bf16[80,1024]{1,0:T(8,128)(2,1)} %get-tuple-element.35), channel_id=1, source_target_pairs={{0,28},{1,29},{2,30},{3,31},{4,24},{5,25},{6,26},{7,27},{8,20},{9,... | collective-permute-start | bytes 491528 | tf_op jit(solution)/shard_map/ppermute | solution.py:317
  67.0 2.7 %collective-permute-start.17 = (bf16[80,1024]{1,0:T(8,128)(2,1)S(1)}, bf16[80,1024]{1,0:T(8,128)(2,1)S(1)}, u32[]{:S(2)}, u32[]{:S(2)}) collective-permute-start(bf16[80,1024]{1,0:T(8,128)(2,1)S(1)} %copy-done.15), channel_id=1, source_target_pairs={{0,30},{1,31},{2,28},{3,29},{4,26},{5,27},{6,24},{7,25},{8,22},{9,... | collective-permute-start | bytes 491528 | tf_op jit(solution)/shard_map/ppermute | solution.py:317
  70.0 3.9 %collective-permute-start.4 = (bf16[80,1024]{1,0:T(8,128)(2,1)S(1)}, bf16[80,1024]{1,0:T(8,128)(2,1)S(1)}, u32[]{:S(2)}, u32[]{:S(2)}) collective-permute-start(bf16[80,1024]{1,0:T(8,128)(2,1)S(1)} %copy-done.13), channel_id=1, source_target_pairs={{0,4},{1,5},{2,6},{3,7},{4,0},{5,1},{6,2},{7,3},{8,12},{9,13},{10,... | collective-permute-start | bytes 491528 | tf_op jit(solution)/shard_map/ppermute | solution.py:317
  73.8 11.6 %collective-permute-done.15.refs_13_ = bf16[80,1024]{1,0:T(8,128)(2,1)S(1)} collective-permute-done((bf16[80,1024]{1,0:T(8,128)(2,1)}, bf16[80,1024]{1,0:T(8,128)(2,1)S(1)}, u32[]{:S(2)}, u32[]{:S(2)}) %collective-permute-start.15) | collective-permute-done | bytes 163872 | tf_op jit(solution)/shard_map/ppermute | solution.py:317
  85.4 4.6 %collective-permute-start.5 = (bf16[80,1024]{1,0:T(8,128)(2,1)S(1)}, bf16[80,1024]{1,0:T(8,128)(2,1)S(1)}, u32[]{:S(2)}, u32[]{:S(2)}) collective-permute-start(bf16[80,1024]{1,0:T(8,128)(2,1)S(1)} %copy-done.12), channel_id=1, source_target_pairs={{0,6},{1,7},{2,4},{3,5},{4,2},{5,3},{6,0},{7,1},{8,14},{9,15},{10,... | collective-permute-start | bytes 491528 | tf_op jit(solution)/shard_map/ppermute | solution.py:317
  90.1 1.4 collective-permute-done.16.refs_14_
  91.4 2.0 %collective-permute-start.6 = (bf16[80,1024]{1,0:T(8,128)(2,1)S(1)}, bf16[80,1024]{1,0:T(8,128)(2,1)S(1)}, u32[]{:S(2)}, u32[]{:S(2)}) collective-permute-start(bf16[80,1024]{1,0:T(8,128)(2,1)S(1)} %copy-done.11), channel_id=1, source_target_pairs={{0,8},{1,9},{2,10},{3,11},{4,12},{5,13},{6,14},{7,15},{8,0},{9,1},... | collective-permute-start | bytes 491528 | tf_op jit(solution)/shard_map/ppermute | solution.py:317
  93.5 1.5 collective-permute-start.8
  95.0 3.5 %collective-permute-done.4.refs_2_ = bf16[80,1024]{1,0:T(8,128)(2,1)S(1)} collective-permute-done((bf16[80,1024]{1,0:T(8,128)(2,1)S(1)}, bf16[80,1024]{1,0:T(8,128)(2,1)S(1)}, u32[]{:S(2)}, u32[]{:S(2)}) %collective-permute-start.4) | collective-permute-done | bytes 163872 | tf_op jit(solution)/shard_map/ppermute | solution.py:317
  98.6 1.9 %collective-permute-done.6.refs_4_ = bf16[80,1024]{1,0:T(8,128)(2,1)S(1)} collective-permute-done((bf16[80,1024]{1,0:T(8,128)(2,1)S(1)}, bf16[80,1024]{1,0:T(8,128)(2,1)S(1)}, u32[]{:S(2)}, u32[]{:S(2)}) %collective-permute-start.6) | collective-permute-done | bytes 163872 | tf_op jit(solution)/shard_map/ppermute | solution.py:317
  100.5 2.8 %collective-permute-done.8.refs_6_ = bf16[80,1024]{1,0:T(8,128)(2,1)S(1)} collective-permute-done((bf16[80,1024]{1,0:T(8,128)(2,1)S(1)}, bf16[80,1024]{1,0:T(8,128)(2,1)S(1)}, u32[]{:S(2)}, u32[]{:S(2)}) %collective-permute-start.8) | collective-permute-done | bytes 163872 | tf_op jit(solution)/shard_map/ppermute | solution.py:317
  103.3 3.4 %collective-permute-done.9.refs_7_ = bf16[80,1024]{1,0:T(8,128)(2,1)S(1)} collective-permute-done((bf16[80,1024]{1,0:T(8,128)(2,1)S(1)}, bf16[80,1024]{1,0:T(8,128)(2,1)S(1)}, u32[]{:S(2)}, u32[]{:S(2)}) %collective-permute-start.9) | collective-permute-done | bytes 163872 | tf_op jit(solution)/shard_map/ppermute | solution.py:317
  106.7 15.2 %shard_map.127 = bf16[16,40,1024]{2,1,0:T(8,128)(2,1)} custom-call(s32[1]{0:T(128)} %bitcast.15.place_ref, bf16[80,1024]{1,0:T(8,128)(2,1)} %get-tuple-element.21.refs_0_, bf16[80,1024]{1,0:T(8,128)(2,1)S(1)} %collective-permute-done.3.refs_1_, bf16[80,1024]{1,0:T(8,128)(2,1)S(1)} %collective-permute-done.4.refs_2_, ...), custom_call_target="tpu_custom_call" | custom-call | flops 8053063680 | bytes 19398658 | tf_op jit(solution)/shard_map/pallas_call | solution.py:298
  121.9 4.1 %all-to-all-start.2 = ((bf16[16,40,1024]{2,1,0:T(8,128)(2,1)}), bf16[16,40,1024]{2,1,0:T(8,128)(2,1)S(1)}, u32[]{:S(2)}, u32[]{:S(2)}) async-start(bf16[16,40,1024]{2,1,0:T(8,128)(2,1)} %shard_map.127), calls=%async_computation.2 | async-start | bytes 2621440 | tf_op jit(solution)/shard_map/all_to_all | solution.py:325
  126.1 3.5 %shard_map.124 = f32[128,2048]{1,0:T(8,128)} custom-call(bf16[640,1024]{1,0:T(8,128)(2,1)S(1)} %bitcast.30, f32[2,128]{1,0:T(2,128)S(1)} %bitcast.42, s32[2,128]{1,0:T(2,128)S(1)} %bitcast.41, f32[128,2048]{1,0:T(8,128)} %bitcast.48, f32[3,1,2048]{2,1,0:T(1,128)S(1)} %bitcast.37), custom_call_target="tpu_custom_call" | custom-call | flops 671088640 | bytes 1848320 | tf_op jit(solution)/shard_map/pallas_call | solution.py:298
  129.6 3.5 %collective-permute-start.2 = (f32[1,128,2048]{2,1,0:T(8,128)}, f32[1,128,2048]{2,1,0:T(8,128)S(1)}, u32[]{:S(2)}, u32[]{:S(2)}) collective-permute-start(f32[1,128,2048]{2,1,0:T(8,128)} %bitcast.50), channel_id=1, source_target_pairs={{0,32},{32,64},{64,96},{1,33},{33,65},{65,97},{2,34},{34,66},{66,9... | collective-permute-start | bytes 3145736 | tf_op jit(solution)/shard_map/ppermute | solution.py:312
  133.0 12.8 %all-to-all-done.2 = bf16[16,40,1024]{2,1,0:T(8,128)(2,1)S(1)} async-done(((bf16[16,40,1024]{2,1,0:T(8,128)(2,1)}), bf16[16,40,1024]{2,1,0:T(8,128)(2,1)S(1)}, u32[]{:S(2)}, u32[]{:S(2)}) %all-to-all-start.2) | async-done | bytes 1310752 | tf_op jit(solution)/shard_map/all_to_all | solution.py:325
  145.8 2.2 %shard_map.128 = bf16[128,2048]{1,0:T(8,128)(2,1)S(1)} custom-call(bf16[640,1024]{1,0:T(8,128)(2,1)S(1)} %bitcast.29, s32[128,8]{1,0:T(8,128)S(1)} %get-tuple-element.37.where_ref, f32[128,2048]{1,0:T(8,128)} %get-tuple-element.38.norm_far, f32[128,1]{1,0:T(8,128)S(1)} %get-tuple-element.39.inv_ref, bf16[128,2048]{1,0:T(8,128)(2,1)} %bitcast.33, ...), custom_call_target="tpu_custom_call" | custom-call | flops 335544320 | bytes 2373888 | tf_op jit(solution)/shard_map/pallas_call | solution.py:298
  148.0 1.3 collective-permute-start.18
  149.3 11.4 %collective-permute-done.18 = bf16[1,128,2048]{2,1,0:T(8,128)(2,1)S(1)} collective-permute-done((bf16[1,128,2048]{2,1,0:T(8,128)(2,1)S(1)}, bf16[1,128,2048]{2,1,0:T(8,128)(2,1)S(1)}, u32[]{:S(2)}, u32[]{:S(2)}) %collective-permute-start.18) | collective-permute-done | bytes 524320 | tf_op jit(solution)/shard_map/ppermute | solution.py:312
  160.7 1.0 shard_map.125
  (52 shorter events, 1.9 us)
Async XLA Ops:
  0.6 25.8 %collective-permute-start = (bf16[2048,1024]{1,0:T(8,128)(2,1)}, bf16[2048,1024]{1,0:T(8,128)(2,1)}, u32[]{:S(2)}, u32[]{:S(2)}) collective-permute-start(bf16[2048,1024]{1,0:T(8,128)(2,1)} %bitcast.52), channel_id=1, source_target_pairs={{0,1},{1,0},{2,3},{3,2},{4,5},{5,4},{6,7},{7,6},{8,9},{9,8},{10,11... | collective-permute-start | bytes 12582920 | tf_op jit(solution)/shard_map/ppermute | solution.py:358
  0.7 25.8 %collective-permute-start.1 = (bf16[1024,2048]{1,0:T(8,128)(2,1)}, bf16[1024,2048]{1,0:T(8,128)(2,1)}, u32[]{:S(2)}, u32[]{:S(2)}) collective-permute-start(bf16[1024,2048]{1,0:T(8,128)(2,1)} %bitcast.55), channel_id=1, source_target_pairs={{0,1},{1,0},{2,3},{3,2},{4,5},{5,4},{6,7},{7,6},{8,9},{9,8},{10,11... | collective-permute-start | bytes 12582920 | tf_op jit(solution)/shard_map/ppermute | solution.py:358
  4.4 8.4 %copy-start.6 = (f32[1,128,2]{1,2,0:T(2,128)S(1)}, f32[1,128,2]{1,2,0:T(2,128)}, u32[]{:S(2)}) copy-start(f32[1,128,2]{1,2,0:T(2,128)} %param.18) | copy-start | bytes 3076
  4.4 8.4 %copy-start.7 = (s32[1,128,2]{1,2,0:T(2,128)S(1)}, s32[1,128,2]{1,2,0:T(2,128)}, u32[]{:S(2)}) copy-start(s32[1,128,2]{1,2,0:T(2,128)} %param.17) | copy-start | bytes 3076
  4.4 32.0 %all-to-all-start = ((bf16[16,40,1024]{2,1,0:T(8,128)(2,1)}), bf16[16,40,1024]{2,1,0:T(8,128)(2,1)S(1)}, u32[]{:S(2)}, u32[]{:S(2)}) async-start(bf16[16,40,1024]{2,1,0:T(8,128)(2,1)} %bitcast.46), calls=%async_computation | async-start | bytes 2621440 | tf_op jit(solution)/shard_map/all_to_all | solution.py:325
  16.4 43.8 %collective-permute-start.10 = (bf16[80,1024]{1,0:T(8,128)(2,1)}, bf16[80,1024]{1,0:T(8,128)(2,1)S(1)}, u32[]{:S(2)}, u32[]{:S(2)}) collective-permute-start(bf16[80,1024]{1,0:T(8,128)(2,1)} %get-tuple-element.29), channel_id=1, source_target_pairs={{0,16},{1,17},{2,18},{3,19},{4,20},{5,21},{6,22},{7,23},{8,24},{9,... | collective-permute-start | bytes 491528 | tf_op jit(solution)/shard_map/ppermute | solution.py:317
  19.9 44.4 %collective-permute-start.11 = (bf16[80,1024]{1,0:T(8,128)(2,1)}, bf16[80,1024]{1,0:T(8,128)(2,1)S(1)}, u32[]{:S(2)}, u32[]{:S(2)}) collective-permute-start(bf16[80,1024]{1,0:T(8,128)(2,1)} %get-tuple-element.30), channel_id=1, source_target_pairs={{0,18},{1,19},{2,16},{3,17},{4,22},{5,23},{6,20},{7,21},{8,26},{9,... | collective-permute-start | bytes 491528 | tf_op jit(solution)/shard_map/ppermute | solution.py:317
  21.4 45.6 %collective-permute-start.12 = (bf16[80,1024]{1,0:T(8,128)(2,1)}, bf16[80,1024]{1,0:T(8,128)(2,1)S(1)}, u32[]{:S(2)}, u32[]{:S(2)}) collective-permute-start(bf16[80,1024]{1,0:T(8,128)(2,1)} %get-tuple-element.31), channel_id=1, source_target_pairs={{0,20},{1,21},{2,22},{3,23},{4,16},{5,17},{6,18},{7,19},{8,28},{9,... | collective-permute-start | bytes 491528 | tf_op jit(solution)/shard_map/ppermute | solution.py:317
  26.5 43.2 %collective-permute-start.13 = (bf16[80,1024]{1,0:T(8,128)(2,1)}, bf16[80,1024]{1,0:T(8,128)(2,1)S(1)}, u32[]{:S(2)}, u32[]{:S(2)}) collective-permute-start(bf16[80,1024]{1,0:T(8,128)(2,1)} %get-tuple-element.32), channel_id=1, source_target_pairs={{0,22},{1,23},{2,20},{3,21},{4,18},{5,19},{6,16},{7,17},{8,30},{9,... | collective-permute-start | bytes 491528 | tf_op jit(solution)/shard_map/ppermute | solution.py:317
  26.6 43.4 %collective-permute-start.14 = (bf16[80,1024]{1,0:T(8,128)(2,1)}, bf16[80,1024]{1,0:T(8,128)(2,1)}, u32[]{:S(2)}, u32[]{:S(2)}) collective-permute-start(bf16[80,1024]{1,0:T(8,128)(2,1)} %get-tuple-element.33), channel_id=1, source_target_pairs={{0,24},{1,25},{2,26},{3,27},{4,28},{5,29},{6,30},{7,31},{8,16},{9,... | collective-permute-start | bytes 491528 | tf_op jit(solution)/shard_map/ppermute | solution.py:317
  47.2 19.9 %copy-start.15 = (bf16[80,1024]{1,0:T(8,128)(2,1)S(1)}, bf16[80,1024]{1,0:T(8,128)(2,1)}, u32[]{:S(2)}) copy-start(bf16[80,1024]{1,0:T(8,128)(2,1)} %get-tuple-element.36) | copy-start | bytes 491524
  47.2 22.5 %copy-start.14 = (bf16[80,1024]{1,0:T(8,128)(2,1)S(1)}, bf16[80,1024]{1,0:T(8,128)(2,1)}, u32[]{:S(2)}) copy-start(bf16[80,1024]{1,0:T(8,128)(2,1)} %get-tuple-element.22) | copy-start | bytes 491524
  47.2 22.8 %copy-start.13 = (bf16[80,1024]{1,0:T(8,128)(2,1)S(1)}, bf16[80,1024]{1,0:T(8,128)(2,1)}, u32[]{:S(2)}) copy-start(bf16[80,1024]{1,0:T(8,128)(2,1)} %get-tuple-element.23) | copy-start | bytes 491524
  47.2 38.2 %copy-start.12 = (bf16[80,1024]{1,0:T(8,128)(2,1)S(1)}, bf16[80,1024]{1,0:T(8,128)(2,1)}, u32[]{:S(2)}) copy-start(bf16[80,1024]{1,0:T(8,128)(2,1)} %get-tuple-element.24) | copy-start | bytes 491524
  47.2 44.2 %copy-start.11 = (bf16[80,1024]{1,0:T(8,128)(2,1)S(1)}, bf16[80,1024]{1,0:T(8,128)(2,1)}, u32[]{:S(2)}) copy-start(bf16[80,1024]{1,0:T(8,128)(2,1)} %get-tuple-element.25) | copy-start | bytes 491524
  47.2 46.3 %copy-start.10 = (bf16[80,1024]{1,0:T(8,128)(2,1)S(1)}, bf16[80,1024]{1,0:T(8,128)(2,1)}, u32[]{:S(2)}) copy-start(bf16[80,1024]{1,0:T(8,128)(2,1)} %get-tuple-element.26) | copy-start | bytes 491524
  47.2 46.3 %copy-start.9 = (bf16[80,1024]{1,0:T(8,128)(2,1)S(1)}, bf16[80,1024]{1,0:T(8,128)(2,1)}, u32[]{:S(2)}) copy-start(bf16[80,1024]{1,0:T(8,128)(2,1)} %get-tuple-element.27) | copy-start | bytes 491524
  47.2 51.3 %copy-start.8 = (bf16[80,1024]{1,0:T(8,128)(2,1)S(1)}, bf16[80,1024]{1,0:T(8,128)(2,1)}, u32[]{:S(2)}) copy-start(bf16[80,1024]{1,0:T(8,128)(2,1)} %get-tuple-element.28) | copy-start | bytes 491524
  47.2 74.7 %all-to-all-start.1 = ((bf16[16,40,1024]{2,1,0:T(8,128)(2,1)}), bf16[16,40,1024]{2,1,0:T(8,128)(2,1)S(1)}, u32[]{:S(2)}, u32[]{:S(2)}) async-start(bf16[16,40,1024]{2,1,0:T(8,128)(2,1)} %bitcast.49), calls=%async_computation.1 | async-start | bytes 2621440 | tf_op jit(solution)/shard_map/all_to_all | solution.py:325
  60.2 25.2 %collective-permute-start.15 = (bf16[80,1024]{1,0:T(8,128)(2,1)}, bf16[80,1024]{1,0:T(8,128)(2,1)S(1)}, u32[]{:S(2)}, u32[]{:S(2)}) collective-permute-start(bf16[80,1024]{1,0:T(8,128)(2,1)} %get-tuple-element.34), channel_id=1, source_target_pairs={{0,26},{1,27},{2,24},{3,25},{4,30},{5,31},{6,28},{7,29},{8,18},{9,... | collective-permute-start | bytes 491528 | tf_op jit(solution)/shard_map/ppermute | solution.py:317
  64.3 27.1 %collective-permute-start.16 = (bf16[80,1024]{1,0:T(8,128)(2,1)}, bf16[80,1024]{1,0:T(8,128)(2,1)S(1)}, u32[]{:S(2)}, u32[]{:S(2)}) collective-permute-start(bf16[80,1024]{1,0:T(8,128)(2,1)} %get-tuple-element.35), channel_id=1, source_target_pairs={{0,28},{1,29},{2,30},{3,31},{4,24},{5,25},{6,26},{7,27},{8,20},{9,... | collective-permute-start | bytes 491528 | tf_op jit(solution)/shard_map/ppermute | solution.py:317
  67.0 26.5 %collective-permute-start.17 = (bf16[80,1024]{1,0:T(8,128)(2,1)S(1)}, bf16[80,1024]{1,0:T(8,128)(2,1)S(1)}, u32[]{:S(2)}, u32[]{:S(2)}) collective-permute-start(bf16[80,1024]{1,0:T(8,128)(2,1)S(1)} %copy-done.15), channel_id=1, source_target_pairs={{0,30},{1,31},{2,28},{3,29},{4,26},{5,27},{6,24},{7,25},{8,22},{9,... | collective-permute-start | bytes 491528 | tf_op jit(solution)/shard_map/ppermute | solution.py:317
  69.7 23.8 %collective-permute-start.3 = (bf16[80,1024]{1,0:T(8,128)(2,1)S(1)}, bf16[80,1024]{1,0:T(8,128)(2,1)S(1)}, u32[]{:S(2)}, u32[]{:S(2)}) collective-permute-start(bf16[80,1024]{1,0:T(8,128)(2,1)S(1)} %copy-done.14), channel_id=1, source_target_pairs={{0,2},{1,3},{2,0},{3,1},{4,6},{5,7},{6,4},{7,5},{8,10},{9,11},{10,... | collective-permute-start | bytes 491528 | tf_op jit(solution)/shard_map/ppermute | solution.py:317
  70.0 28.6 %collective-permute-start.4 = (bf16[80,1024]{1,0:T(8,128)(2,1)S(1)}, bf16[80,1024]{1,0:T(8,128)(2,1)S(1)}, u32[]{:S(2)}, u32[]{:S(2)}) collective-permute-start(bf16[80,1024]{1,0:T(8,128)(2,1)S(1)} %copy-done.13), channel_id=1, source_target_pairs={{0,4},{1,5},{2,6},{3,7},{4,0},{5,1},{6,2},{7,3},{8,12},{9,13},{10,... | collective-permute-start | bytes 491528 | tf_op jit(solution)/shard_map/ppermute | solution.py:317
  85.4 13.2 %collective-permute-start.5 = (bf16[80,1024]{1,0:T(8,128)(2,1)S(1)}, bf16[80,1024]{1,0:T(8,128)(2,1)S(1)}, u32[]{:S(2)}, u32[]{:S(2)}) collective-permute-start(bf16[80,1024]{1,0:T(8,128)(2,1)S(1)} %copy-done.12), channel_id=1, source_target_pairs={{0,6},{1,7},{2,4},{3,5},{4,2},{5,3},{6,0},{7,1},{8,14},{9,15},{10,... | collective-permute-start | bytes 491528 | tf_op jit(solution)/shard_map/ppermute | solution.py:317
  91.4 9.1 %collective-permute-start.6 = (bf16[80,1024]{1,0:T(8,128)(2,1)S(1)}, bf16[80,1024]{1,0:T(8,128)(2,1)S(1)}, u32[]{:S(2)}, u32[]{:S(2)}) collective-permute-start(bf16[80,1024]{1,0:T(8,128)(2,1)S(1)} %copy-done.11), channel_id=1, source_target_pairs={{0,8},{1,9},{2,10},{3,11},{4,12},{5,13},{6,14},{7,15},{8,0},{9,1},... | collective-permute-start | bytes 491528 | tf_op jit(solution)/shard_map/ppermute | solution.py:317
  93.5 7.0 %collective-permute-start.7 = (bf16[80,1024]{1,0:T(8,128)(2,1)S(1)}, bf16[80,1024]{1,0:T(8,128)(2,1)S(1)}, u32[]{:S(2)}, u32[]{:S(2)}) collective-permute-start(bf16[80,1024]{1,0:T(8,128)(2,1)S(1)} %copy-done.10), channel_id=1, source_target_pairs={{0,10},{1,11},{2,8},{3,9},{4,14},{5,15},{6,12},{7,13},{8,2},{9,3},... | collective-permute-start | bytes 491528 | tf_op jit(solution)/shard_map/ppermute | solution.py:317
  93.5 9.8 %collective-permute-start.8 = (bf16[80,1024]{1,0:T(8,128)(2,1)S(1)}, bf16[80,1024]{1,0:T(8,128)(2,1)S(1)}, u32[]{:S(2)}, u32[]{:S(2)}) collective-permute-start(bf16[80,1024]{1,0:T(8,128)(2,1)S(1)} %copy-done.9), channel_id=1, source_target_pairs={{0,12},{1,13},{2,14},{3,15},{4,8},{5,9},{6,10},{7,11},{8,4},{9,5},... | collective-permute-start | bytes 491528 | tf_op jit(solution)/shard_map/ppermute | solution.py:317
  98.5 8.2 %collective-permute-start.9 = (bf16[80,1024]{1,0:T(8,128)(2,1)S(1)}, bf16[80,1024]{1,0:T(8,128)(2,1)S(1)}, u32[]{:S(2)}, u32[]{:S(2)}) collective-permute-start(bf16[80,1024]{1,0:T(8,128)(2,1)S(1)} %copy-done.8), channel_id=1, source_target_pairs={{0,14},{1,15},{2,12},{3,13},{4,10},{5,11},{6,8},{7,9},{8,6},{9,7},... | collective-permute-start | bytes 491528 | tf_op jit(solution)/shard_map/ppermute | solution.py:317
  121.9 23.8 %all-to-all-start.2 = ((bf16[16,40,1024]{2,1,0:T(8,128)(2,1)}), bf16[16,40,1024]{2,1,0:T(8,128)(2,1)S(1)}, u32[]{:S(2)}, u32[]{:S(2)}) async-start(bf16[16,40,1024]{2,1,0:T(8,128)(2,1)} %shard_map.127), calls=%async_computation.2 | async-start | bytes 2621440 | tf_op jit(solution)/shard_map/all_to_all | solution.py:325
  129.6 31.2 %collective-permute-start.2 = (f32[1,128,2048]{2,1,0:T(8,128)}, f32[1,128,2048]{2,1,0:T(8,128)S(1)}, u32[]{:S(2)}, u32[]{:S(2)}) collective-permute-start(f32[1,128,2048]{2,1,0:T(8,128)} %bitcast.50), channel_id=1, source_target_pairs={{0,32},{32,64},{64,96},{1,33},{33,65},{65,97},{2,34},{34,66},{66,9... | collective-permute-start | bytes 3145736 | tf_op jit(solution)/shard_map/ppermute | solution.py:312
  148.0 12.7 %collective-permute-start.18 = (bf16[1,128,2048]{2,1,0:T(8,128)(2,1)S(1)}, bf16[1,128,2048]{2,1,0:T(8,128)(2,1)S(1)}, u32[]{:S(2)}, u32[]{:S(2)}) collective-permute-start(bf16[1,128,2048]{2,1,0:T(8,128)(2,1)S(1)} %bitcast.35), channel_id=1, source_target_pairs={{32,0},{64,32},{96,64},{33,1},{65,33},{97,65},{34,2},{66,34},{98,6... | collective-permute-start | bytes 1572872 | tf_op jit(solution)/shard_map/ppermute | solution.py:312
  (6 other events, 37.5 us)
